TPU v7x, 256 devices: a 2x2x32 block of a 4x8x32 slice. The times are simulated.
256 devices in a mesh: scene: 4 (over x, y), az: 64 (over z, core).
Axes of the slice: x: 2, y: 2, z: 32, core: 2. Of those that a mesh axis runs over, the one named last changes fastest.
The devices are a block of a 4x8x32 slice.
Arguments:
- secondary: bfloat16 [2, 16384, 12288], P(None, ('scene', 'az')), parts along dimension 1, may hold values from -6 to 6
- line_valid: int32 [16384], P(('scene', 'az')), parts along dimension 0, may hold values 0 or 1
- first_valid: int32 [16384], P(('scene', 'az')), parts along dimension 0, may hold values from 0 to 3071
- last_valid: int32 [16384], P(('scene', 'az')), parts along dimension 0, may hold values from 9216 to 12288
- az_coef: float32 [3, 16384], P(None, ('scene', 'az')), parts along dimension 1, may hold values from -0.33 to 0.33
- az_base: int32 [16384], P(('scene', 'az')), parts along dimension 0, may hold values from -3 to 3
- rg_base: int32 [16384], P(('scene', 'az')), parts along dimension 0, may hold values from -8 to 8
- rg_coef: float32 [16], P('scene'), parts along dimension 0, may hold values from -3 to 3
- block_dest: int32 [16384], P(('scene', 'az')), parts along dimension 0, may hold values from 0 to 4095, as said below
Outputs:
- coreg: bfloat16 [2, 16384, 12288], P(None, ('scene', 'az')), parts along dimension 1
- mean_power: float32 [4], P('scene'), parts along dimension 0
- valid_share: float32 [4], P('scene'), parts along dimension 0
There are 4 independent parts, one for each index of `scene`. A program takes and returns all parts, laid end to end along the dimension named above; each array names one. Nothing has to cross between parts.
Inputs may be any that keep to these rules, and one draw needn't show every extreme that they name: `block_dest`: A permutation of 0 to 4095. The 64 line blocks of each device of az take exactly one place on every device of az, itself included (place // 64 runs over all devices).
All inputs are finite; a program needn't handle non-finite values. No bound on the sum of `line_valid` on one device may be relied on, other than what follows from the above.
Results may differ from a plain program's by a relative error of at most 0.0066.
Values may be sent and summed in bfloat16 or wider, within the bound.
No kernel may reach another device: no remote copies, remote signals or barrier semaphores. Data moves between devices by JAX's collectives and lax.ppermute only.
A program may use at most 128 MiB of HBM per device.

v0:
```python
import jax
import jax.numpy as jnp
from jax import lax
from jax.sharding import PartitionSpec as P

LINES = 1
RBMAX = 8
HALO = 7


def with_halo(block, sides, width):
    for axis, dim in sides:
        count = lax.axis_size(axis)
        forward = [(i, i + 1) for i in range(count - 1)]
        backward = [(target, source) for source, target in forward]
        low = lax.ppermute(
            lax.slice_in_dim(block, block.shape[dim] - width, None, axis=dim), axis, forward
        )
        high = lax.ppermute(lax.slice_in_dim(block, 0, width, axis=dim), axis, backward)
        block = jnp.concatenate([low, block, high], axis=dim)
    return block


def grouped_exchange(shard, axis, split_dim, concat_dim, work, item_dim, out_dim):

    def moved(group):
        return lax.all_to_all(group, axis, split_axis=split_dim, concat_axis=concat_dim, tiled=True)

    items = jax.tree.leaves(shard)[0].shape[item_dim]
    ends = [items * k // 2 for k in range(2 + 1)] if items % 2 == 0 else [0, items]
    groups = [
        jax.tree.map(lambda a: lax.slice_in_dim(a, low, high, axis=item_dim), shard)
        for low, high in zip(ends, ends[1:])
    ]
    arrived = [moved(group) for group in groups]
    made = [work(group) for group in arrived]
    return jax.tree.map(lambda *parts: jnp.concatenate(parts, axis=out_dim), *made)


def from_everyone(shard, axis):
    copies = jnp.broadcast_to(shard, (lax.axis_size(axis), *shard.shape))
    return lax.all_to_all(copies, axis, split_axis=0, concat_axis=0, tiled=True)


def over_copies(shard, axis):
    return from_everyone(shard, axis).sum(axis=0)


def packed_total(arrays, axis):
    flat, at, outs = (jnp.concatenate([a.reshape(-1) for a in arrays]), 0, [])
    subtotal = over_copies(flat, axis)
    for a in arrays:
        outs.append(subtotal[at : at + a.size].reshape(a.shape))
        at += a.size
    return tuple(outs)


def sinc_taper(distance):
    in_reach = jnp.abs(distance) < 4.0
    shaped = jnp.sinc(distance) * (0.5 + 0.5 * jnp.cos(jnp.pi * distance / 4.0))
    return jnp.where(in_reach, shaped, jnp.zeros_like(distance))


def tap_weights(az_coef, line_count):
    position = (jnp.arange(line_count, dtype=jnp.float32) + 0.5) / line_count
    fraction = (
        az_coef[0][:, None]
        + az_coef[1][:, None] * position
        + az_coef[2][:, None] * position * position
    )
    tap_offsets = jnp.arange(9, dtype=jnp.float32) - 4.0
    return sinc_taper(tap_offsets[None, None, :] - fraction[:, :, None]).astype(jnp.bfloat16)


def range_tiles(rg_coef, col_count):
    tile_total = col_count // 128
    col_index = jnp.arange(col_count, dtype=jnp.float32)
    along = (col_index + 0.5) / col_count
    offsets = (
        rg_coef[0]
        + rg_coef[1] * along
        + rg_coef[2] * along * along
        + rg_coef[3] * along * along * along
    )
    offsets = offsets.reshape(tile_total, 128)
    inner = jnp.arange(128, dtype=jnp.float32)
    tile_gaps = (jnp.arange(3, dtype=jnp.float32) - 1.0) * 128.0
    distance = (
        tile_gaps[:, None, None, None]
        + inner[None, None, :, None]
        - inner[None, None, None, :]
        - offsets[None, :, None, :]
    )
    return sinc_taper(distance).astype(jnp.bfloat16)


def range_apply(lines, kernel):
    col_count = lines.shape[-1]
    tile_total = col_count // 128
    tiled_rows = lines.reshape(lines.shape[:-1] + (tile_total, 128))
    padded = jnp.pad(tiled_rows, ((0, 0), (0, 0), (1, 1), (0, 0)))
    ranged = jnp.zeros(tiled_rows.shape, jnp.float32)
    for shift_tile in range(3):
        ranged = ranged + jnp.einsum(
            "npti,tij->nptj",
            padded[:, :, shift_tile : shift_tile + tile_total],
            kernel[shift_tile],
            preferred_element_type=jnp.float32,
        )
    return ranged.reshape(lines.shape).astype(jnp.bfloat16)


def shards(
    secondary, line_valid, first_valid, last_valid, az_coef, az_base, rg_base, rg_coef, block_dest
):
    col_count = secondary.shape[2]
    blocks = block_dest.shape[0]
    row_total = blocks * LINES
    col_index = jnp.arange(col_count, dtype=jnp.int32)
    kept_mask = (
        (line_valid[:, None] > 0)
        & (col_index[None, :] >= first_valid[:, None])
        & (col_index[None, :] < last_valid[:, None])
    )
    masked = jnp.where(kept_mask[None], secondary, jnp.zeros((), jnp.bfloat16))
    own_count = jnp.sum(kept_mask.astype(jnp.int32)).astype(jnp.float32)
    extended = with_halo(masked, (("az", 1),), HALO)
    padded = jnp.pad(extended, ((0, 0), (0, 0), (RBMAX, RBMAX)))
    span = row_total + 2 * HALO
    weights = tap_weights(az_coef, LINES)
    kernel = range_tiles(rg_coef, col_count)
    target = block_dest // blocks
    places = block_dest % blocks
    send_order = jnp.zeros((blocks,), jnp.int32).at[target].set(jnp.arange(blocks, dtype=jnp.int32))
    line_pos = (
        jnp.arange(blocks, dtype=jnp.int32)[:, None] * LINES
        + jnp.arange(LINES, dtype=jnp.int32)[None, :]
        + az_base[:, None]
        - 4
        + HALO
    )
    source_lines = jnp.arange(span, dtype=jnp.int32)
    taps = jnp.arange(9, dtype=jnp.int32)
    hit = (
        source_lines[None, None, None, :] == line_pos[:, :, None, None] + taps[None, None, :, None]
    )
    band = jnp.sum(jnp.where(hit, weights[..., None].astype(jnp.float32), 0.0), axis=2)
    band = band[send_order]
    shift_sent = rg_base[send_order]
    summed = jnp.zeros((row_total, 2, col_count), jnp.float32)
    for shift in range(-RBMAX, RBMAX + 1):
        picked = (
            jnp.where((shift_sent == shift)[:, None, None], band, 0.0)
            .astype(jnp.bfloat16)
            .reshape(row_total, span)
        )
        summed = summed + jnp.einsum(
            "rs,psc->rpc",
            picked,
            padded[:, :, RBMAX + shift : RBMAX + shift + col_count],
            preferred_element_type=jnp.float32,
        )
    azimuthal = summed.astype(jnp.bfloat16)
    sent_places = places[send_order]

    def finish(pieces):
        line_part, tag_part = pieces
        done = range_apply(line_part.reshape((-1,) + line_part.shape[2:]), kernel)
        return (done.reshape(line_part.shape), tag_part)

    tag_grid = sent_places[:, None]
    arrived, tag_back = grouped_exchange(
        (azimuthal.reshape(blocks, LINES, 2, col_count), tag_grid), "az", 0, 0, finish, 1, 1
    )
    place_tags = tag_back[:, 0]
    own_power = jnp.sum(jnp.square(arrived.astype(jnp.float32)))
    total_power, total_count = packed_total((own_power, own_count), "az")
    mean_power = total_power / jnp.maximum(total_count, 1.0)
    power_gain = lax.rsqrt(mean_power + 0.5)
    arrange = (place_tags[None, :] == jnp.arange(blocks, dtype=jnp.int32)[:, None]).astype(
        jnp.bfloat16
    )
    ordered = jnp.einsum("qb,blpc->pqlc", arrange, arrived, preferred_element_type=jnp.float32)
    scaled = (ordered * power_gain).astype(jnp.bfloat16)
    coregistered = scaled.reshape(2, row_total, col_count)
    valid_share = total_count / float(col_count * row_total * lax.axis_size("az"))
    return (coregistered, mean_power.reshape(1), valid_share.reshape(1))


def solution(mesh):
    placed = (
        P(None, ("scene", "az"), None),
        P(("scene", "az")),
        P(("scene", "az")),
        P(("scene", "az")),
        P(None, ("scene", "az")),
        P(("scene", "az")),
        P(("scene", "az")),
        P("scene"),
        P(("scene", "az")),
    )
    return jax.shard_map(
        shards,
        mesh=mesh,
        in_specs=placed,
        out_specs=(P(None, ("scene", "az"), None), P("scene"), P("scene")),
        check_vma=False,
    )
```

profile of v0, /device:TPU:46, one launch (start us, length us, event | category | flops | bytes accessed | tf_op | source)
XLA Modules:
  0.0 479.1 jit_solution(14402592561803436990)
XLA Ops:
  0.6 0.7 broadcast_compare_fusion.17
  1.3 1.6 fusion.61
  2.9 2.4 broadcast_select_fusion
  5.3 1.0 fusion.205
  6.3 2.6 collective-permute-start
  8.9 1.3 collective-permute-start.1
  10.3 0.8 scatter_custom_fusion
  11.1 0.8 gather_fusion
  12.9 1.1 collective-permute-done.1
  13.9 2.5 pad_maximum_fusion
  16.4 1.4 fusion.50
  17.9 1.4 fusion.42
  19.3 1.7 convolution_add_fusion.14
  21.0 1.7 convolution_add_fusion.13
  22.7 1.7 convolution_add_fusion.12
  24.3 1.7 convolution_add_fusion.11
  26.0 1.7 convolution_add_fusion.10
  27.7 2.1 convolution_add_fusion.9
  29.8 1.7 convolution_add_fusion.8
  31.5 3.3 fusion.30
  34.8 1.7 convolution_add_fusion.6
  36.5 1.7 convolution_add_fusion.5
  38.2 1.7 convolution_add_fusion.4
  40.0 1.7 convolution_add_fusion.3
  41.7 1.7 convolution_add_fusion.2
  43.4 1.9 convolution_add_fusion.1
  45.4 1.8 fusion.34
  47.2 4.9 %copy.32 = bf16[64,1,2,12288]{3,2,1,0:T(2,128)(2,1)} copy(bf16[64,1,2,12288]{3,0,2,1:T(8,128)(2,1)S(1)} %fusion.34) | data formatting | bytes 6291456 | tf_op jit(solution)/shard_map/reshape | solution.py:173
  52.1 39.6 %all-to-all-start = ((bf16[64,1,2,12288]{3,2,1,0:T(2,128)(2,1)}), bf16[64,1,2,12288]{3,2,1,0:T(2,128)(2,1)S(1)}, u32[]{:S(2)}, u32[]{:S(2)}) async-start(bf16[64,1,2,12288]{3,2,1,0:T(2,128)(2,1)} %copy.32), calls=%async_computation | async-start | bytes 6291456 | tf_op jit(solution)/shard_map/all_to_all | solution.py:27
  91.7 1.8 convert_reduce_fusion
  94.2 0.7 fusion.207
  96.7 0.8 gather_fusion.2
  97.5 0.7 copy.37
  98.2 0.7 fusion.64
  99.1 86.0 %fusion.29 = bf16[3,96,128,128]{3,2,1,0:T(8,128)(2,1)} fusion(f32[96,128]{1,0:T(8,128)S(1)} %fusion.64, f32[3,128,128]{2,1,0:T(8,128)S(1)} %iota_subtract_fusion), kind=kLoop, calls=%fused_computation.41 | loop fusion | flops 193462272 | bytes 9682944 | tf_op jit(solution)/shard_map/convert_element_type | solution.py:94
  185.1 195.5 %all-to-all-done = bf16[64,1,2,12288]{3,2,1,0:T(2,128)(2,1)S(1)} async-done(((bf16[64,1,2,12288]{3,2,1,0:T(2,128)(2,1)}), bf16[64,1,2,12288]{3,2,1,0:T(2,128)(2,1)S(1)}, u32[]{:S(2)}, u32[]{:S(2)}) %all-to-all-start) | async-done | bytes 3145760 | tf_op jit(solution)/shard_map/all_to_all | solution.py:27
  380.6 1.7 copy-done.2
  382.3 6.7 %all-to-all-start.1 = ((s32[64,1,1]{2,1,0:T(1,128)}), s32[64,1,1]{2,1,0:T(1,128)S(1)}, u32[]{:S(2)}, u32[]{:S(2)}) async-start(s32[64,1,1]{2,1,0:T(1,128)} %copy.37), calls=%async_computation.1 | async-start | bytes 65536 | tf_op jit(solution)/shard_map/all_to_all | solution.py:27
  389.0 8.5 %reshape.706 = bf16[64,2,96,128]{3,2,1,0:T(8,128)(2,1)} reshape(bf16[64,1,2,12288]{3,2,1,0:T(2,128)(2,1)} %copy-done.2) | data formatting | bytes 6291456 | tf_op jit(solution)/shard_map/reshape;reshape | solution.py:100
  397.5 4.1 copy.34
  401.6 5.7 %fusion.55 = f32[96,128,64,2]{1,2,3,0:T(8,128)} fusion(bf16[3,96,128,128]{3,2,1,0:T(8,128)(2,1)} %fusion.29, bf16[64,2,96,128]{3,0,1,2:T(8,128)(2,1)S(1)} %copy.34), kind=kOutput, calls=%fused_computation.87 | convolution fusion | flops 402653184 | bytes 12582912 | tf_op jit(solution)/shard_map/npti,tij->nptj/dot_general | solution.py:104
  407.3 3.6 fusion.57
  410.9 11.5 %multiply_reduce_fusion = (f32[]{:T(128)}, bf16[96,128,64,2]{1,2,3,0:T(8,128)(2,1)}) fusion(f32[96,128,64,2]{1,2,3,0:T(8,128)} %fusion.55, f32[96,128,64,2]{1,2,3,0:T(8,128)} %fusion.57, bf16[64,2,96,128]{3,2,1,0:T(8,128)(2,1)} %reshape.706, bf16[3,96,128,128]{3,2,1,0:T(8,128)(2,1)S(1)} %bitcast.105), kind=kOutput, calls=%fused_computation.63 | convolution fusion | flops 412090368 | bytes 22020100 | tf_op jit(solution)/shard_map/npti,tij->nptj/dot_general | solution.py:104
  422.4 0.7 pad_maximum_fusion.1
  423.8 23.6 %all-to-all-start.2 = ((f32[64,1,2]{2,1,0:T(1,128)}), f32[64,1,2]{2,1,0:T(1,128)S(1)}, u32[]{:S(2)}, u32[]{:S(2)}) async-start(f32[64,1,2]{2,1,0:T(1,128)} %broadcast_in_dim.215), calls=%async_computation.2 | async-start | bytes 65536 | tf_op jit(solution)/shard_map/all_to_all | solution.py:42
  447.5 1.2 reduce.3
  448.7 20.7 %all-to-all-done.2 = f32[64,1,2]{2,1,0:T(1,128)S(1)} async-done(((f32[64,1,2]{2,1,0:T(1,128)}), f32[64,1,2]{2,1,0:T(1,128)S(1)}, u32[]{:S(2)}, u32[]{:S(2)}) %all-to-all-start.2) | async-done | bytes 544 | tf_op jit(solution)/shard_map/all_to_all | solution.py:42
  472.1 4.5 fusion.33
  (44 shorter events, 2.6 us)
Async XLA Ops:
  0.6 10.4 %copy-start = (s32[64]{0:T(128)S(1)}, s32[64]{0:T(128)}, u32[]{:S(2)}) copy-start(s32[64]{0:T(128)} %param.15) | copy-start | bytes 772
  1.3 8.9 %copy-start.4 = (f32[3,64]{1,0:T(4,128)S(1)}, f32[3,64]{1,0:T(4,128)}, u32[]{:S(2)}) copy-start(f32[3,64]{1,0:T(4,128)} %param.13) | copy-start | bytes 2308
  1.3 8.9 %copy-start.7 = (s32[64]{0:T(128)S(1)}, s32[64]{0:T(128)}, u32[]{:S(2)}) copy-start(s32[64]{0:T(128)} %param.14) | copy-start | bytes 772
  1.3 8.9 %copy-start.8 = (s32[64]{0:T(128)S(1)}, s32[64]{0:T(128)}, u32[]{:S(2)}) copy-start(s32[64]{0:T(128)} %param.17) | copy-start | bytes 772
  6.3 6.6 %collective-permute-start = (bf16[2,7,12288]{2,1,0:T(8,128)(2,1)}, bf16[2,7,12288]{2,1,0:T(8,128)(2,1)}, u32[]{:S(2)}, u32[]{:S(2)}) collective-permute-start(bf16[2,7,12288]{2,1,0:T(8,128)(2,1)} %get-tuple-element.3), channel_id=1, source_target_pairs={{0,1},{1,2},{2,3},{3,4},{4,5},{5,6},{6,7},{7,8},{8,9},{9,10},{10,1... | collective-permute-start | bytes 1032200 | tf_op jit(solution)/shard_map/ppermute | solution.py:16
  8.9 5.1 %collective-permute-start.1 = (bf16[2,7,12288]{2,1,0:T(8,128)(2,1)}, bf16[2,7,12288]{2,1,0:T(8,128)(2,1)}, u32[]{:S(2)}, u32[]{:S(2)}) collective-permute-start(bf16[2,7,12288]{2,1,0:T(8,128)(2,1)} %get-tuple-element.4), channel_id=1, source_target_pairs={{1,0},{2,1},{3,2},{4,3},{5,4},{6,5},{7,6},{8,7},{9,8},{10,9},{11,1... | collective-permute-start | bytes 1032200 | tf_op jit(solution)/shard_map/ppermute | solution.py:19
  52.1 39.6 %copy-start.5 = (s32[64]{0:T(128)S(1)}, s32[64]{0:T(128)}, u32[]{:S(2)}) copy-start(s32[64]{0:T(128)} %param.12) | copy-start | bytes 772
  52.1 39.6 %copy-start.6 = (s32[64]{0:T(128)S(1)}, s32[64]{0:T(128)}, u32[]{:S(2)}) copy-start(s32[64]{0:T(128)} %param.11) | copy-start | bytes 772
  52.1 42.1 %copy-start.3 = (f32[4]{0:T(128)S(1)}, f32[4]{0:T(128)}, u32[]{:S(2)}) copy-start(f32[4]{0:T(128)} %param.16) | copy-start | bytes 52
  52.1 328.5 %all-to-all-start = ((bf16[64,1,2,12288]{3,2,1,0:T(2,128)(2,1)}), bf16[64,1,2,12288]{3,2,1,0:T(2,128)(2,1)S(1)}, u32[]{:S(2)}, u32[]{:S(2)}) async-start(bf16[64,1,2,12288]{3,2,1,0:T(2,128)(2,1)} %copy.32), calls=%async_computation | async-start | bytes 6291456 | tf_op jit(solution)/shard_map/all_to_all | solution.py:27
  380.6 1.7 copy-start.2
  382.3 40.9 %all-to-all-start.1 = ((s32[64,1,1]{2,1,0:T(1,128)}), s32[64,1,1]{2,1,0:T(1,128)S(1)}, u32[]{:S(2)}, u32[]{:S(2)}) async-start(s32[64,1,1]{2,1,0:T(1,128)} %copy.37), calls=%async_computation.1 | async-start | bytes 65536 | tf_op jit(solution)/shard_map/all_to_all | solution.py:27
  389.0 18.3 %slice-start = ((s8[9437184]{0:T(1024)(128)(4,1)}), s8[1048576]{0:T(1024)(128)(4,1)S(1)}, s32[]{:S(2)}) async-start(s8[9437184]{0:T(1024)(128)(4,1)} %bitcast.104), calls=%async_computation.3 | async-start | bytes 2097152
  397.5 9.8 %slice-start.1 = ((s8[9437184]{0:T(1024)(128)(4,1)}), s8[4194304]{0:T(1024)(128)(4,1)S(1)}, s32[]{:S(2)}) async-start(s8[9437184]{0:T(1024)(128)(4,1)} %bitcast.104), calls=%async_computation.4 | async-start | bytes 8388608
  401.6 5.7 %slice-start.2 = ((s8[9437184]{0:T(1024)(128)(4,1)}), s8[4194304]{0:T(1024)(128)(4,1)S(1)}, s32[]{:S(2)}) async-start(s8[9437184]{0:T(1024)(128)(4,1)} %bitcast.104), calls=%async_computation.5 | async-start | bytes 8388608
  410.9 65.7 %copy-start.1 = (s32[64]{0:T(128)S(1)}, s32[64]{0:T(128)}, u32[]{:S(2)}) copy-start(s32[64]{0:T(128)} %param.15) | copy-start | bytes 772
  423.8 45.6 %all-to-all-start.2 = ((f32[64,1,2]{2,1,0:T(1,128)}), f32[64,1,2]{2,1,0:T(1,128)S(1)}, u32[]{:S(2)}, u32[]{:S(2)}) async-start(f32[64,1,2]{2,1,0:T(1,128)} %broadcast_in_dim.215), calls=%async_computation.2 | async-start | bytes 65536 | tf_op jit(solution)/shard_map/all_to_all | solution.py:42
where the time goes:
time: 483 us; the launch traced here: 479 us
  waiting for transfers between devices  217 us (45%)
  other arithmetic  98.3 us (20%)
  starting transfers between devices  73.8 us (15%)
  matrix products  56 us (12%)
  local copies, waits for them, and re-layouts  25.7 us (5%)
  between operations  7.96 us (2%)
    all_to_all x2, waiting for transfers between devices, moved(): lax.all_to_all(group, axis, split_axis=split_dim, concat_axis=concat_dim,...  196 us
    convert_element_type x1, other arithmetic, range_tiles(): return sinc_taper(distance).astype(jnp.bfloat16)  86 us
    all_to_all x2, starting transfers between devices, moved(): lax.all_to_all(group, axis, split_axis=split_dim, concat_axis=concat_dim,...  46.2 us
    dot_general x17, matrix products, shards(): jnp.einsum('rs,psc->rpc', picked, padded[:, :, RBMAX + shift:RBMAX + shif...  30.7 us
    all_to_all x1, starting transfers between devices, from_everyone(): return lax.all_to_all(copies, axis, split_axis=0, concat_axis=0, tiled=True)  23.6 us
    dot_general x3, matrix products, range_apply(): jnp.einsum('npti,tij->nptj', padded[:, :, shift_tile:shift_tile + tile_to...  20.8 us
    all_to_all x1, waiting for transfers between devices, from_everyone(): return lax.all_to_all(copies, axis, split_axis=0, concat_axis=0, tiled=True)  20.7 us
    another operation x2, local copies, waits for them, and re-layouts, range_apply(): tiled_rows = lines.reshape(lines.shape[:-1] + (tile_total, 128))  12.6 us
  transfers between devices with their start and end apart: 5, of which 3 were waited for; matrix products, arithmetic and copies ran while one was open for 27% of the time, Pallas kernels for 0%

commit v1 on v0

v1 whole, which is shorter than its diff:
```python
import functools
import math

import jax
import jax.numpy as jnp
from jax import lax
from jax.experimental import pallas as pl
from jax.experimental.pallas import tpu as pltpu
from jax.sharding import PartitionSpec as P


EDGE = 8
TAPS = 9
LANES = 128
PAIR = 2 * LANES
MAIN_TILES = 24
UNROLL = 8
TABLE_TILES = 8
PLACE_TILES = 32
EDGE_CHUNKS = 8


def sinc_taper(distance):
    in_reach = jnp.abs(distance) < 4.0
    turn = jnp.pi * distance
    ratio = jnp.where(distance == 0.0, 1.0, jnp.sin(turn) / jnp.where(distance == 0.0, 1.0, turn))
    shaped = ratio * (0.5 + 0.5 * jnp.cos(jnp.pi * distance / 4.0))
    return jnp.where(in_reach, shaped, jnp.zeros_like(distance))


def shift_list(chips):
    half = chips // 2
    rising = [k for k in (3, 5, 8, 13) if k < half]
    falling = [k for k in range(half - 1, 0, -1) if k not in rising]
    return [s * k for k in rising + falling for s in (1, -1)]


def chip_pairs(chips, shift):
    return [(2 * z + c, 2 * ((z + shift) % chips) + c) for z in range(chips) for c in range(2)]


def prepare_body(
    pos_ref, lines_ref, coef_ref, az_ref, rg_ref, dest_ref, valid_ref, first_ref, last_ref, meta_ref, edge_ref
):
    cols = lines_ref.shape[2]
    count = dest_ref.shape[1]
    low = jnp.where(valid_ref[...] > 0, first_ref[...], 2 * cols)
    high = last_ref[...]
    meta_ref[...] = jnp.zeros(meta_ref.shape, jnp.float32)
    meta_ref[0:3, :] = coef_ref[...]
    for row, value in enumerate((az_ref[...], rg_ref[...], dest_ref[...], low, high)):
        meta_ref[3 + row : 4 + row, :] = value.astype(jnp.float32)
    begin = pos_ref[1] * (count - EDGE)
    here = lax.broadcasted_iota(jnp.int32, (EDGE, count), 1) == lax.broadcasted_iota(jnp.int32, (EDGE, count), 0) + begin

    def upright(values):
        spread = jnp.where(here, values.astype(jnp.float32), 0.0)
        return jnp.sum(spread, axis=1, keepdims=True).astype(jnp.int32)

    low_at, high_at = upright(low), upright(high)
    width = cols // EDGE_CHUNKS
    for chunk in range(EDGE_CHUNKS):
        at = slice(chunk * width, (chunk + 1) * width)
        column = lax.broadcasted_iota(jnp.int32, (EDGE, width), 1) + chunk * width
        keep = (column >= low_at) & (column < high_at)
        for part in range(2):
            edge_ref[part, :, at] = jnp.where(keep, lines_ref[part, :, at].astype(jnp.float32), 0.0).astype(jnp.bfloat16)


def prepare_call(pos, secondary, az_coef, *vectors):
    lines, cols = secondary.shape[1:]
    flat = pl.BlockSpec((1, lines), lambda i, pos: (0, 0))
    return pl.pallas_call(
        prepare_body,
        grid_spec=pltpu.PrefetchScalarGridSpec(
            num_scalar_prefetch=1,
            grid=(1,),
            in_specs=[
                pl.BlockSpec((2, EDGE, cols), lambda i, pos: (0, pos[1] * (lines // EDGE - 1), 0)),
                pl.BlockSpec((3, lines), lambda i, pos: (0, 0)),
            ]
            + [flat] * len(vectors),
            out_specs=[
                pl.BlockSpec((16, lines), lambda i, pos: (0, 0)),
                pl.BlockSpec((2, EDGE, cols), lambda i, pos: (0, 0, 0)),
            ],
        ),
        out_shape=[
            jax.ShapeDtypeStruct((16, lines), jnp.float32),
            jax.ShapeDtypeStruct((2, EDGE, cols), jnp.bfloat16),
        ],
        name="prepare",
    )(pos, secondary, az_coef, *[v.reshape(1, lines) for v in vectors])


def table_body(cols, coef_ref, out_ref, taps_ref, whole_ref):
    step = pl.program_id(0)
    tiles = cols // LANES

    @pl.when(step == 0)
    def _():
        shape = (tiles, LANES)
        column = lax.broadcasted_iota(jnp.int32, shape, 0) * LANES + lax.broadcasted_iota(jnp.int32, shape, 1)
        v = (column.astype(jnp.float32) + 0.5) / cols
        offsets = coef_ref[0] + coef_ref[1] * v + coef_ref[2] * v * v + coef_ref[3] * v * v * v
        whole = jnp.round(offsets)
        part = offsets - whole
        whole_ref[...] = whole
        sine = jnp.sin(jnp.pi * part)
        cosine4 = jnp.cos(jnp.pi / 4.0 * part)
        sine4 = jnp.sin(jnp.pi / 4.0 * part)
        for k in range(TAPS):
            m = k - 4
            x = m - part
            turn = jnp.pi * x
            lifted = sine if m % 2 else -sine
            ratio = jnp.where(x == 0.0, 1.0, lifted / jnp.where(x == 0.0, 1.0, turn))
            taper = 0.5 + 0.5 * (math.cos(math.pi * m / 4) * cosine4 + math.sin(math.pi * m / 4) * sine4)
            value = jnp.where(jnp.abs(x) < 4.0, ratio * taper, 0.0)
            taps_ref[k] = value

    gap = (lax.broadcasted_iota(jnp.int32, (16, LANES), 0) - lax.broadcasted_iota(jnp.int32, (16, LANES), 1)).astype(jnp.float32)
    blank = jnp.zeros((16, LANES), jnp.bfloat16)
    pieces = [(16 * g, 16 * g) for g in range(8)] + [(LANES, LANES), (2 * LANES - 16, -16)]
    for tile in range(TABLE_TILES):
        at = pl.ds(step * TABLE_TILES + tile, 1)
        near = (gap - whole_ref[at, :]).astype(jnp.bfloat16)
        taps = [jnp.broadcast_to(taps_ref[k, at, :], (16, LANES)).astype(jnp.bfloat16) for k in range(TAPS)]
        for row, distance in pieces:
            total = blank
            for k in range(TAPS):
                total = jnp.where(near == jnp.bfloat16(k - 4 - distance), taps[k], total)
            out_ref[tile, row : row + 16, :] = total
        for g in range(1, 7):
            out_ref[tile, LANES + 16 * g : LANES + 16 * g + 16, :] = blank


def table_call(coef, cols):
    tiles = cols // LANES
    return pl.pallas_call(
        functools.partial(table_body, cols),
        grid=(tiles // TABLE_TILES,),
        in_specs=[pl.BlockSpec(memory_space=pltpu.SMEM)],
        out_specs=pl.BlockSpec((TABLE_TILES, PAIR, LANES), lambda i: (i, 0, 0)),
        out_shape=jax.ShapeDtypeStruct((tiles, PAIR, LANES), jnp.bfloat16),
        scratch_shapes=[pltpu.VMEM((TAPS, tiles, LANES), jnp.float32), pltpu.VMEM((tiles, LANES), jnp.float32)],
        name="range_table",
    )(coef)


def plan(chips, pos_ref, meta_ref, meta_sib_ref, lhs_ref, lhs_edge_ref, marks_ref):
    chip, core = pos_ref[0], pos_ref[1]
    lines = meta_ref.shape[1]
    count = 2 * lines
    row = lax.broadcasted_iota(jnp.int32, (count, lines), 0)
    turn = row // 4
    shift = jnp.where(turn == chips - 1, chips // 2, 0)
    for at, distance in enumerate(shift_list(chips)):
        shift = jnp.where(turn == at + 1, distance, shift)
    goal = chip + shift
    goal = 2 * jnp.where(goal < 0, goal + chips, jnp.where(goal >= chips, goal - chips, goal)) + core
    from_sib = (row // 2) % 2 == 1
    line = lax.broadcasted_iota(jnp.int32, (count, lines), 1)
    tap = lax.broadcasted_iota(jnp.int32, (16, lines), 0)
    along = lax.broadcasted_iota(jnp.int32, (16, lines), 1)
    picked = None
    for source, (ref, home) in enumerate(((meta_ref, core), (meta_sib_ref, 1 - core))):
        fraction = ref[0:1, :] + ref[1:2, :] * 0.5 + ref[2:3, :] * 0.5 * 0.5
        features = sinc_taper((tap - 4).astype(jnp.float32) - fraction)
        start = (along + home * lines - 4).astype(jnp.float32) + ref[3:4, :]
        features = jnp.where(tap < TAPS, features, jnp.where(tap == TAPS, start, ref[4:5, :]))
        owner = ref[5:6, :].astype(jnp.int32) // lines
        chosen = (owner == goal) & (from_sib if source else ~from_sib)
        found = lax.dot_general(
            jnp.where(chosen, 1.0, 0.0).astype(jnp.bfloat16),
            features.astype(jnp.bfloat16),
            (((1,), (1,)), ((), ())),
            preferred_element_type=jnp.float32,
        )
        picked = found if picked is None else picked + found
    begin = picked[:, TAPS : TAPS + 1]

    def band(coordinate, part):
        row_part = lax.broadcasted_iota(jnp.int32, part.shape, 0) % 2
        step = jnp.where(part == row_part, coordinate.astype(jnp.float32) - begin, -1.0)
        total = jnp.zeros(step.shape, jnp.float32)
        for k in range(TAPS):
            total = jnp.where(step == k, picked[:, k : k + 1], total)
        return total.astype(jnp.bfloat16)

    lane = lax.broadcasted_iota(jnp.int32, (count, count), 1)
    lhs_ref[:, 0:count] = band(lane % lines + core * lines, lane // lines)
    lhs_ref[:, count : 2 * count] = band(lane % lines + (1 - core) * lines, lane // lines)
    slot = lax.broadcasted_iota(jnp.int32, (count, 4 * EDGE), 1)
    high = (slot // (2 * EDGE) + core) % 2 == 1
    coordinate = slot % EDGE + jnp.where(high, 2 * lines, -EDGE)
    lhs_edge_ref[...] = band(coordinate, slot // EDGE % 2)

    level = line == row % lines
    for at, (ref, which) in enumerate(((meta_ref, 6), (meta_ref, 7), (meta_sib_ref, 6), (meta_sib_ref, 7))):
        upright = jnp.sum(jnp.where(level, ref[which : which + 1, :], 0.0), axis=1, keepdims=True)
        marks_ref[at] = jnp.broadcast_to(upright, (count, LANES)).astype(jnp.int32)
    marks_ref[4] = jnp.broadcast_to(picked[:, TAPS + 1 : TAPS + 2], (count, LANES)).astype(jnp.int32)


def filter_body(
    chips, steps, outs, pos_ref, meta_ref, meta_sib_ref, own_ref, sib_ref, near_ref, far_ref, table_ref, *rest
):
    out_refs, power_ref = rest[:outs], rest[outs]
    turned_ref, lhs_ref, lhs_edge_ref, marks_ref, squares_ref = rest[outs + 1 :]
    step = pl.program_id(0)
    lines = own_ref.shape[1]
    count = 2 * lines
    tiles = steps * MAIN_TILES

    @pl.when(step == 0)
    def _():
        plan(chips, pos_ref, meta_ref, meta_sib_ref, lhs_ref, lhs_edge_ref, marks_ref)
        zeros = jnp.zeros((count, LANES), jnp.float32)
        for row in (0, 1, tiles + 2, tiles + 3):
            turned_ref[row] = zeros
        squares_ref[...] = zeros

    lane = lax.broadcasted_iota(jnp.int32, (count, LANES), 1)
    source = lane + marks_ref[4]
    before = source < 0
    after = source >= LANES
    wrapped = source & (LANES - 1)

    @pl.when(step < steps)
    def _():
        def run(turn, _):
            for pair in range(UNROLL // 2):
                tile = turn * UNROLL + 2 * pair
                here = step * MAIN_TILES + tile
                both = pl.ds(pl.multiple_of(tile * LANES, PAIR), PAIR)

                def kept(ref, low, high):
                    values = ref[:, :, both].reshape(count, PAIR).astype(jnp.float32)
                    halves = []
                    for half in range(2):
                        column = lane + (here + half) * LANES
                        inside = (column >= marks_ref[low]) & (column < marks_ref[high])
                        value = values[:, half * LANES : (half + 1) * LANES]
                        halves.append(jnp.where(inside, value, 0.0).astype(jnp.bfloat16))
                    return jnp.concatenate(halves, axis=1)

                data = jnp.concatenate([kept(own_ref, 0, 1), kept(sib_ref, 2, 3)], axis=0)
                edges = jnp.concatenate(
                    [near_ref[:, :, both].reshape(2 * EDGE, PAIR), far_ref[:, :, both].reshape(2 * EDGE, PAIR)], axis=0
                )
                summed = jnp.dot(lhs_ref[...], data, preferred_element_type=jnp.float32)
                summed += jnp.dot(lhs_edge_ref[...], edges, preferred_element_type=jnp.float32)
                rounded = summed.astype(jnp.bfloat16).astype(jnp.float32)
                for half in range(2):
                    turned_ref[here + half + 2] = jnp.take_along_axis(
                        rounded[:, half * LANES : (half + 1) * LANES], wrapped, axis=1, mode="promise_in_bounds"
                    )
            return None

        lax.fori_loop(0, MAIN_TILES // UNROLL, run, None)

    def move(tile):
        here = jnp.where(before, turned_ref[tile + 1], jnp.where(after, turned_ref[tile + 3], turned_ref[tile + 2]))
        return jnp.where((tile >= 0) & (tile < tiles), here, 0.0)

    @pl.when(step > 0)
    def _():
        left = lane < LANES // 2
        first = (step - 1) * MAIN_TILES

        def run(turn, carry):
            squares, previous, middle = carry
            for inner in range(UNROLL):
                tile = turn * UNROLL + inner
                at = pl.ds(pl.multiple_of(tile * LANES, LANES), LANES)
                following = move(first + tile + 1)
                window = jnp.concatenate([middle, jnp.where(left, following, previous)], axis=1).astype(jnp.bfloat16)
                done = jnp.dot(window, table_ref[tile], preferred_element_type=jnp.float32).astype(jnp.bfloat16)
                wide = done.astype(jnp.float32)
                squares += wide * wide
                row = 0
                for ref in out_refs:
                    ref[:, at] = wide[row : row + ref.shape[0]].astype(jnp.bfloat16)
                    row += ref.shape[0]
                previous, middle = middle, following
            return squares, previous, middle

        start = (squares_ref[...], move(first - 1), move(first))
        squares_ref[...] = lax.fori_loop(0, MAIN_TILES // UNROLL, run, start)[0]

    @pl.when(step == steps)
    def _():
        power_ref[0] = jnp.sum(squares_ref[...])


def filter_call(chips, pos, meta, meta_sib, own, sib, near, far, table, row_counts):
    lines, cols = own.shape[1:]
    count = 2 * lines
    tiles = cols // LANES
    steps = tiles // MAIN_TILES
    block = MAIN_TILES * LANES

    def incoming(i):
        return (0, 0, jnp.minimum(i, steps - 1))

    def outgoing(i):
        return (0, jnp.maximum(i - 1, 0))

    smem = pl.BlockSpec(memory_space=pltpu.SMEM)
    return pl.pallas_call(
        functools.partial(filter_body, chips, steps, len(row_counts)),
        grid=(steps + 1,),
        in_specs=[
            smem,
            pl.BlockSpec(meta.shape, lambda i: (0, 0)),
            pl.BlockSpec(meta.shape, lambda i: (0, 0)),
            pl.BlockSpec((2, lines, block), incoming),
            pl.BlockSpec((2, lines, block), incoming),
            pl.BlockSpec((2, EDGE, block), incoming),
            pl.BlockSpec((2, EDGE, block), incoming),
            pl.BlockSpec((MAIN_TILES, PAIR, LANES), lambda i: (jnp.maximum(i - 1, 0), 0, 0)),
        ],
        out_specs=[pl.BlockSpec((rows, block), outgoing) for rows in row_counts] + [smem],
        out_shape=[jax.ShapeDtypeStruct((rows, cols), jnp.bfloat16) for rows in row_counts]
        + [jax.ShapeDtypeStruct((1,), jnp.float32)],
        scratch_shapes=[
            pltpu.VMEM((tiles + 4, count, LANES), jnp.float32),
            pltpu.VMEM((count, 2 * count), jnp.bfloat16),
            pltpu.VMEM((count, 4 * EDGE), jnp.bfloat16),
            pltpu.VMEM((5, count, LANES), jnp.int32),
            pltpu.VMEM((count, LANES), jnp.float32),
        ],
        name="line_filter",
    )(pos, meta, meta_sib, own, sib, near, far, table)


def place_body(ins, gain_ref, arrange_ref, *rest):
    in_refs, out_ref, rows_ref = rest[:ins], rest[ins], rest[ins + 1]
    row = 0
    for ref in in_refs:
        rows_ref[row : row + ref.shape[0], :] = ref[...].astype(jnp.float32)
        row += ref.shape[0]
    ordered = jnp.dot(arrange_ref[...], rows_ref[...].astype(jnp.bfloat16), preferred_element_type=jnp.float32)
    out_ref[...] = (ordered * gain_ref[0]).astype(jnp.bfloat16).reshape(out_ref.shape)


def place_call(gain, arrange, pieces, lines):
    cols = pieces[0].shape[1]
    block = PLACE_TILES * LANES
    return pl.pallas_call(
        functools.partial(place_body, len(pieces)),
        grid=(cols // block,),
        in_specs=[
            pl.BlockSpec(memory_space=pltpu.SMEM),
            pl.BlockSpec(arrange.shape, lambda i: (0, 0)),
        ]
        + [pl.BlockSpec((piece.shape[0], block), lambda i: (0, i)) for piece in pieces],
        out_specs=pl.BlockSpec((2, lines, block), lambda i: (0, 0, i)),
        out_shape=jax.ShapeDtypeStruct((2, lines, cols), jnp.bfloat16),
        scratch_shapes=[pltpu.VMEM((2 * lines, block), jnp.float32)],
        name="place_lines",
    )(gain, arrange, *pieces)


def shards(
    secondary, line_valid, first_valid, last_valid, az_coef, az_base, rg_base, rg_coef, block_dest
):
    lines, cols = secondary.shape[1:]
    devices = lax.axis_size("az")
    chips = devices // 2
    half = chips // 2
    me = lax.axis_index("az")
    chip, core = me // 2, me % 2
    pos = jnp.stack([chip, core]).astype(jnp.int32)
    sibling = [(i, i ^ 1) for i in range(devices)]
    order = shift_list(chips)

    sib = lax.ppermute(secondary, "az", sibling)
    meta, edge = prepare_call(
        pos, secondary, az_coef, az_base, rg_base, block_dest, line_valid, first_valid, last_valid
    )
    across = [(2 * z + 1, 2 * z + 2) for z in range(chips - 1)] + [(2 * z + 2, 2 * z + 1) for z in range(chips - 1)]
    along = [(2 * z + 1, 2 * z + 3) for z in range(chips - 1)] + [(2 * z + 2, 2 * z) for z in range(chips - 1)]
    near = lax.ppermute(edge, "az", across)
    far = lax.ppermute(edge, "az", along)
    meta_sib = lax.ppermute(meta, "az", sibling)
    table = table_call(rg_coef, cols)

    rows = [4] * (len(order) + 1) + [2, 2]
    *made, power = filter_call(chips, pos, meta, meta_sib, secondary, sib, near, far, table, rows)

    up = lax.ppermute(made[-2], "az", chip_pairs(chips, half // 2))
    down = lax.ppermute(made[-1], "az", chip_pairs(chips, -(half // 2)))
    arrived = []
    for at, shift in enumerate(order):
        arrived.append(lax.ppermute(made[at + 1], "az", chip_pairs(chips, shift)))
    up, power, valid, first, last, dest = lax.optimization_barrier(
        (up, power, line_valid, first_valid, last_valid, block_dest)
    )
    up = lax.ppermute(up, "az", chip_pairs(chips, half - half // 2))
    down = lax.ppermute(down, "az", chip_pairs(chips, -(half - half // 2)))

    spans = jnp.maximum(last - first, 0)
    own_count = jnp.sum(jnp.where(valid > 0, spans, 0)).astype(jnp.float32)
    target = jnp.arange(devices, dtype=jnp.int32)[:, None]
    to_each = jnp.sum(jnp.where((dest // lines)[None] == target, (dest % lines)[None], 0), axis=1)
    sums = jnp.stack(
        [jnp.broadcast_to(power, (devices,)), jnp.broadcast_to(own_count, (devices,)), to_each.astype(jnp.float32)],
        axis=1,
    )
    gathered = lax.all_to_all(sums, "az", split_axis=0, concat_axis=0, tiled=True)
    totals = jnp.sum(gathered[:, :2], axis=0)
    total_power, total_count = totals[0], totals[1]
    mean_power = total_power / jnp.maximum(total_count, 1.0)
    power_gain = lax.rsqrt(mean_power + 0.5)

    shifts = jnp.array([0] + order + [half], jnp.int32)
    source_chip = (chip - shifts) % chips
    source = (2 * source_chip[:, None] + jnp.stack([core, 1 - core])[None]).reshape(-1)
    seat = jnp.sum(
        jnp.where(source[:, None] == jnp.arange(devices, dtype=jnp.int32)[None], gathered[:, 2][None], 0.0), axis=1
    )
    spot = jnp.repeat(seat, 2)[None] + jnp.tile(jnp.arange(2, dtype=jnp.float32) * lines, lines)[None]
    arrange = (spot == jnp.arange(2 * lines, dtype=jnp.float32)[:, None]).astype(jnp.bfloat16)
    coregistered = place_call(power_gain.reshape(1), arrange, [made[0]] + arrived + [up, down], lines)
    valid_share = total_count / float(cols * lines * devices)
    return (coregistered, mean_power.reshape(1), valid_share.reshape(1))


def solution(mesh):
    placed = (
        P(None, ("scene", "az"), None),
        P(("scene", "az")),
        P(("scene", "az")),
        P(("scene", "az")),
        P(None, ("scene", "az")),
        P(("scene", "az")),
        P(("scene", "az")),
        P("scene"),
        P(("scene", "az")),
    )
    return jax.shard_map(
        shards,
        mesh=mesh,
        in_specs=placed,
        out_specs=(P(None, ("scene", "az"), None), P("scene"), P("scene")),
        check_vma=False,
    )
```

time: 483 us -> 381 us (0.79)
  starting transfers between devices: 73.8 us -> 232 us
  waiting for transfers between devices: 217 us -> 100 us
  other arithmetic: 98.3 us -> 5.67 us
  matrix products: 56 us -> 0 us
  Pallas kernels: 0 us -> 30.9 us
  local copies, waits for them, and re-layouts: 25.7 us -> 4.56 us
    all_to_all x3 -> x1, waiting for transfers between devices: 216 us -> 0.01 us  [shards(): lax.all_to_all(sums, 'az', split_axis=0, concat_axis=0, tiled=True)]
    ppermute x2 -> x38, starting transfers between devices: 3.88 us -> 208 us  [the longest x30 164 us: shards(): arrived.append(lax.ppermute(made[at + 1], 'az', chip_pairs(chips, shift)))]
    ppermute x2 -> x38, waiting for transfers between devices: 1.05 us -> 100 us  [the longest x30 98.3 us: shards(): arrived.append(lax.ppermute(made[at + 1], 'az', chip_pairs(chips, shift)))]
    convert_element_type x2, other arithmetic: 86.2 us -> 0.63 us  [the longest x1 0.62 us: shards(): (spot == jnp.arange(2 * lines, dtype=jnp.float32)[:, None]).astype(jnp.bf...]
    dot_general x21 -> x0, matrix products: 56 us -> none  [the longest x17 30.7 us: shards(): jnp.einsum('rs,psc->rpc', picked, padded[:, :, RBMAX + shift:RBMAX + shif...]
    all_to_all x3 -> x1, starting transfers between devices: 69.9 us -> 24.3 us  [shards(): lax.all_to_all(sums, 'az', split_axis=0, concat_axis=0, tiled=True)]
    pallas_call x0 -> x4, Pallas kernels: none -> 30.9 us  [the longest x1 15.2 us: filter_call(): pl.pallas_call(functools.partial(filter_body, chips, steps, len(row_count...]
    another operation x2 -> x0, local copies, waits for them, and re-layouts: 12.6 us -> none  [range_apply(): tiled_rows = lines.reshape(lines.shape[:-1] + (tile_total, 128))]
  transfers between devices with their start and end apart: 5 -> 39, of which waited for: 3 -> 10; matrix products, arithmetic and copies ran while one was open for 27% -> 2% of each run, Pallas kernels for 0% -> 3%
where the time goes in v1:
time: 381 us; the launch traced here: 380 us
  starting transfers between devices  232 us (61%)
  waiting for transfers between devices  100 us (26%)
  Pallas kernels  30.9 us (8%)
  between operations  6.01 us (2%)
  other arithmetic  5.67 us (1%)
  local copies, waits for them, and re-layouts  4.56 us (1%)
    ppermute x30, starting transfers between devices, shards(): arrived.append(lax.ppermute(made[at + 1], 'az', chip_pairs(chips, shift)))  164 us
    ppermute x30, waiting for transfers between devices, shards(): arrived.append(lax.ppermute(made[at + 1], 'az', chip_pairs(chips, shift)))  98.3 us
    all_to_all x1, starting transfers between devices, shards(): lax.all_to_all(sums, 'az', split_axis=0, concat_axis=0, tiled=True)  24.3 us
    ppermute x1, starting transfers between devices, shards(): up = lax.ppermute(made[-2], 'az', chip_pairs(chips, half // 2))  16.3 us
    pallas_call x1, Pallas kernels, filter_call(): pl.pallas_call(functools.partial(filter_body, chips, steps, len(row_count...  15.2 us
    ppermute x1, starting transfers between devices, shards(): down = lax.ppermute(made[-1], 'az', chip_pairs(chips, -(half // 2)))  10.5 us
    ppermute x1, starting transfers between devices, shards(): up = lax.ppermute(up, 'az', chip_pairs(chips, half - half // 2))  9.53 us
    pallas_call x1, Pallas kernels, table_call(): pl.pallas_call(functools.partial(table_body, cols), grid=(tiles // TABLE_...  7.91 us
  transfers between devices with their start and end apart: 39, of which 10 were waited for; matrix products, arithmetic and copies ran while one was open for 2% of the time, Pallas kernels for 3%

profile of v1, /device:TPU:46, one launch (start us, length us, event | category | flops | bytes accessed | tf_op | source)
XLA Modules:
  0.0 379.9 jit_solution(10559038575003447444)
XLA Ops:
  1.5 2.7 prepare.1
  4.1 1.3 collective-permute-start.3
  5.4 1.4 collective-permute-start.2
  6.8 3.6 collective-permute-start
  11.6 7.9 %range_table.1.table_ref = bf16[96,256,128]{2,1,0:T(8,128)(2,1)} custom-call(f32[4]{0:T(128)} %coef_ref.3), custom_call_target="tpu_custom_call" | custom-call | tf_op jit(solution)/shard_map/range_table/pallas_call | solution.py:140
  20.3 1.7 copy-done
  21.9 15.2 %line_filter.1 = (bf16[4,12288]{1,0:T(4,128)(2,1)}, bf16[4,12288]{1,0:T(4,128)(2,1)}, bf16[4,12288]{1,0:T(4,128)(2,1)}, bf16[4,12288]{1,0:T(4,128)(2,1)}, bf16[4...) custom-call(s32[2]{0:T(128)} %pad_add_fusion.pos_ref, ...), custom_call_target="tpu_custom_call" | custom-call | tf_op jit(solution)/shard_map/line_filter/pallas_call | solution.py:311
  37.2 16.3 %collective-permute-start.4 = (bf16[2,12288]{1,0:T(2,128)(2,1)}, bf16[2,12288]{1,0:T(2,128)(2,1)S(1)}, u32[]{:S(2)}, u32[]{:S(2)}) collective-permute-start(bf16[2,12288]{1,0:T(2,128)(2,1)} %get-tuple-element.47), channel_id=1, source_target_pairs={{0,16},{1,17},{2,18},{3,19},{4,20},{5,21},{6,22},{7,23},{8,24},{9,... | collective-permute-start | bytes 147464 | tf_op jit(solution)/shard_map/ppermute | solution.py:393
  54.2 10.5 %collective-permute-start.36 = (bf16[2,12288]{1,0:T(2,128)(2,1)}, bf16[2,12288]{1,0:T(2,128)(2,1)S(1)}, u32[]{:S(2)}, u32[]{:S(2)}) collective-permute-start(bf16[2,12288]{1,0:T(2,128)(2,1)} %get-tuple-element.86), channel_id=1, source_target_pairs={{0,48},{1,49},{2,50},{3,51},{4,52},{5,53},{6,54},{7,55},{8,56},{9,... | collective-permute-start | bytes 147464 | tf_op jit(solution)/shard_map/ppermute | solution.py:394
  64.7 2.1 collective-permute-done.4
  66.8 1.3 and_select_fusion.2
  70.5 24.3 %all-to-all-start = ((f32[64,1,3]{2,1,0:T(1,128)}), f32[64,1,3]{2,1,0:T(1,128)S(1)}, u32[]{:S(2)}, u32[]{:S(2)}) async-start(f32[64,1,3]{2,1,0:T(1,128)} %copy.15), calls=%async_computation | async-start | bytes 65536 | tf_op jit(solution)/shard_map/all_to_all | solution.py:412
  94.7 9.5 %collective-permute-start.35 = (bf16[2,12288]{1,0:T(2,128)(2,1)S(1)}, bf16[2,12288]{1,0:T(2,128)(2,1)S(1)}, u32[]{:S(2)}, u32[]{:S(2)}) collective-permute-start(bf16[2,12288]{1,0:T(2,128)(2,1)S(1)} %collective-permute-done.4), channel_id=1, source_target_pairs={{0,16},{1,17},{2,18},{3,19},{4,20},{5,21},{6,22},{7,23},{8,24},{9,... | collective-permute-start | bytes 147464 | tf_op jit(solution)/shard_map/ppermute | solution.py:401
  104.3 1.3 collective-permute-start.37
  105.7 2.6 collective-permute-start.5
  108.3 2.5 collective-permute-start.6
  110.9 5.5 %collective-permute-start.7 = (bf16[4,12288]{1,0:T(4,128)(2,1)}, bf16[4,12288]{1,0:T(4,128)(2,1)S(1)}, u32[]{:S(2)}, u32[]{:S(2)}) collective-permute-start(bf16[4,12288]{1,0:T(4,128)(2,1)} %get-tuple-element.57), channel_id=1, source_target_pairs={{0,10},{1,11},{2,12},{3,13},{4,14},{5,15},{6,16},{7,17},{8,18},{9,... | collective-permute-start | bytes 294920 | tf_op jit(solution)/shard_map/ppermute | solution.py:397
  116.4 7.2 %collective-permute-start.8 = (bf16[4,12288]{1,0:T(4,128)(2,1)}, bf16[4,12288]{1,0:T(4,128)(2,1)S(1)}, u32[]{:S(2)}, u32[]{:S(2)}) collective-permute-start(bf16[4,12288]{1,0:T(4,128)(2,1)} %get-tuple-element.58), channel_id=1, source_target_pairs={{0,54},{1,55},{2,56},{3,57},{4,58},{5,59},{6,60},{7,61},{8,62},{9,... | collective-permute-start | bytes 294920 | tf_op jit(solution)/shard_map/ppermute | solution.py:397
  123.5 8.4 %collective-permute-start.9 = (bf16[4,12288]{1,0:T(4,128)(2,1)}, bf16[4,12288]{1,0:T(4,128)(2,1)S(1)}, u32[]{:S(2)}, u32[]{:S(2)}) collective-permute-start(bf16[4,12288]{1,0:T(4,128)(2,1)} %get-tuple-element.59), channel_id=1, source_target_pairs={{0,16},{1,17},{2,18},{3,19},{4,20},{5,21},{6,22},{7,23},{8,24},{9,... | collective-permute-start | bytes 294920 | tf_op jit(solution)/shard_map/ppermute | solution.py:397
  132.1 2.5 collective-permute-start.10
  134.6 10.7 %collective-permute-start.11 = (bf16[4,12288]{1,0:T(4,128)(2,1)}, bf16[4,12288]{1,0:T(4,128)(2,1)S(1)}, u32[]{:S(2)}, u32[]{:S(2)}) collective-permute-start(bf16[4,12288]{1,0:T(4,128)(2,1)} %get-tuple-element.61), channel_id=1, source_target_pairs={{0,26},{1,27},{2,28},{3,29},{4,30},{5,31},{6,32},{7,33},{8,34},{9,... | collective-permute-start | bytes 294920 | tf_op jit(solution)/shard_map/ppermute | solution.py:397
  145.3 7.0 %collective-permute-start.12 = (bf16[4,12288]{1,0:T(4,128)(2,1)}, bf16[4,12288]{1,0:T(4,128)(2,1)S(1)}, u32[]{:S(2)}, u32[]{:S(2)}) collective-permute-start(bf16[4,12288]{1,0:T(4,128)(2,1)} %get-tuple-element.62), channel_id=1, source_target_pairs={{0,38},{1,39},{2,40},{3,41},{4,42},{5,43},{6,44},{7,45},{8,46},{9,... | collective-permute-start | bytes 294920 | tf_op jit(solution)/shard_map/ppermute | solution.py:397
  152.3 10.3 %collective-permute-start.13 = (bf16[4,12288]{1,0:T(4,128)(2,1)}, bf16[4,12288]{1,0:T(4,128)(2,1)S(1)}, u32[]{:S(2)}, u32[]{:S(2)}) collective-permute-start(bf16[4,12288]{1,0:T(4,128)(2,1)} %get-tuple-element.63), channel_id=1, source_target_pairs={{0,30},{1,31},{2,32},{3,33},{4,34},{5,35},{6,36},{7,37},{8,38},{9,... | collective-permute-start | bytes 294920 | tf_op jit(solution)/shard_map/ppermute | solution.py:397
  162.6 9.1 %collective-permute-start.14 = (bf16[4,12288]{1,0:T(4,128)(2,1)}, bf16[4,12288]{1,0:T(4,128)(2,1)S(1)}, u32[]{:S(2)}, u32[]{:S(2)}) collective-permute-start(bf16[4,12288]{1,0:T(4,128)(2,1)} %get-tuple-element.64), channel_id=1, source_target_pairs={{0,34},{1,35},{2,36},{3,37},{4,38},{5,39},{6,40},{7,41},{8,42},{9,... | collective-permute-start | bytes 294920 | tf_op jit(solution)/shard_map/ppermute | solution.py:397
  171.9 10.2 %collective-permute-start.15 = (bf16[4,12288]{1,0:T(4,128)(2,1)}, bf16[4,12288]{1,0:T(4,128)(2,1)S(1)}, u32[]{:S(2)}, u32[]{:S(2)}) collective-permute-start(bf16[4,12288]{1,0:T(4,128)(2,1)} %get-tuple-element.65), channel_id=1, source_target_pairs={{0,28},{1,29},{2,30},{3,31},{4,32},{5,33},{6,34},{7,35},{8,36},{9,... | collective-permute-start | bytes 294920 | tf_op jit(solution)/shard_map/ppermute | solution.py:397
  182.1 9.0 %collective-permute-done.11.rest_7_ = bf16[4,12288]{1,0:T(4,128)(2,1)S(1)} collective-permute-done((bf16[4,12288]{1,0:T(4,128)(2,1)}, bf16[4,12288]{1,0:T(4,128)(2,1)S(1)}, u32[]{:S(2)}, u32[]{:S(2)}) %collective-permute-start.11) | collective-permute-done | bytes 98336 | tf_op jit(solution)/shard_map/ppermute | solution.py:397
  191.2 13.5 %collective-permute-start.16 = (bf16[4,12288]{1,0:T(4,128)(2,1)}, bf16[4,12288]{1,0:T(4,128)(2,1)S(1)}, u32[]{:S(2)}, u32[]{:S(2)}) collective-permute-start(bf16[4,12288]{1,0:T(4,128)(2,1)} %get-tuple-element.66), channel_id=1, source_target_pairs={{0,36},{1,37},{2,38},{3,39},{4,40},{5,41},{6,42},{7,43},{8,44},{9,... | collective-permute-start | bytes 294920 | tf_op jit(solution)/shard_map/ppermute | solution.py:397
  204.7 16.8 %collective-permute-done.13.rest_9_ = bf16[4,12288]{1,0:T(4,128)(2,1)S(1)} collective-permute-done((bf16[4,12288]{1,0:T(4,128)(2,1)}, bf16[4,12288]{1,0:T(4,128)(2,1)S(1)}, u32[]{:S(2)}, u32[]{:S(2)}) %collective-permute-start.13) | collective-permute-done | bytes 98336 | tf_op jit(solution)/shard_map/ppermute | solution.py:397
  221.5 2.1 collective-permute-start.18
  223.6 9.2 %collective-permute-done.14.rest_10_ = bf16[4,12288]{1,0:T(4,128)(2,1)S(1)} collective-permute-done((bf16[4,12288]{1,0:T(4,128)(2,1)}, bf16[4,12288]{1,0:T(4,128)(2,1)S(1)}, u32[]{:S(2)}, u32[]{:S(2)}) %collective-permute-start.14) | collective-permute-done | bytes 98336 | tf_op jit(solution)/shard_map/ppermute | solution.py:397
  233.0 17.3 %collective-permute-done.15.rest_11_ = bf16[4,12288]{1,0:T(4,128)(2,1)S(1)} collective-permute-done((bf16[4,12288]{1,0:T(4,128)(2,1)}, bf16[4,12288]{1,0:T(4,128)(2,1)S(1)}, u32[]{:S(2)}, u32[]{:S(2)}) %collective-permute-start.15) | collective-permute-done | bytes 98336 | tf_op jit(solution)/shard_map/ppermute | solution.py:397
  250.4 6.0 %collective-permute-start.21 = (bf16[4,12288]{1,0:T(4,128)(2,1)}, bf16[4,12288]{1,0:T(4,128)(2,1)S(1)}, u32[]{:S(2)}, u32[]{:S(2)}) collective-permute-start(bf16[4,12288]{1,0:T(4,128)(2,1)} %get-tuple-element.71), channel_id=1, source_target_pairs={{0,20},{1,21},{2,22},{3,23},{4,24},{5,25},{6,26},{7,27},{8,28},{9,... | collective-permute-start | bytes 294920 | tf_op jit(solution)/shard_map/ppermute | solution.py:397
  256.3 18.0 %collective-permute-done.17.rest_13_ = bf16[4,12288]{1,0:T(4,128)(2,1)S(1)} collective-permute-done((bf16[4,12288]{1,0:T(4,128)(2,1)}, bf16[4,12288]{1,0:T(4,128)(2,1)S(1)}, u32[]{:S(2)}, u32[]{:S(2)}) %collective-permute-start.17) | collective-permute-done | bytes 98336 | tf_op jit(solution)/shard_map/ppermute | solution.py:397
  274.3 6.5 %collective-permute-start.22 = (bf16[4,12288]{1,0:T(4,128)(2,1)}, bf16[4,12288]{1,0:T(4,128)(2,1)S(1)}, u32[]{:S(2)}, u32[]{:S(2)}) collective-permute-start(bf16[4,12288]{1,0:T(4,128)(2,1)} %get-tuple-element.72), channel_id=1, source_target_pairs={{0,44},{1,45},{2,46},{3,47},{4,48},{5,49},{6,50},{7,51},{8,52},{9,... | collective-permute-start | bytes 294920 | tf_op jit(solution)/shard_map/ppermute | solution.py:397
  280.8 3.3 collective-permute-start.23
  284.1 21.2 %collective-permute-done.19.rest_15_ = bf16[4,12288]{1,0:T(4,128)(2,1)S(1)} collective-permute-done((bf16[4,12288]{1,0:T(4,128)(2,1)}, bf16[4,12288]{1,0:T(4,128)(2,1)S(1)}, u32[]{:S(2)}, u32[]{:S(2)}) %collective-permute-start.19) | collective-permute-done | bytes 98336 | tf_op jit(solution)/shard_map/ppermute | solution.py:397
  306.3 11.0 %collective-permute-start.25 = (bf16[4,12288]{1,0:T(4,128)(2,1)}, bf16[4,12288]{1,0:T(4,128)(2,1)S(1)}, u32[]{:S(2)}, u32[]{:S(2)}) collective-permute-start(bf16[4,12288]{1,0:T(4,128)(2,1)} %get-tuple-element.75), channel_id=1, source_target_pairs={{0,14},{1,15},{2,16},{3,17},{4,18},{5,19},{6,20},{7,21},{8,22},{9,... | collective-permute-start | bytes 294920 | tf_op jit(solution)/shard_map/ppermute | solution.py:397
  317.3 14.5 %collective-permute-start.27 = (bf16[4,12288]{1,0:T(4,128)(2,1)}, bf16[4,12288]{1,0:T(4,128)(2,1)S(1)}, u32[]{:S(2)}, u32[]{:S(2)}) collective-permute-start(bf16[4,12288]{1,0:T(4,128)(2,1)} %get-tuple-element.77), channel_id=1, source_target_pairs={{0,12},{1,13},{2,14},{3,15},{4,16},{5,17},{6,18},{7,19},{8,20},{9,... | collective-permute-start | bytes 294920 | tf_op jit(solution)/shard_map/ppermute | solution.py:397
  331.9 3.8 collective-permute-start.28
  335.6 6.9 %collective-permute-start.29 = (bf16[4,12288]{1,0:T(4,128)(2,1)}, bf16[4,12288]{1,0:T(4,128)(2,1)S(1)}, u32[]{:S(2)}, u32[]{:S(2)}) collective-permute-start(bf16[4,12288]{1,0:T(4,128)(2,1)} %get-tuple-element.79), channel_id=1, source_target_pairs={{0,8},{1,9},{2,10},{3,11},{4,12},{5,13},{6,14},{7,15},{8,16},{9,17... | collective-permute-start | bytes 294920 | tf_op jit(solution)/shard_map/ppermute | solution.py:397
  342.6 3.2 collective-permute-start.30
  345.8 5.9 %collective-permute-start.31 = (bf16[4,12288]{1,0:T(4,128)(2,1)}, bf16[4,12288]{1,0:T(4,128)(2,1)S(1)}, u32[]{:S(2)}, u32[]{:S(2)}) collective-permute-start(bf16[4,12288]{1,0:T(4,128)(2,1)} %get-tuple-element.81), channel_id=1, source_target_pairs={{0,4},{1,5},{2,6},{3,7},{4,8},{5,9},{6,10},{7,11},{8,12},{9,13},{1... | collective-permute-start | bytes 294920 | tf_op jit(solution)/shard_map/ppermute | solution.py:397
  351.7 3.6 collective-permute-start.32
  355.3 5.5 %collective-permute-start.33 = (bf16[4,12288]{1,0:T(4,128)(2,1)}, bf16[4,12288]{1,0:T(4,128)(2,1)S(1)}, u32[]{:S(2)}, u32[]{:S(2)}) collective-permute-start(bf16[4,12288]{1,0:T(4,128)(2,1)} %get-tuple-element.83), channel_id=1, source_target_pairs={{0,2},{1,3},{2,4},{3,5},{4,6},{5,7},{6,8},{7,9},{8,10},{9,11},{10,... | collective-permute-start | bytes 294920 | tf_op jit(solution)/shard_map/ppermute | solution.py:397
  360.8 1.9 collective-permute-start.34
  365.3 2.4 collective-permute-done.30.rest_26_
  367.6 3.6 collective-permute-done.32.rest_28_
  372.5 5.1 %place_lines.1 = bf16[2,64,12288]{2,1,0:T(8,128)(2,1)} custom-call(f32[1]{0:T(128)S(6)} %rsqrt.4.gain_ref, bf16[128,128]{1,0:T(8,128)(2,1)} %fusion.arrange_ref, bf16[4,12288]{1,0:T(4,128)(2,1)} %get-tuple-element.54.rest_0_, bf16[4,12288]{1,0:T(4,128)(2,1)} %copy-done.2, bf16[4,12288]{1,0:T(4,128)(2,1)} %copy-done.3, bf16[4,12288]{1,0:T(4,128)(2,1)} %copy-done.4, ...), custom_call_target="tpu_custom_call" | custom-call | tf_op jit(solution)/shard_map/place_lines/pallas_call | solution.py:351
  (129 shorter events, 8.5 us)
Async XLA Ops:
  0.6 18.9 %collective-permute-start.1 = (bf16[2,64,12288]{2,1,0:T(8,128)(2,1)}, bf16[2,64,12288]{2,1,0:T(8,128)(2,1)S(1)}, u32[]{:S(2)}, u32[]{:S(2)}) collective-permute-start(bf16[2,64,12288]{2,1,0:T(8,128)(2,1)} %own_ref.1), channel_id=1, source_target_pairs={{0,1},{1,0},{2,3},{3,2},{4,5},{5,4},{6,7},{7,6},{8,9},{9,8},{10,11... | collective-permute-start | bytes 9437192 | tf_op jit(solution)/shard_map/ppermute | solution.py:379
  4.1 15.4 %collective-permute-start.3 = (bf16[2,8,12288]{2,1,0:T(8,128)(2,1)}, bf16[2,8,12288]{2,1,0:T(8,128)(2,1)S(1)}, u32[]{:S(2)}, u32[]{:S(2)}) collective-permute-start(bf16[2,8,12288]{2,1,0:T(8,128)(2,1)} %get-tuple-element.46), channel_id=1, source_target_pairs={{1,3},{3,5},{5,7},{7,9},{9,11},{11,13},{13,15},{15,17},{17,19},{19... | collective-permute-start | bytes 1179656 | tf_op jit(solution)/shard_map/ppermute | solution.py:386
  5.4 14.1 %collective-permute-start.2 = (bf16[2,8,12288]{2,1,0:T(8,128)(2,1)}, bf16[2,8,12288]{2,1,0:T(8,128)(2,1)}, u32[]{:S(2)}, u32[]{:S(2)}) collective-permute-start(bf16[2,8,12288]{2,1,0:T(8,128)(2,1)} %get-tuple-element.46), channel_id=1, source_target_pairs={{1,2},{3,4},{5,6},{7,8},{9,10},{11,12},{13,14},{15,16},{17,18},{19... | collective-permute-start | bytes 1179656 | tf_op jit(solution)/shard_map/ppermute | solution.py:385
  6.8 12.7 %collective-permute-start = (f32[16,64]{1,0:T(8,128)}, f32[16,64]{1,0:T(8,128)S(1)}, u32[]{:S(2)}, u32[]{:S(2)}) collective-permute-start(f32[16,64]{1,0:T(8,128)} %get-tuple-element.45.meta_ref), channel_id=1, source_target_pairs={{0,1},{1,0},{2,3},{3,2},{4,5},{5,4},{6,7},{7,6},{8,9},{9,8},{10,11... | collective-permute-start | bytes 12296 | tf_op jit(solution)/shard_map/ppermute | solution.py:387
  37.2 29.6 %collective-permute-start.4 = (bf16[2,12288]{1,0:T(2,128)(2,1)}, bf16[2,12288]{1,0:T(2,128)(2,1)S(1)}, u32[]{:S(2)}, u32[]{:S(2)}) collective-permute-start(bf16[2,12288]{1,0:T(2,128)(2,1)} %get-tuple-element.47), channel_id=1, source_target_pairs={{0,16},{1,17},{2,18},{3,19},{4,20},{5,21},{6,22},{7,23},{8,24},{9,... | collective-permute-start | bytes 147464 | tf_op jit(solution)/shard_map/ppermute | solution.py:393
  54.2 50.1 %collective-permute-start.36 = (bf16[2,12288]{1,0:T(2,128)(2,1)}, bf16[2,12288]{1,0:T(2,128)(2,1)S(1)}, u32[]{:S(2)}, u32[]{:S(2)}) collective-permute-start(bf16[2,12288]{1,0:T(2,128)(2,1)} %get-tuple-element.86), channel_id=1, source_target_pairs={{0,48},{1,49},{2,50},{3,51},{4,52},{5,53},{6,54},{7,55},{8,56},{9,... | collective-permute-start | bytes 147464 | tf_op jit(solution)/shard_map/ppermute | solution.py:394
  70.5 61.5 %all-to-all-start = ((f32[64,1,3]{2,1,0:T(1,128)}), f32[64,1,3]{2,1,0:T(1,128)S(1)}, u32[]{:S(2)}, u32[]{:S(2)}) async-start(f32[64,1,3]{2,1,0:T(1,128)} %copy.15), calls=%async_computation | async-start | bytes 65536 | tf_op jit(solution)/shard_map/all_to_all | solution.py:412
  94.7 21.6 %collective-permute-start.35 = (bf16[2,12288]{1,0:T(2,128)(2,1)S(1)}, bf16[2,12288]{1,0:T(2,128)(2,1)S(1)}, u32[]{:S(2)}, u32[]{:S(2)}) collective-permute-start(bf16[2,12288]{1,0:T(2,128)(2,1)S(1)} %collective-permute-done.4), channel_id=1, source_target_pairs={{0,16},{1,17},{2,18},{3,19},{4,20},{5,21},{6,22},{7,23},{8,24},{9,... | collective-permute-start | bytes 147464 | tf_op jit(solution)/shard_map/ppermute | solution.py:401
  104.3 19.3 %collective-permute-start.37 = (bf16[2,12288]{1,0:T(2,128)(2,1)S(1)}, bf16[2,12288]{1,0:T(2,128)(2,1)S(1)}, u32[]{:S(2)}, u32[]{:S(2)}) collective-permute-start(bf16[2,12288]{1,0:T(2,128)(2,1)S(1)} %collective-permute-done.36), channel_id=1, source_target_pairs={{0,48},{1,49},{2,50},{3,51},{4,52},{5,53},{6,54},{7,55},{8,56},{9,... | collective-permute-start | bytes 147464 | tf_op jit(solution)/shard_map/ppermute | solution.py:402
  105.7 26.4 %collective-permute-start.5 = (bf16[4,12288]{1,0:T(4,128)(2,1)}, bf16[4,12288]{1,0:T(4,128)(2,1)S(1)}, u32[]{:S(2)}, u32[]{:S(2)}) collective-permute-start(bf16[4,12288]{1,0:T(4,128)(2,1)} %get-tuple-element.55), channel_id=1, source_target_pairs={{0,6},{1,7},{2,8},{3,9},{4,10},{5,11},{6,12},{7,13},{8,14},{9,15},... | collective-permute-start | bytes 294920 | tf_op jit(solution)/shard_map/ppermute | solution.py:397
  108.3 26.3 %collective-permute-start.6 = (bf16[4,12288]{1,0:T(4,128)(2,1)}, bf16[4,12288]{1,0:T(4,128)(2,1)S(1)}, u32[]{:S(2)}, u32[]{:S(2)}) collective-permute-start(bf16[4,12288]{1,0:T(4,128)(2,1)} %get-tuple-element.56), channel_id=1, source_target_pairs={{0,58},{1,59},{2,60},{3,61},{4,62},{5,63},{6,0},{7,1},{8,2},{9,3},... | collective-permute-start | bytes 294920 | tf_op jit(solution)/shard_map/ppermute | solution.py:397
  110.9 34.4 %collective-permute-start.7 = (bf16[4,12288]{1,0:T(4,128)(2,1)}, bf16[4,12288]{1,0:T(4,128)(2,1)S(1)}, u32[]{:S(2)}, u32[]{:S(2)}) collective-permute-start(bf16[4,12288]{1,0:T(4,128)(2,1)} %get-tuple-element.57), channel_id=1, source_target_pairs={{0,10},{1,11},{2,12},{3,13},{4,14},{5,15},{6,16},{7,17},{8,18},{9,... | collective-permute-start | bytes 294920 | tf_op jit(solution)/shard_map/ppermute | solution.py:397
  116.4 255.5 %copy-start.32 = (bf16[2,12288]{1,0:T(2,128)(2,1)}, bf16[2,12288]{1,0:T(2,128)(2,1)S(1)}, u32[]{:S(2)}) copy-start(bf16[2,12288]{1,0:T(2,128)(2,1)S(1)} %collective-permute-done.35.rest_31_) | copy-start | bytes 147460
  116.4 35.9 %collective-permute-start.8 = (bf16[4,12288]{1,0:T(4,128)(2,1)}, bf16[4,12288]{1,0:T(4,128)(2,1)S(1)}, u32[]{:S(2)}, u32[]{:S(2)}) collective-permute-start(bf16[4,12288]{1,0:T(4,128)(2,1)} %get-tuple-element.58), channel_id=1, source_target_pairs={{0,54},{1,55},{2,56},{3,57},{4,58},{5,59},{6,60},{7,61},{8,62},{9,... | collective-permute-start | bytes 294920 | tf_op jit(solution)/shard_map/ppermute | solution.py:397
  123.5 248.4 %copy-start.33 = (bf16[2,12288]{1,0:T(2,128)(2,1)}, bf16[2,12288]{1,0:T(2,128)(2,1)S(1)}, u32[]{:S(2)}) copy-start(bf16[2,12288]{1,0:T(2,128)(2,1)S(1)} %collective-permute-done.37.rest_32_) | copy-start | bytes 147460
  123.5 39.0 %collective-permute-start.9 = (bf16[4,12288]{1,0:T(4,128)(2,1)}, bf16[4,12288]{1,0:T(4,128)(2,1)S(1)}, u32[]{:S(2)}, u32[]{:S(2)}) collective-permute-start(bf16[4,12288]{1,0:T(4,128)(2,1)} %get-tuple-element.59), channel_id=1, source_target_pairs={{0,16},{1,17},{2,18},{3,19},{4,20},{5,21},{6,22},{7,23},{8,24},{9,... | collective-permute-start | bytes 294920 | tf_op jit(solution)/shard_map/ppermute | solution.py:397
  132.1 239.8 %copy-start.2 = (bf16[4,12288]{1,0:T(4,128)(2,1)}, bf16[4,12288]{1,0:T(4,128)(2,1)S(1)}, u32[]{:S(2)}) copy-start(bf16[4,12288]{1,0:T(4,128)(2,1)S(1)} %collective-permute-done.5.rest_1_) | copy-start | bytes 294916
  132.1 39.8 %collective-permute-start.10 = (bf16[4,12288]{1,0:T(4,128)(2,1)}, bf16[4,12288]{1,0:T(4,128)(2,1)S(1)}, u32[]{:S(2)}, u32[]{:S(2)}) collective-permute-start(bf16[4,12288]{1,0:T(4,128)(2,1)} %get-tuple-element.60), channel_id=1, source_target_pairs={{0,48},{1,49},{2,50},{3,51},{4,52},{5,53},{6,54},{7,55},{8,56},{9,... | collective-permute-start | bytes 294920 | tf_op jit(solution)/shard_map/ppermute | solution.py:397
  134.6 237.3 %copy-start.3 = (bf16[4,12288]{1,0:T(4,128)(2,1)}, bf16[4,12288]{1,0:T(4,128)(2,1)S(1)}, u32[]{:S(2)}) copy-start(bf16[4,12288]{1,0:T(4,128)(2,1)S(1)} %collective-permute-done.6.rest_2_) | copy-start | bytes 294916
  134.6 56.6 %collective-permute-start.11 = (bf16[4,12288]{1,0:T(4,128)(2,1)}, bf16[4,12288]{1,0:T(4,128)(2,1)S(1)}, u32[]{:S(2)}, u32[]{:S(2)}) collective-permute-start(bf16[4,12288]{1,0:T(4,128)(2,1)} %get-tuple-element.61), channel_id=1, source_target_pairs={{0,26},{1,27},{2,28},{3,29},{4,30},{5,31},{6,32},{7,33},{8,34},{9,... | collective-permute-start | bytes 294920 | tf_op jit(solution)/shard_map/ppermute | solution.py:397
  145.3 226.6 %copy-start.4 = (bf16[4,12288]{1,0:T(4,128)(2,1)}, bf16[4,12288]{1,0:T(4,128)(2,1)S(1)}, u32[]{:S(2)}) copy-start(bf16[4,12288]{1,0:T(4,128)(2,1)S(1)} %collective-permute-done.7.rest_3_) | copy-start | bytes 294916
  145.3 59.4 %collective-permute-start.12 = (bf16[4,12288]{1,0:T(4,128)(2,1)}, bf16[4,12288]{1,0:T(4,128)(2,1)S(1)}, u32[]{:S(2)}, u32[]{:S(2)}) collective-permute-start(bf16[4,12288]{1,0:T(4,128)(2,1)} %get-tuple-element.62), channel_id=1, source_target_pairs={{0,38},{1,39},{2,40},{3,41},{4,42},{5,43},{6,44},{7,45},{8,46},{9,... | collective-permute-start | bytes 294920 | tf_op jit(solution)/shard_map/ppermute | solution.py:397
  152.3 219.7 %copy-start.5 = (bf16[4,12288]{1,0:T(4,128)(2,1)}, bf16[4,12288]{1,0:T(4,128)(2,1)S(1)}, u32[]{:S(2)}) copy-start(bf16[4,12288]{1,0:T(4,128)(2,1)S(1)} %collective-permute-done.8.rest_4_) | copy-start | bytes 294916
  152.3 69.2 %collective-permute-start.13 = (bf16[4,12288]{1,0:T(4,128)(2,1)}, bf16[4,12288]{1,0:T(4,128)(2,1)S(1)}, u32[]{:S(2)}, u32[]{:S(2)}) collective-permute-start(bf16[4,12288]{1,0:T(4,128)(2,1)} %get-tuple-element.63), channel_id=1, source_target_pairs={{0,30},{1,31},{2,32},{3,33},{4,34},{5,35},{6,36},{7,37},{8,38},{9,... | collective-permute-start | bytes 294920 | tf_op jit(solution)/shard_map/ppermute | solution.py:397
  162.6 209.4 %copy-start.6 = (bf16[4,12288]{1,0:T(4,128)(2,1)}, bf16[4,12288]{1,0:T(4,128)(2,1)S(1)}, u32[]{:S(2)}) copy-start(bf16[4,12288]{1,0:T(4,128)(2,1)S(1)} %collective-permute-done.9.rest_5_) | copy-start | bytes 294916
  162.6 70.2 %collective-permute-start.14 = (bf16[4,12288]{1,0:T(4,128)(2,1)}, bf16[4,12288]{1,0:T(4,128)(2,1)S(1)}, u32[]{:S(2)}, u32[]{:S(2)}) collective-permute-start(bf16[4,12288]{1,0:T(4,128)(2,1)} %get-tuple-element.64), channel_id=1, source_target_pairs={{0,34},{1,35},{2,36},{3,37},{4,38},{5,39},{6,40},{7,41},{8,42},{9,... | collective-permute-start | bytes 294920 | tf_op jit(solution)/shard_map/ppermute | solution.py:397
  171.9 200.1 %copy-start.7 = (bf16[4,12288]{1,0:T(4,128)(2,1)}, bf16[4,12288]{1,0:T(4,128)(2,1)S(1)}, u32[]{:S(2)}) copy-start(bf16[4,12288]{1,0:T(4,128)(2,1)S(1)} %collective-permute-done.10.rest_6_) | copy-start | bytes 294916
  171.9 78.4 %collective-permute-start.15 = (bf16[4,12288]{1,0:T(4,128)(2,1)}, bf16[4,12288]{1,0:T(4,128)(2,1)S(1)}, u32[]{:S(2)}, u32[]{:S(2)}) collective-permute-start(bf16[4,12288]{1,0:T(4,128)(2,1)} %get-tuple-element.65), channel_id=1, source_target_pairs={{0,28},{1,29},{2,30},{3,31},{4,32},{5,33},{6,34},{7,35},{8,36},{9,... | collective-permute-start | bytes 294920 | tf_op jit(solution)/shard_map/ppermute | solution.py:397
  191.2 180.8 %copy-start.8 = (bf16[4,12288]{1,0:T(4,128)(2,1)}, bf16[4,12288]{1,0:T(4,128)(2,1)S(1)}, u32[]{:S(2)}) copy-start(bf16[4,12288]{1,0:T(4,128)(2,1)S(1)} %collective-permute-done.11.rest_7_) | copy-start | bytes 294916
  191.2 59.2 %collective-permute-start.16 = (bf16[4,12288]{1,0:T(4,128)(2,1)}, bf16[4,12288]{1,0:T(4,128)(2,1)S(1)}, u32[]{:S(2)}, u32[]{:S(2)}) collective-permute-start(bf16[4,12288]{1,0:T(4,128)(2,1)} %get-tuple-element.66), channel_id=1, source_target_pairs={{0,36},{1,37},{2,38},{3,39},{4,40},{5,41},{6,42},{7,43},{8,44},{9,... | collective-permute-start | bytes 294920 | tf_op jit(solution)/shard_map/ppermute | solution.py:397
  204.7 69.7 %collective-permute-start.17 = (bf16[4,12288]{1,0:T(4,128)(2,1)}, bf16[4,12288]{1,0:T(4,128)(2,1)S(1)}, u32[]{:S(2)}, u32[]{:S(2)}) collective-permute-start(bf16[4,12288]{1,0:T(4,128)(2,1)} %get-tuple-element.67), channel_id=1, source_target_pairs={{0,24},{1,25},{2,26},{3,27},{4,28},{5,29},{6,30},{7,31},{8,32},{9,... | collective-permute-start | bytes 294920 | tf_op jit(solution)/shard_map/ppermute | solution.py:397
  221.5 59.3 %collective-permute-start.18 = (bf16[4,12288]{1,0:T(4,128)(2,1)}, bf16[4,12288]{1,0:T(4,128)(2,1)S(1)}, u32[]{:S(2)}, u32[]{:S(2)}) collective-permute-start(bf16[4,12288]{1,0:T(4,128)(2,1)} %get-tuple-element.68), channel_id=1, source_target_pairs={{0,40},{1,41},{2,42},{3,43},{4,44},{5,45},{6,46},{7,47},{8,48},{9,... | collective-permute-start | bytes 294920 | tf_op jit(solution)/shard_map/ppermute | solution.py:397
  232.8 72.5 %collective-permute-start.19 = (bf16[4,12288]{1,0:T(4,128)(2,1)}, bf16[4,12288]{1,0:T(4,128)(2,1)S(1)}, u32[]{:S(2)}, u32[]{:S(2)}) collective-permute-start(bf16[4,12288]{1,0:T(4,128)(2,1)} %get-tuple-element.69), channel_id=1, source_target_pairs={{0,22},{1,23},{2,24},{3,25},{4,26},{5,27},{6,28},{7,29},{8,30},{9,... | collective-permute-start | bytes 294920 | tf_op jit(solution)/shard_map/ppermute | solution.py:397
  250.4 56.0 %collective-permute-start.20 = (bf16[4,12288]{1,0:T(4,128)(2,1)}, bf16[4,12288]{1,0:T(4,128)(2,1)S(1)}, u32[]{:S(2)}, u32[]{:S(2)}) collective-permute-start(bf16[4,12288]{1,0:T(4,128)(2,1)} %get-tuple-element.70), channel_id=1, source_target_pairs={{0,42},{1,43},{2,44},{3,45},{4,46},{5,47},{6,48},{7,49},{8,50},{9,... | collective-permute-start | bytes 294920 | tf_op jit(solution)/shard_map/ppermute | solution.py:397
  250.4 66.9 %collective-permute-start.21 = (bf16[4,12288]{1,0:T(4,128)(2,1)}, bf16[4,12288]{1,0:T(4,128)(2,1)S(1)}, u32[]{:S(2)}, u32[]{:S(2)}) collective-permute-start(bf16[4,12288]{1,0:T(4,128)(2,1)} %get-tuple-element.71), channel_id=1, source_target_pairs={{0,20},{1,21},{2,22},{3,23},{4,24},{5,25},{6,26},{7,27},{8,28},{9,... | collective-permute-start | bytes 294920 | tf_op jit(solution)/shard_map/ppermute | solution.py:397
  274.3 43.0 %collective-permute-start.22 = (bf16[4,12288]{1,0:T(4,128)(2,1)}, bf16[4,12288]{1,0:T(4,128)(2,1)S(1)}, u32[]{:S(2)}, u32[]{:S(2)}) collective-permute-start(bf16[4,12288]{1,0:T(4,128)(2,1)} %get-tuple-element.72), channel_id=1, source_target_pairs={{0,44},{1,45},{2,46},{3,47},{4,48},{5,49},{6,50},{7,51},{8,52},{9,... | collective-permute-start | bytes 294920 | tf_op jit(solution)/shard_map/ppermute | solution.py:397
  280.8 51.0 %collective-permute-start.23 = (bf16[4,12288]{1,0:T(4,128)(2,1)}, bf16[4,12288]{1,0:T(4,128)(2,1)S(1)}, u32[]{:S(2)}, u32[]{:S(2)}) collective-permute-start(bf16[4,12288]{1,0:T(4,128)(2,1)} %get-tuple-element.73), channel_id=1, source_target_pairs={{0,18},{1,19},{2,20},{3,21},{4,22},{5,23},{6,24},{7,25},{8,26},{9,... | collective-permute-start | bytes 294920 | tf_op jit(solution)/shard_map/ppermute | solution.py:397
  305.3 30.3 %collective-permute-start.24 = (bf16[4,12288]{1,0:T(4,128)(2,1)}, bf16[4,12288]{1,0:T(4,128)(2,1)S(1)}, u32[]{:S(2)}, u32[]{:S(2)}) collective-permute-start(bf16[4,12288]{1,0:T(4,128)(2,1)} %get-tuple-element.74), channel_id=1, source_target_pairs={{0,46},{1,47},{2,48},{3,49},{4,50},{5,51},{6,52},{7,53},{8,54},{9,... | collective-permute-start | bytes 294920 | tf_op jit(solution)/shard_map/ppermute | solution.py:397
  306.3 36.2 %collective-permute-start.25 = (bf16[4,12288]{1,0:T(4,128)(2,1)}, bf16[4,12288]{1,0:T(4,128)(2,1)S(1)}, u32[]{:S(2)}, u32[]{:S(2)}) collective-permute-start(bf16[4,12288]{1,0:T(4,128)(2,1)} %get-tuple-element.75), channel_id=1, source_target_pairs={{0,14},{1,15},{2,16},{3,17},{4,18},{5,19},{6,20},{7,21},{8,22},{9,... | collective-permute-start | bytes 294920 | tf_op jit(solution)/shard_map/ppermute | solution.py:397
  317.3 28.5 %collective-permute-start.26 = (bf16[4,12288]{1,0:T(4,128)(2,1)}, bf16[4,12288]{1,0:T(4,128)(2,1)S(1)}, u32[]{:S(2)}, u32[]{:S(2)}) collective-permute-start(bf16[4,12288]{1,0:T(4,128)(2,1)} %get-tuple-element.76), channel_id=1, source_target_pairs={{0,50},{1,51},{2,52},{3,53},{4,54},{5,55},{6,56},{7,57},{8,58},{9,... | collective-permute-start | bytes 294920 | tf_op jit(solution)/shard_map/ppermute | solution.py:397
  317.3 34.3 %collective-permute-start.27 = (bf16[4,12288]{1,0:T(4,128)(2,1)}, bf16[4,12288]{1,0:T(4,128)(2,1)S(1)}, u32[]{:S(2)}, u32[]{:S(2)}) collective-permute-start(bf16[4,12288]{1,0:T(4,128)(2,1)} %get-tuple-element.77), channel_id=1, source_target_pairs={{0,12},{1,13},{2,14},{3,15},{4,16},{5,17},{6,18},{7,19},{8,20},{9,... | collective-permute-start | bytes 294920 | tf_op jit(solution)/shard_map/ppermute | solution.py:397
  331.9 23.4 %collective-permute-start.28 = (bf16[4,12288]{1,0:T(4,128)(2,1)}, bf16[4,12288]{1,0:T(4,128)(2,1)S(1)}, u32[]{:S(2)}, u32[]{:S(2)}) collective-permute-start(bf16[4,12288]{1,0:T(4,128)(2,1)} %get-tuple-element.78), channel_id=1, source_target_pairs={{0,52},{1,53},{2,54},{3,55},{4,56},{5,57},{6,58},{7,59},{8,60},{9,... | collective-permute-start | bytes 294920 | tf_op jit(solution)/shard_map/ppermute | solution.py:397
  335.6 25.1 %collective-permute-start.29 = (bf16[4,12288]{1,0:T(4,128)(2,1)}, bf16[4,12288]{1,0:T(4,128)(2,1)S(1)}, u32[]{:S(2)}, u32[]{:S(2)}) collective-permute-start(bf16[4,12288]{1,0:T(4,128)(2,1)} %get-tuple-element.79), channel_id=1, source_target_pairs={{0,8},{1,9},{2,10},{3,11},{4,12},{5,13},{6,14},{7,15},{8,16},{9,17... | collective-permute-start | bytes 294920 | tf_op jit(solution)/shard_map/ppermute | solution.py:397
  342.6 25.1 %collective-permute-start.30 = (bf16[4,12288]{1,0:T(4,128)(2,1)}, bf16[4,12288]{1,0:T(4,128)(2,1)S(1)}, u32[]{:S(2)}, u32[]{:S(2)}) collective-permute-start(bf16[4,12288]{1,0:T(4,128)(2,1)} %get-tuple-element.80), channel_id=1, source_target_pairs={{0,56},{1,57},{2,58},{3,59},{4,60},{5,61},{6,62},{7,63},{8,0},{9,1... | collective-permute-start | bytes 294920 | tf_op jit(solution)/shard_map/ppermute | solution.py:397
  345.8 21.9 %collective-permute-start.31 = (bf16[4,12288]{1,0:T(4,128)(2,1)}, bf16[4,12288]{1,0:T(4,128)(2,1)S(1)}, u32[]{:S(2)}, u32[]{:S(2)}) collective-permute-start(bf16[4,12288]{1,0:T(4,128)(2,1)} %get-tuple-element.81), channel_id=1, source_target_pairs={{0,4},{1,5},{2,6},{3,7},{4,8},{5,9},{6,10},{7,11},{8,12},{9,13},{1... | collective-permute-start | bytes 294920 | tf_op jit(solution)/shard_map/ppermute | solution.py:397
  351.7 19.6 %collective-permute-start.32 = (bf16[4,12288]{1,0:T(4,128)(2,1)}, bf16[4,12288]{1,0:T(4,128)(2,1)S(1)}, u32[]{:S(2)}, u32[]{:S(2)}) collective-permute-start(bf16[4,12288]{1,0:T(4,128)(2,1)} %get-tuple-element.82), channel_id=1, source_target_pairs={{0,60},{1,61},{2,62},{3,63},{4,0},{5,1},{6,2},{7,3},{8,4},{9,5},{1... | collective-permute-start | bytes 294920 | tf_op jit(solution)/shard_map/ppermute | solution.py:397
  355.3 16.0 %collective-permute-start.33 = (bf16[4,12288]{1,0:T(4,128)(2,1)}, bf16[4,12288]{1,0:T(4,128)(2,1)S(1)}, u32[]{:S(2)}, u32[]{:S(2)}) collective-permute-start(bf16[4,12288]{1,0:T(4,128)(2,1)} %get-tuple-element.83), channel_id=1, source_target_pairs={{0,2},{1,3},{2,4},{3,5},{4,6},{5,7},{6,8},{7,9},{8,10},{9,11},{10,... | collective-permute-start | bytes 294920 | tf_op jit(solution)/shard_map/ppermute | solution.py:397
  360.8 11.1 %collective-permute-start.34 = (bf16[4,12288]{1,0:T(4,128)(2,1)}, bf16[4,12288]{1,0:T(4,128)(2,1)S(1)}, u32[]{:S(2)}, u32[]{:S(2)}) collective-permute-start(bf16[4,12288]{1,0:T(4,128)(2,1)} %get-tuple-element.84), channel_id=1, source_target_pairs={{0,62},{1,63},{2,0},{3,1},{4,2},{5,3},{6,4},{7,5},{8,6},{9,7},{10,... | collective-permute-start | bytes 294920 | tf_op jit(solution)/shard_map/ppermute | solution.py:397
  (29 other events, 1431.7 us)

commit v2 on v1

--- a/solution.py
+++ b/solution.py
@@ -18,6 +18,7 @@
 TABLE_TILES = 8
 PLACE_TILES = 32
 EDGE_CHUNKS = 8
+AHEAD = 8
 
 
 def sinc_taper(distance):
@@ -30,7 +31,7 @@
 
 def shift_list(chips):
     half = chips // 2
-    rising = [k for k in (3, 5, 8, 13) if k < half]
+    rising = [k for k in (3, 5, 8, 15, 11) if k < half]
     falling = [k for k in range(half - 1, 0, -1) if k not in rising]
     return [s * k for k in rising + falling for s in (1, -1)]
 
@@ -148,19 +149,19 @@
     )(coef)
 
 
-def plan(chips, pos_ref, meta_ref, meta_sib_ref, lhs_ref, lhs_edge_ref, marks_ref):
+def plan(chips, shifts, pos_ref, meta_ref, meta_sib_ref, lhs_ref, lhs_edge_ref, marks_ref, moves_ref):
     chip, core = pos_ref[0], pos_ref[1]
     lines = meta_ref.shape[1]
     count = 2 * lines
-    row = lax.broadcasted_iota(jnp.int32, (count, lines), 0)
+    rows = 4 * len(shifts)
+    row = lax.broadcasted_iota(jnp.int32, (rows, lines), 0)
     turn = row // 4
-    shift = jnp.where(turn == chips - 1, chips // 2, 0)
-    for at, distance in enumerate(shift_list(chips)):
-        shift = jnp.where(turn == at + 1, distance, shift)
+    shift = jnp.zeros(turn.shape, jnp.int32)
+    for at, distance in enumerate(shifts):
+        shift = jnp.where(turn == at, distance, shift)
     goal = chip + shift
     goal = 2 * jnp.where(goal < 0, goal + chips, jnp.where(goal >= chips, goal - chips, goal)) + core
     from_sib = (row // 2) % 2 == 1
-    line = lax.broadcasted_iota(jnp.int32, (count, lines), 1)
     tap = lax.broadcasted_iota(jnp.int32, (16, lines), 0)
     along = lax.broadcasted_iota(jnp.int32, (16, lines), 1)
     picked = None
@@ -188,26 +189,27 @@
             total = jnp.where(step == k, picked[:, k : k + 1], total)
         return total.astype(jnp.bfloat16)
 
-    lane = lax.broadcasted_iota(jnp.int32, (count, count), 1)
+    lane = lax.broadcasted_iota(jnp.int32, (rows, count), 1)
     lhs_ref[:, 0:count] = band(lane % lines + core * lines, lane // lines)
     lhs_ref[:, count : 2 * count] = band(lane % lines + (1 - core) * lines, lane // lines)
-    slot = lax.broadcasted_iota(jnp.int32, (count, 4 * EDGE), 1)
+    slot = lax.broadcasted_iota(jnp.int32, (rows, 4 * EDGE), 1)
     high = (slot // (2 * EDGE) + core) % 2 == 1
     coordinate = slot % EDGE + jnp.where(high, 2 * lines, -EDGE)
     lhs_edge_ref[...] = band(coordinate, slot // EDGE % 2)
 
-    level = line == row % lines
+    line = lax.broadcasted_iota(jnp.int32, (count, lines), 1)
+    level = line == lax.broadcasted_iota(jnp.int32, (count, lines), 0) % lines
     for at, (ref, which) in enumerate(((meta_ref, 6), (meta_ref, 7), (meta_sib_ref, 6), (meta_sib_ref, 7))):
         upright = jnp.sum(jnp.where(level, ref[which : which + 1, :], 0.0), axis=1, keepdims=True)
         marks_ref[at] = jnp.broadcast_to(upright, (count, LANES)).astype(jnp.int32)
-    marks_ref[4] = jnp.broadcast_to(picked[:, TAPS + 1 : TAPS + 2], (count, LANES)).astype(jnp.int32)
+    moves_ref[...] = jnp.broadcast_to(picked[:, TAPS + 1 : TAPS + 2], (rows, LANES)).astype(jnp.int32)
 
 
 def filter_body(
-    chips, steps, outs, pos_ref, meta_ref, meta_sib_ref, own_ref, sib_ref, near_ref, far_ref, table_ref, *rest
+    chips, shifts, steps, outs, pos_ref, meta_ref, meta_sib_ref, own_ref, sib_ref, near_ref, far_ref, table_ref, *rest
 ):
     out_refs, power_ref = rest[:outs], rest[outs]
-    turned_ref, lhs_ref, lhs_edge_ref, marks_ref, squares_ref = rest[outs + 1 :]
+    turned_ref, lhs_ref, lhs_edge_ref, marks_ref, moves_ref, squares_ref = rest[outs + 1 :]
     step = pl.program_id(0)
     lines = own_ref.shape[1]
     count = 2 * lines
@@ -215,14 +217,15 @@
 
     @pl.when(step == 0)
     def _():
-        plan(chips, pos_ref, meta_ref, meta_sib_ref, lhs_ref, lhs_edge_ref, marks_ref)
-        zeros = jnp.zeros((count, LANES), jnp.float32)
+        plan(chips, shifts, pos_ref, meta_ref, meta_sib_ref, lhs_ref, lhs_edge_ref, marks_ref, moves_ref)
+        zeros = jnp.zeros(squares_ref.shape, jnp.float32)
         for row in (0, 1, tiles + 2, tiles + 3):
             turned_ref[row] = zeros
         squares_ref[...] = zeros
 
     lane = lax.broadcasted_iota(jnp.int32, (count, LANES), 1)
-    source = lane + marks_ref[4]
+    row_lane = lax.broadcasted_iota(jnp.int32, moves_ref.shape, 1)
+    source = row_lane + moves_ref[...]
     before = source < 0
     after = source >= LANES
     wrapped = source & (LANES - 1)
@@ -266,7 +269,7 @@
 
     @pl.when(step > 0)
     def _():
-        left = lane < LANES // 2
+        left = row_lane < LANES // 2
         first = (step - 1) * MAIN_TILES
 
         def run(turn, carry):
@@ -294,9 +297,10 @@
         power_ref[0] = jnp.sum(squares_ref[...])
 
 
-def filter_call(chips, pos, meta, meta_sib, own, sib, near, far, table, row_counts):
+def filter_call(chips, shifts, pos, meta, meta_sib, own, sib, near, far, table, row_counts):
     lines, cols = own.shape[1:]
     count = 2 * lines
+    made = sum(row_counts)
     tiles = cols // LANES
     steps = tiles // MAIN_TILES
     block = MAIN_TILES * LANES
@@ -309,7 +313,7 @@
 
     smem = pl.BlockSpec(memory_space=pltpu.SMEM)
     return pl.pallas_call(
-        functools.partial(filter_body, chips, steps, len(row_counts)),
+        functools.partial(filter_body, chips, shifts, steps, len(row_counts)),
         grid=(steps + 1,),
         in_specs=[
             smem,
@@ -325,11 +329,12 @@
         out_shape=[jax.ShapeDtypeStruct((rows, cols), jnp.bfloat16) for rows in row_counts]
         + [jax.ShapeDtypeStruct((1,), jnp.float32)],
         scratch_shapes=[
-            pltpu.VMEM((tiles + 4, count, LANES), jnp.float32),
-            pltpu.VMEM((count, 2 * count), jnp.bfloat16),
-            pltpu.VMEM((count, 4 * EDGE), jnp.bfloat16),
-            pltpu.VMEM((5, count, LANES), jnp.int32),
-            pltpu.VMEM((count, LANES), jnp.float32),
+            pltpu.VMEM((tiles + 4, made, LANES), jnp.float32),
+            pltpu.VMEM((made, 2 * count), jnp.bfloat16),
+            pltpu.VMEM((made, 4 * EDGE), jnp.bfloat16),
+            pltpu.VMEM((4, count, LANES), jnp.int32),
+            pltpu.VMEM((made, LANES), jnp.int32),
+            pltpu.VMEM((made, LANES), jnp.float32),
         ],
         name="line_filter",
     )(pos, meta, meta_sib, own, sib, near, far, table)
@@ -385,18 +390,22 @@
     near = lax.ppermute(edge, "az", across)
     far = lax.ppermute(edge, "az", along)
     meta_sib = lax.ppermute(meta, "az", sibling)
-    table = table_call(rg_coef, cols)
-
-    rows = [4] * (len(order) + 1) + [2, 2]
-    *made, power = filter_call(chips, pos, meta, meta_sib, secondary, sib, near, far, table, rows)
+    coef, sib = lax.optimization_barrier((rg_coef, sib))
+    table = table_call(coef, cols)
+
+    inputs = (pos, meta, meta_sib, secondary, sib, near, far, table)
+    ahead, behind = order[:AHEAD], [0] + order[AHEAD:] + [half]
+    *made_ahead, power_ahead = filter_call(chips, ahead, *inputs, [4] * AHEAD)
+    *made, power = filter_call(chips, behind, *inputs, [4] * (len(behind) - 1) + [2, 2])
+    made = made[:1] + made_ahead + made[1:]
 
     up = lax.ppermute(made[-2], "az", chip_pairs(chips, half // 2))
     down = lax.ppermute(made[-1], "az", chip_pairs(chips, -(half // 2)))
     arrived = []
     for at, shift in enumerate(order):
         arrived.append(lax.ppermute(made[at + 1], "az", chip_pairs(chips, shift)))
-    up, power, valid, first, last, dest = lax.optimization_barrier(
-        (up, power, line_valid, first_valid, last_valid, block_dest)
+    arrived[0], power, valid, first, last, dest = lax.optimization_barrier(
+        (arrived[0], power + power_ahead, line_valid, first_valid, last_valid, block_dest)
     )
     up = lax.ppermute(up, "az", chip_pairs(chips, half - half // 2))
     down = lax.ppermute(down, "az", chip_pairs(chips, -(half - half // 2)))
@@ -415,6 +424,7 @@
     mean_power = total_power / jnp.maximum(total_count, 1.0)
     power_gain = lax.rsqrt(mean_power + 0.5)
 
+    chip, core, _ = lax.optimization_barrier((chip, core, gathered))
     shifts = jnp.array([0] + order + [half], jnp.int32)
     source_chip = (chip - shifts) % chips
     source = (2 * source_chip[:, None] + jnp.stack([core, 1 - core])[None]).reshape(-1)

time: 381 us -> 424 us (1.11)
  the two profiles are of different devices: /device:TPU:46 before, /device:TPU:231 now
where the time goes in v2:
time: 424 us; the launch traced here: 423 us
  starting transfers between devices  249 us (59%)
  waiting for transfers between devices  121 us (29%)
  Pallas kernels  40.1 us (9%)
  between operations  7.52 us (2%)
    ppermute x30, starting transfers between devices, shards(): arrived.append(lax.ppermute(made[at + 1], 'az', chip_pairs(chips, shift)))  184 us
    ppermute x30, waiting for transfers between devices, shards(): arrived.append(lax.ppermute(made[at + 1], 'az', chip_pairs(chips, shift)))  74.4 us
    ppermute x1, waiting for transfers between devices, shards(): up = lax.ppermute(up, 'az', chip_pairs(chips, half - half // 2))  36.4 us
    pallas_call x2, Pallas kernels, filter_call(): pl.pallas_call(functools.partial(filter_body, chips, shifts, steps, len(r...  24.4 us
    all_to_all x1, starting transfers between devices, shards(): lax.all_to_all(sums, 'az', split_axis=0, concat_axis=0, tiled=True)  16.1 us
    ppermute x1, starting transfers between devices, shards(): up = lax.ppermute(made[-2], 'az', chip_pairs(chips, half // 2))  15.3 us
    ppermute x1, waiting for transfers between devices, shards(): down = lax.ppermute(down, 'az', chip_pairs(chips, -(half - half // 2)))  9.78 us
    ppermute x1, starting transfers between devices, shards(): up = lax.ppermute(up, 'az', chip_pairs(chips, half - half // 2))  9.31 us
  transfers between devices with their start and end apart: 39, of which 11 were waited for; matrix products, arithmetic and copies ran while one was open for 1% of the time, Pallas kernels for 6%

profile of v2, /device:TPU:231, one launch (start us, length us, event | category | flops | bytes accessed | tf_op | source)
XLA Modules:
  0.0 423.2 jit_solution(4926302116824006479)
XLA Ops:
  0.6 0.7 collective-permute-start.1
  1.9 2.7 prepare.1
  4.6 4.9 %collective-permute-start.2 = (bf16[2,8,12288]{2,1,0:T(8,128)(2,1)}, bf16[2,8,12288]{2,1,0:T(8,128)(2,1)S(1)}, u32[]{:S(2)}, u32[]{:S(2)}) collective-permute-start(bf16[2,8,12288]{2,1,0:T(8,128)(2,1)} %get-tuple-element.52), channel_id=1, source_target_pairs={{1,2},{3,4},{5,6},{7,8},{9,10},{11,12},{13,14},{15,16},{17,18},{19... | collective-permute-start | bytes 1179656 | tf_op jit(solution)/shard_map/ppermute | solution.py:390
  9.5 3.8 collective-permute-start.3
  13.5 8.0 %range_table.1.table_ref = bf16[96,256,128]{2,1,0:T(8,128)(2,1)} custom-call(f32[4]{0:T(128)} %coef_ref.2), custom_call_target="tpu_custom_call" | custom-call | tf_op jit(solution)/shard_map/range_table/pallas_call | solution.py:141
  22.2 10.9 %line_filter.2 = (bf16[4,12288]{1,0:T(4,128)(2,1)}, bf16[4,12288]{1,0:T(4,128)(2,1)}, bf16[4,12288]{1,0:T(4,128)(2,1)}, bf16[4,12288]{1,0:T(4,128)(2,1)}, bf16[4...) custom-call(s32[2]{0:T(128)} %pad_add_fusion.pos_ref, ...), custom_call_target="tpu_custom_call" | custom-call | tf_op jit(solution)/shard_map/line_filter/pallas_call | solution.py:315
  33.3 6.3 %collective-permute-start.4 = (bf16[4,12288]{1,0:T(4,128)(2,1)}, bf16[4,12288]{1,0:T(4,128)(2,1)S(1)}, u32[]{:S(2)}, u32[]{:S(2)}) collective-permute-start(bf16[4,12288]{1,0:T(4,128)(2,1)} %get-tuple-element.54), channel_id=1, source_target_pairs={{0,6},{1,7},{2,8},{3,9},{4,10},{5,11},{6,12},{7,13},{8,14},{9,15},... | collective-permute-start | bytes 294920 | tf_op jit(solution)/shard_map/ppermute | solution.py:406
  39.5 13.5 %line_filter.3 = (bf16[4,12288]{1,0:T(4,128)(2,1)}, bf16[4,12288]{1,0:T(4,128)(2,1)}, bf16[4,12288]{1,0:T(4,128)(2,1)}, bf16[4,12288]{1,0:T(4,128)(2,1)}, bf16[4...) custom-call(s32[2]{0:T(128)} %pad_add_fusion.pos_ref, ...), custom_call_target="tpu_custom_call" | custom-call | tf_op jit(solution)/shard_map/line_filter/pallas_call | solution.py:315
  53.0 15.3 %collective-permute-start.34 = (bf16[2,12288]{1,0:T(2,128)(2,1)}, bf16[2,12288]{1,0:T(2,128)(2,1)S(1)}, u32[]{:S(2)}, u32[]{:S(2)}) collective-permute-start(bf16[2,12288]{1,0:T(2,128)(2,1)} %get-tuple-element.95), channel_id=1, source_target_pairs={{0,16},{1,17},{2,18},{3,19},{4,20},{5,21},{6,22},{7,23},{8,24},{9,... | collective-permute-start | bytes 147464 | tf_op jit(solution)/shard_map/ppermute | solution.py:402
  71.2 0.7 copy.15
  72.0 16.1 %all-to-all-start = ((f32[64,1,3]{2,1,0:T(1,128)}), f32[64,1,3]{2,1,0:T(1,128)S(1)}, u32[]{:S(2)}, u32[]{:S(2)}) async-start(f32[64,1,3]{2,1,0:T(1,128)} %copy.15), calls=%async_computation | async-start | bytes 65536 | tf_op jit(solution)/shard_map/all_to_all | solution.py:421
  88.0 8.0 %collective-permute-start.36 = (bf16[2,12288]{1,0:T(2,128)(2,1)}, bf16[2,12288]{1,0:T(2,128)(2,1)S(1)}, u32[]{:S(2)}, u32[]{:S(2)}) collective-permute-start(bf16[2,12288]{1,0:T(2,128)(2,1)} %get-tuple-element.96), channel_id=1, source_target_pairs={{0,48},{1,49},{2,50},{3,51},{4,52},{5,53},{6,54},{7,55},{8,56},{9,... | collective-permute-start | bytes 147464 | tf_op jit(solution)/shard_map/ppermute | solution.py:403
  96.1 6.2 %collective-permute-start.12 = (bf16[4,12288]{1,0:T(4,128)(2,1)}, bf16[4,12288]{1,0:T(4,128)(2,1)S(1)}, u32[]{:S(2)}, u32[]{:S(2)}) collective-permute-start(bf16[4,12288]{1,0:T(4,128)(2,1)} %get-tuple-element.73), channel_id=1, source_target_pairs={{0,22},{1,23},{2,24},{3,25},{4,26},{5,27},{6,28},{7,29},{8,30},{9,... | collective-permute-start | bytes 294920 | tf_op jit(solution)/shard_map/ppermute | solution.py:406
  102.3 6.6 %collective-permute-start.13 = (bf16[4,12288]{1,0:T(4,128)(2,1)}, bf16[4,12288]{1,0:T(4,128)(2,1)S(1)}, u32[]{:S(2)}, u32[]{:S(2)}) collective-permute-start(bf16[4,12288]{1,0:T(4,128)(2,1)} %get-tuple-element.74), channel_id=1, source_target_pairs={{0,42},{1,43},{2,44},{3,45},{4,46},{5,47},{6,48},{7,49},{8,50},{9,... | collective-permute-start | bytes 294920 | tf_op jit(solution)/shard_map/ppermute | solution.py:406
  109.0 11.3 %collective-permute-start.14 = (bf16[4,12288]{1,0:T(4,128)(2,1)}, bf16[4,12288]{1,0:T(4,128)(2,1)S(1)}, u32[]{:S(2)}, u32[]{:S(2)}) collective-permute-start(bf16[4,12288]{1,0:T(4,128)(2,1)} %get-tuple-element.75), channel_id=1, source_target_pairs={{0,28},{1,29},{2,30},{3,31},{4,32},{5,33},{6,34},{7,35},{8,36},{9,... | collective-permute-start | bytes 294920 | tf_op jit(solution)/shard_map/ppermute | solution.py:406
  120.3 9.3 %collective-permute-start.35 = (bf16[2,12288]{1,0:T(2,128)(2,1)S(1)}, bf16[2,12288]{1,0:T(2,128)(2,1)S(1)}, u32[]{:S(2)}, u32[]{:S(2)}) collective-permute-start(bf16[2,12288]{1,0:T(2,128)(2,1)S(1)} %collective-permute-done.34), channel_id=1, source_target_pairs={{0,16},{1,17},{2,18},{3,19},{4,20},{5,21},{6,22},{7,23},{8,24},{9,... | collective-permute-start | bytes 147464 | tf_op jit(solution)/shard_map/ppermute | solution.py:410
  129.8 36.4 %collective-permute-done.35.rest_31_ = bf16[2,12288]{1,0:T(2,128)(2,1)S(1)} collective-permute-done((bf16[2,12288]{1,0:T(2,128)(2,1)S(1)}, bf16[2,12288]{1,0:T(2,128)(2,1)S(1)}, u32[]{:S(2)}, u32[]{:S(2)}) %collective-permute-start.35) | collective-permute-done | bytes 49184 | tf_op jit(solution)/shard_map/ppermute | solution.py:410
  166.2 7.6 %collective-permute-start.37 = (bf16[2,12288]{1,0:T(2,128)(2,1)S(1)}, bf16[2,12288]{1,0:T(2,128)(2,1)S(1)}, u32[]{:S(2)}, u32[]{:S(2)}) collective-permute-start(bf16[2,12288]{1,0:T(2,128)(2,1)S(1)} %collective-permute-done.36), channel_id=1, source_target_pairs={{0,48},{1,49},{2,50},{3,51},{4,52},{5,53},{6,54},{7,55},{8,56},{9,... | collective-permute-start | bytes 147464 | tf_op jit(solution)/shard_map/ppermute | solution.py:411
  174.1 9.8 %collective-permute-done.37.rest_32_ = bf16[2,12288]{1,0:T(2,128)(2,1)S(1)} collective-permute-done((bf16[2,12288]{1,0:T(2,128)(2,1)S(1)}, bf16[2,12288]{1,0:T(2,128)(2,1)S(1)}, u32[]{:S(2)}, u32[]{:S(2)}) %collective-permute-start.37) | collective-permute-done | bytes 49184 | tf_op jit(solution)/shard_map/ppermute | solution.py:411
  183.8 6.1 %collective-permute-start.16 = (bf16[4,12288]{1,0:T(4,128)(2,1)}, bf16[4,12288]{1,0:T(4,128)(2,1)S(1)}, u32[]{:S(2)}, u32[]{:S(2)}) collective-permute-start(bf16[4,12288]{1,0:T(4,128)(2,1)} %get-tuple-element.77), channel_id=1, source_target_pairs={{0,26},{1,27},{2,28},{3,29},{4,30},{5,31},{6,32},{7,33},{8,34},{9,... | collective-permute-start | bytes 294920 | tf_op jit(solution)/shard_map/ppermute | solution.py:406
  189.9 9.8 %collective-permute-start.17 = (bf16[4,12288]{1,0:T(4,128)(2,1)}, bf16[4,12288]{1,0:T(4,128)(2,1)S(1)}, u32[]{:S(2)}, u32[]{:S(2)}) collective-permute-start(bf16[4,12288]{1,0:T(4,128)(2,1)} %get-tuple-element.78), channel_id=1, source_target_pairs={{0,38},{1,39},{2,40},{3,41},{4,42},{5,43},{6,44},{7,45},{8,46},{9,... | collective-permute-start | bytes 294920 | tf_op jit(solution)/shard_map/ppermute | solution.py:406
  199.7 3.6 collective-permute-start.18
  203.3 11.4 %collective-permute-start.19 = (bf16[4,12288]{1,0:T(4,128)(2,1)}, bf16[4,12288]{1,0:T(4,128)(2,1)S(1)}, u32[]{:S(2)}, u32[]{:S(2)}) collective-permute-start(bf16[4,12288]{1,0:T(4,128)(2,1)} %get-tuple-element.80), channel_id=1, source_target_pairs={{0,40},{1,41},{2,42},{3,43},{4,44},{5,45},{6,46},{7,47},{8,48},{9,... | collective-permute-start | bytes 294920 | tf_op jit(solution)/shard_map/ppermute | solution.py:406
  214.7 5.3 %collective-permute-start.20 = (bf16[4,12288]{1,0:T(4,128)(2,1)}, bf16[4,12288]{1,0:T(4,128)(2,1)S(1)}, u32[]{:S(2)}, u32[]{:S(2)}) collective-permute-start(bf16[4,12288]{1,0:T(4,128)(2,1)} %get-tuple-element.81), channel_id=1, source_target_pairs={{0,20},{1,21},{2,22},{3,23},{4,24},{5,25},{6,26},{7,27},{8,28},{9,... | collective-permute-start | bytes 294920 | tf_op jit(solution)/shard_map/ppermute | solution.py:406
  220.2 6.8 %collective-permute-start.21 = (bf16[4,12288]{1,0:T(4,128)(2,1)}, bf16[4,12288]{1,0:T(4,128)(2,1)S(1)}, u32[]{:S(2)}, u32[]{:S(2)}) collective-permute-start(bf16[4,12288]{1,0:T(4,128)(2,1)} %get-tuple-element.82), channel_id=1, source_target_pairs={{0,44},{1,45},{2,46},{3,47},{4,48},{5,49},{6,50},{7,51},{8,52},{9,... | collective-permute-start | bytes 294920 | tf_op jit(solution)/shard_map/ppermute | solution.py:406
  227.0 24.8 %collective-permute-done.17.rest_14_ = bf16[4,12288]{1,0:T(4,128)(2,1)S(1)} collective-permute-done((bf16[4,12288]{1,0:T(4,128)(2,1)}, bf16[4,12288]{1,0:T(4,128)(2,1)S(1)}, u32[]{:S(2)}, u32[]{:S(2)}) %collective-permute-start.17) | collective-permute-done | bytes 98336 | tf_op jit(solution)/shard_map/ppermute | solution.py:406
  251.8 4.3 %collective-permute-done.18.rest_15_ = bf16[4,12288]{1,0:T(4,128)(2,1)S(1)} collective-permute-done((bf16[4,12288]{1,0:T(4,128)(2,1)}, bf16[4,12288]{1,0:T(4,128)(2,1)S(1)}, u32[]{:S(2)}, u32[]{:S(2)}) %collective-permute-start.18) | collective-permute-done | bytes 98336 | tf_op jit(solution)/shard_map/ppermute | solution.py:406
  256.1 6.8 %collective-permute-start.23 = (bf16[4,12288]{1,0:T(4,128)(2,1)}, bf16[4,12288]{1,0:T(4,128)(2,1)S(1)}, u32[]{:S(2)}, u32[]{:S(2)}) collective-permute-start(bf16[4,12288]{1,0:T(4,128)(2,1)} %get-tuple-element.84), channel_id=1, source_target_pairs={{0,46},{1,47},{2,48},{3,49},{4,50},{5,51},{6,52},{7,53},{8,54},{9,... | collective-permute-start | bytes 294920 | tf_op jit(solution)/shard_map/ppermute | solution.py:406
  262.9 0.6 collective-permute-start.24
  263.5 5.1 %collective-permute-done.20.rest_17_ = bf16[4,12288]{1,0:T(4,128)(2,1)S(1)} collective-permute-done((bf16[4,12288]{1,0:T(4,128)(2,1)}, bf16[4,12288]{1,0:T(4,128)(2,1)S(1)}, u32[]{:S(2)}, u32[]{:S(2)}) %collective-permute-start.20) | collective-permute-done | bytes 98336 | tf_op jit(solution)/shard_map/ppermute | solution.py:406
  268.6 3.4 collective-permute-start.25
  272.3 17.3 %collective-permute-start.26 = (bf16[4,12288]{1,0:T(4,128)(2,1)}, bf16[4,12288]{1,0:T(4,128)(2,1)S(1)}, u32[]{:S(2)}, u32[]{:S(2)}) collective-permute-start(bf16[4,12288]{1,0:T(4,128)(2,1)} %get-tuple-element.87), channel_id=1, source_target_pairs={{0,12},{1,13},{2,14},{3,15},{4,16},{5,17},{6,18},{7,19},{8,20},{9,... | collective-permute-start | bytes 294920 | tf_op jit(solution)/shard_map/ppermute | solution.py:406
  289.6 9.6 %collective-permute-start.28 = (bf16[4,12288]{1,0:T(4,128)(2,1)}, bf16[4,12288]{1,0:T(4,128)(2,1)S(1)}, u32[]{:S(2)}, u32[]{:S(2)}) collective-permute-start(bf16[4,12288]{1,0:T(4,128)(2,1)} %get-tuple-element.89), channel_id=1, source_target_pairs={{0,8},{1,9},{2,10},{3,11},{4,12},{5,13},{6,14},{7,15},{8,16},{9,17... | collective-permute-start | bytes 294920 | tf_op jit(solution)/shard_map/ppermute | solution.py:406
  299.2 3.9 collective-permute-start.29
  303.1 1.5 collective-permute-start.30
  305.2 2.7 collective-permute-done.26.rest_23_
  307.9 11.1 %collective-permute-start.31 = (bf16[4,12288]{1,0:T(4,128)(2,1)}, bf16[4,12288]{1,0:T(4,128)(2,1)S(1)}, u32[]{:S(2)}, u32[]{:S(2)}) collective-permute-start(bf16[4,12288]{1,0:T(4,128)(2,1)} %get-tuple-element.92), channel_id=1, source_target_pairs={{0,60},{1,61},{2,62},{3,63},{4,0},{5,1},{6,2},{7,3},{8,4},{9,5},{1... | collective-permute-start | bytes 294920 | tf_op jit(solution)/shard_map/ppermute | solution.py:406
  319.0 5.6 %collective-permute-done.27.rest_24_ = bf16[4,12288]{1,0:T(4,128)(2,1)S(1)} collective-permute-done((bf16[4,12288]{1,0:T(4,128)(2,1)}, bf16[4,12288]{1,0:T(4,128)(2,1)S(1)}, u32[]{:S(2)}, u32[]{:S(2)}) %collective-permute-start.27) | collective-permute-done | bytes 98336 | tf_op jit(solution)/shard_map/ppermute | solution.py:406
  324.7 1.5 collective-permute-start.33
  326.1 9.9 %collective-permute-start.10 = (bf16[4,12288]{1,0:T(4,128)(2,1)S(1)}, bf16[4,12288]{1,0:T(4,128)(2,1)S(1)}, u32[]{:S(2)}, u32[]{:S(2)}) collective-permute-start(bf16[4,12288]{1,0:T(4,128)(2,1)S(1)} %copy-done.44), channel_id=1, source_target_pairs={{0,30},{1,31},{2,32},{3,33},{4,34},{5,35},{6,36},{7,37},{8,38},{9,... | collective-permute-start | bytes 294920 | tf_op jit(solution)/shard_map/ppermute | solution.py:406
  336.1 8.0 %collective-permute-start.11 = (bf16[4,12288]{1,0:T(4,128)(2,1)S(1)}, bf16[4,12288]{1,0:T(4,128)(2,1)S(1)}, u32[]{:S(2)}, u32[]{:S(2)}) collective-permute-start(bf16[4,12288]{1,0:T(4,128)(2,1)S(1)} %copy-done.43), channel_id=1, source_target_pairs={{0,34},{1,35},{2,36},{3,37},{4,38},{5,39},{6,40},{7,41},{8,42},{9,... | collective-permute-start | bytes 294920 | tf_op jit(solution)/shard_map/ppermute | solution.py:406
  344.1 4.0 collective-permute-start.5
  348.1 6.5 %collective-permute-start.6 = (bf16[4,12288]{1,0:T(4,128)(2,1)S(1)}, bf16[4,12288]{1,0:T(4,128)(2,1)S(1)}, u32[]{:S(2)}, u32[]{:S(2)}) collective-permute-start(bf16[4,12288]{1,0:T(4,128)(2,1)S(1)} %copy-done.42), channel_id=1, source_target_pairs={{0,10},{1,11},{2,12},{3,13},{4,14},{5,15},{6,16},{7,17},{8,18},{9,... | collective-permute-start | bytes 294920 | tf_op jit(solution)/shard_map/ppermute | solution.py:406
  354.8 26.0 %collective-permute-start.8 = (bf16[4,12288]{1,0:T(4,128)(2,1)S(1)}, bf16[4,12288]{1,0:T(4,128)(2,1)S(1)}, u32[]{:S(2)}, u32[]{:S(2)}) collective-permute-start(bf16[4,12288]{1,0:T(4,128)(2,1)S(1)} %copy-done.40), channel_id=1, source_target_pairs={{0,16},{1,17},{2,18},{3,19},{4,20},{5,21},{6,22},{7,23},{8,24},{9,... | collective-permute-start | bytes 294920 | tf_op jit(solution)/shard_map/ppermute | solution.py:406
  380.7 8.0 %collective-permute-done.11.rest_8_ = bf16[4,12288]{1,0:T(4,128)(2,1)S(1)} collective-permute-done((bf16[4,12288]{1,0:T(4,128)(2,1)S(1)}, bf16[4,12288]{1,0:T(4,128)(2,1)S(1)}, u32[]{:S(2)}, u32[]{:S(2)}) %collective-permute-start.11) | collective-permute-done | bytes 98336 | tf_op jit(solution)/shard_map/ppermute | solution.py:406
  391.6 2.9 collective-permute-done.8.rest_5_
  394.6 20.7 %collective-permute-done.9.rest_6_ = bf16[4,12288]{1,0:T(4,128)(2,1)S(1)} collective-permute-done((bf16[4,12288]{1,0:T(4,128)(2,1)S(1)}, bf16[4,12288]{1,0:T(4,128)(2,1)S(1)}, u32[]{:S(2)}, u32[]{:S(2)}) %collective-permute-start.9) | collective-permute-done | bytes 98336 | tf_op jit(solution)/shard_map/ppermute | solution.py:406
  415.9 5.1 %place_lines.1 = bf16[2,64,12288]{2,1,0:T(8,128)(2,1)} custom-call(f32[1]{0:T(128)S(6)} %rsqrt.4.gain_ref, bf16[128,128]{1,0:T(8,128)(2,1)} %fusion.arrange_ref, bf16[4,12288]{1,0:T(4,128)(2,1)} %get-tuple-element.64.rest_0_, bf16[4,12288]{1,0:T(4,128)(2,1)} %copy-done.2, bf16[4,12288]{1,0:T(4,128)(2,1)} %copy-done.27, bf16[4,12288]{1,0:T(4,128)(2,1)} %copy-done.28, ...), custom_call_target="tpu_custom_call" | custom-call | tf_op jit(solution)/shard_map/place_lines/pallas_call | solution.py:356
  (146 shorter events, 5.5 us)
Async XLA Ops:
  0.6 12.9 %collective-permute-start.1 = (bf16[2,64,12288]{2,1,0:T(8,128)(2,1)}, bf16[2,64,12288]{2,1,0:T(8,128)(2,1)S(1)}, u32[]{:S(2)}, u32[]{:S(2)}) collective-permute-start(bf16[2,64,12288]{2,1,0:T(8,128)(2,1)} %own_ref.3), channel_id=1, source_target_pairs={{0,1},{1,0},{2,3},{3,2},{4,5},{5,4},{6,7},{7,6},{8,9},{9,8},{10,11... | collective-permute-start | bytes 9437192 | tf_op jit(solution)/shard_map/ppermute | solution.py:384
  4.6 16.9 %collective-permute-start.2 = (bf16[2,8,12288]{2,1,0:T(8,128)(2,1)}, bf16[2,8,12288]{2,1,0:T(8,128)(2,1)S(1)}, u32[]{:S(2)}, u32[]{:S(2)}) collective-permute-start(bf16[2,8,12288]{2,1,0:T(8,128)(2,1)} %get-tuple-element.52), channel_id=1, source_target_pairs={{1,2},{3,4},{5,6},{7,8},{9,10},{11,12},{13,14},{15,16},{17,18},{19... | collective-permute-start | bytes 1179656 | tf_op jit(solution)/shard_map/ppermute | solution.py:390
  9.5 12.0 %collective-permute-start.3 = (bf16[2,8,12288]{2,1,0:T(8,128)(2,1)}, bf16[2,8,12288]{2,1,0:T(8,128)(2,1)}, u32[]{:S(2)}, u32[]{:S(2)}) collective-permute-start(bf16[2,8,12288]{2,1,0:T(8,128)(2,1)} %get-tuple-element.52), channel_id=1, source_target_pairs={{1,3},{3,5},{5,7},{7,9},{9,11},{11,13},{13,15},{15,17},{17,19},{19... | collective-permute-start | bytes 1179656 | tf_op jit(solution)/shard_map/ppermute | solution.py:391
  13.3 8.2 %collective-permute-start = (f32[16,64]{1,0:T(8,128)}, f32[16,64]{1,0:T(8,128)S(1)}, u32[]{:S(2)}, u32[]{:S(2)}) collective-permute-start(f32[16,64]{1,0:T(8,128)} %get-tuple-element.50.meta_ref), channel_id=1, source_target_pairs={{0,1},{1,0},{2,3},{3,2},{4,5},{5,4},{6,7},{7,6},{8,9},{9,8},{10,11... | collective-permute-start | bytes 12296 | tf_op jit(solution)/shard_map/ppermute | solution.py:392
  33.2 292.9 %copy-start.44 = (bf16[4,12288]{1,0:T(4,128)(2,1)S(1)}, bf16[4,12288]{1,0:T(4,128)(2,1)}, u32[]{:S(2)}) copy-start(bf16[4,12288]{1,0:T(4,128)(2,1)} %get-tuple-element.71) | copy-start | bytes 294916
  33.2 302.8 %copy-start.43 = (bf16[4,12288]{1,0:T(4,128)(2,1)S(1)}, bf16[4,12288]{1,0:T(4,128)(2,1)}, u32[]{:S(2)}) copy-start(bf16[4,12288]{1,0:T(4,128)(2,1)} %get-tuple-element.72) | copy-start | bytes 294916
  33.2 314.9 %copy-start.42 = (bf16[4,12288]{1,0:T(4,128)(2,1)S(1)}, bf16[4,12288]{1,0:T(4,128)(2,1)}, u32[]{:S(2)}) copy-start(bf16[4,12288]{1,0:T(4,128)(2,1)} %get-tuple-element.67) | copy-start | bytes 294916
  33.2 321.4 %copy-start.41 = (bf16[4,12288]{1,0:T(4,128)(2,1)S(1)}, bf16[4,12288]{1,0:T(4,128)(2,1)}, u32[]{:S(2)}) copy-start(bf16[4,12288]{1,0:T(4,128)(2,1)} %get-tuple-element.68) | copy-start | bytes 294916
  33.2 321.5 %copy-start.40 = (bf16[4,12288]{1,0:T(4,128)(2,1)S(1)}, bf16[4,12288]{1,0:T(4,128)(2,1)}, u32[]{:S(2)}) copy-start(bf16[4,12288]{1,0:T(4,128)(2,1)} %get-tuple-element.69) | copy-start | bytes 294916
  33.3 355.5 %copy-start.39 = (bf16[4,12288]{1,0:T(4,128)(2,1)S(1)}, bf16[4,12288]{1,0:T(4,128)(2,1)}, u32[]{:S(2)}) copy-start(bf16[4,12288]{1,0:T(4,128)(2,1)} %get-tuple-element.70) | copy-start | bytes 294916
  33.3 36.4 %collective-permute-start.4 = (bf16[4,12288]{1,0:T(4,128)(2,1)}, bf16[4,12288]{1,0:T(4,128)(2,1)S(1)}, u32[]{:S(2)}, u32[]{:S(2)}) collective-permute-start(bf16[4,12288]{1,0:T(4,128)(2,1)} %get-tuple-element.54), channel_id=1, source_target_pairs={{0,6},{1,7},{2,8},{3,9},{4,10},{5,11},{6,12},{7,13},{8,14},{9,15},... | collective-permute-start | bytes 294920 | tf_op jit(solution)/shard_map/ppermute | solution.py:406
  53.0 67.2 %collective-permute-start.34 = (bf16[2,12288]{1,0:T(2,128)(2,1)}, bf16[2,12288]{1,0:T(2,128)(2,1)S(1)}, u32[]{:S(2)}, u32[]{:S(2)}) collective-permute-start(bf16[2,12288]{1,0:T(2,128)(2,1)} %get-tuple-element.95), channel_id=1, source_target_pairs={{0,16},{1,17},{2,18},{3,19},{4,20},{5,21},{6,22},{7,23},{8,24},{9,... | collective-permute-start | bytes 147464 | tf_op jit(solution)/shard_map/ppermute | solution.py:402
  69.7 345.6 %copy-start.2 = (bf16[4,12288]{1,0:T(4,128)(2,1)}, bf16[4,12288]{1,0:T(4,128)(2,1)S(1)}, u32[]{:S(2)}) copy-start(bf16[4,12288]{1,0:T(4,128)(2,1)S(1)} %collective-permute-done.4.rest_1_) | copy-start | bytes 294916
  72.0 57.6 %all-to-all-start = ((f32[64,1,3]{2,1,0:T(1,128)}), f32[64,1,3]{2,1,0:T(1,128)S(1)}, u32[]{:S(2)}, u32[]{:S(2)}) async-start(f32[64,1,3]{2,1,0:T(1,128)} %copy.15), calls=%async_computation | async-start | bytes 65536 | tf_op jit(solution)/shard_map/all_to_all | solution.py:421
  88.0 41.7 %collective-permute-start.36 = (bf16[2,12288]{1,0:T(2,128)(2,1)}, bf16[2,12288]{1,0:T(2,128)(2,1)S(1)}, u32[]{:S(2)}, u32[]{:S(2)}) collective-permute-start(bf16[2,12288]{1,0:T(2,128)(2,1)} %get-tuple-element.96), channel_id=1, source_target_pairs={{0,48},{1,49},{2,50},{3,51},{4,52},{5,53},{6,54},{7,55},{8,56},{9,... | collective-permute-start | bytes 147464 | tf_op jit(solution)/shard_map/ppermute | solution.py:403
  96.1 93.8 %collective-permute-start.12 = (bf16[4,12288]{1,0:T(4,128)(2,1)}, bf16[4,12288]{1,0:T(4,128)(2,1)S(1)}, u32[]{:S(2)}, u32[]{:S(2)}) collective-permute-start(bf16[4,12288]{1,0:T(4,128)(2,1)} %get-tuple-element.73), channel_id=1, source_target_pairs={{0,22},{1,23},{2,24},{3,25},{4,26},{5,27},{6,28},{7,29},{8,30},{9,... | collective-permute-start | bytes 294920 | tf_op jit(solution)/shard_map/ppermute | solution.py:406
  102.3 97.4 %collective-permute-start.13 = (bf16[4,12288]{1,0:T(4,128)(2,1)}, bf16[4,12288]{1,0:T(4,128)(2,1)S(1)}, u32[]{:S(2)}, u32[]{:S(2)}) collective-permute-start(bf16[4,12288]{1,0:T(4,128)(2,1)} %get-tuple-element.74), channel_id=1, source_target_pairs={{0,42},{1,43},{2,44},{3,45},{4,46},{5,47},{6,48},{7,49},{8,50},{9,... | collective-permute-start | bytes 294920 | tf_op jit(solution)/shard_map/ppermute | solution.py:406
  109.0 94.4 %collective-permute-start.14 = (bf16[4,12288]{1,0:T(4,128)(2,1)}, bf16[4,12288]{1,0:T(4,128)(2,1)S(1)}, u32[]{:S(2)}, u32[]{:S(2)}) collective-permute-start(bf16[4,12288]{1,0:T(4,128)(2,1)} %get-tuple-element.75), channel_id=1, source_target_pairs={{0,28},{1,29},{2,30},{3,31},{4,32},{5,33},{6,34},{7,35},{8,36},{9,... | collective-permute-start | bytes 294920 | tf_op jit(solution)/shard_map/ppermute | solution.py:406
  120.3 45.9 %collective-permute-start.35 = (bf16[2,12288]{1,0:T(2,128)(2,1)S(1)}, bf16[2,12288]{1,0:T(2,128)(2,1)S(1)}, u32[]{:S(2)}, u32[]{:S(2)}) collective-permute-start(bf16[2,12288]{1,0:T(2,128)(2,1)S(1)} %collective-permute-done.34), channel_id=1, source_target_pairs={{0,16},{1,17},{2,18},{3,19},{4,20},{5,21},{6,22},{7,23},{8,24},{9,... | collective-permute-start | bytes 147464 | tf_op jit(solution)/shard_map/ppermute | solution.py:410
  129.7 85.0 %collective-permute-start.15 = (bf16[4,12288]{1,0:T(4,128)(2,1)}, bf16[4,12288]{1,0:T(4,128)(2,1)S(1)}, u32[]{:S(2)}, u32[]{:S(2)}) collective-permute-start(bf16[4,12288]{1,0:T(4,128)(2,1)} %get-tuple-element.76), channel_id=1, source_target_pairs={{0,36},{1,37},{2,38},{3,39},{4,40},{5,41},{6,42},{7,43},{8,44},{9,... | collective-permute-start | bytes 294920 | tf_op jit(solution)/shard_map/ppermute | solution.py:406
  166.2 249.0 %copy-start.32 = (bf16[2,12288]{1,0:T(2,128)(2,1)}, bf16[2,12288]{1,0:T(2,128)(2,1)S(1)}, u32[]{:S(2)}) copy-start(bf16[2,12288]{1,0:T(2,128)(2,1)S(1)} %collective-permute-done.35.rest_31_) | copy-start | bytes 147460
  166.2 17.6 %collective-permute-start.37 = (bf16[2,12288]{1,0:T(2,128)(2,1)S(1)}, bf16[2,12288]{1,0:T(2,128)(2,1)S(1)}, u32[]{:S(2)}, u32[]{:S(2)}) collective-permute-start(bf16[2,12288]{1,0:T(2,128)(2,1)S(1)} %collective-permute-done.36), channel_id=1, source_target_pairs={{0,48},{1,49},{2,50},{3,51},{4,52},{5,53},{6,54},{7,55},{8,56},{9,... | collective-permute-start | bytes 147464 | tf_op jit(solution)/shard_map/ppermute | solution.py:411
  183.8 231.4 %copy-start.33 = (bf16[2,12288]{1,0:T(2,128)(2,1)}, bf16[2,12288]{1,0:T(2,128)(2,1)S(1)}, u32[]{:S(2)}) copy-start(bf16[2,12288]{1,0:T(2,128)(2,1)S(1)} %collective-permute-done.37.rest_32_) | copy-start | bytes 147460
  183.8 36.4 %collective-permute-start.16 = (bf16[4,12288]{1,0:T(4,128)(2,1)}, bf16[4,12288]{1,0:T(4,128)(2,1)S(1)}, u32[]{:S(2)}, u32[]{:S(2)}) collective-permute-start(bf16[4,12288]{1,0:T(4,128)(2,1)} %get-tuple-element.77), channel_id=1, source_target_pairs={{0,26},{1,27},{2,28},{3,29},{4,30},{5,31},{6,32},{7,33},{8,34},{9,... | collective-permute-start | bytes 294920 | tf_op jit(solution)/shard_map/ppermute | solution.py:406
  189.9 61.8 %collective-permute-start.17 = (bf16[4,12288]{1,0:T(4,128)(2,1)}, bf16[4,12288]{1,0:T(4,128)(2,1)S(1)}, u32[]{:S(2)}, u32[]{:S(2)}) collective-permute-start(bf16[4,12288]{1,0:T(4,128)(2,1)} %get-tuple-element.78), channel_id=1, source_target_pairs={{0,38},{1,39},{2,40},{3,41},{4,42},{5,43},{6,44},{7,45},{8,46},{9,... | collective-permute-start | bytes 294920 | tf_op jit(solution)/shard_map/ppermute | solution.py:406
  199.7 56.4 %collective-permute-start.18 = (bf16[4,12288]{1,0:T(4,128)(2,1)}, bf16[4,12288]{1,0:T(4,128)(2,1)S(1)}, u32[]{:S(2)}, u32[]{:S(2)}) collective-permute-start(bf16[4,12288]{1,0:T(4,128)(2,1)} %get-tuple-element.79), channel_id=1, source_target_pairs={{0,24},{1,25},{2,26},{3,27},{4,28},{5,29},{6,30},{7,31},{8,32},{9,... | collective-permute-start | bytes 294920 | tf_op jit(solution)/shard_map/ppermute | solution.py:406
  203.3 59.5 %collective-permute-start.19 = (bf16[4,12288]{1,0:T(4,128)(2,1)}, bf16[4,12288]{1,0:T(4,128)(2,1)S(1)}, u32[]{:S(2)}, u32[]{:S(2)}) collective-permute-start(bf16[4,12288]{1,0:T(4,128)(2,1)} %get-tuple-element.80), channel_id=1, source_target_pairs={{0,40},{1,41},{2,42},{3,43},{4,44},{5,45},{6,46},{7,47},{8,48},{9,... | collective-permute-start | bytes 294920 | tf_op jit(solution)/shard_map/ppermute | solution.py:406
  214.7 53.9 %collective-permute-start.20 = (bf16[4,12288]{1,0:T(4,128)(2,1)}, bf16[4,12288]{1,0:T(4,128)(2,1)S(1)}, u32[]{:S(2)}, u32[]{:S(2)}) collective-permute-start(bf16[4,12288]{1,0:T(4,128)(2,1)} %get-tuple-element.81), channel_id=1, source_target_pairs={{0,20},{1,21},{2,22},{3,23},{4,24},{5,25},{6,26},{7,27},{8,28},{9,... | collective-permute-start | bytes 294920 | tf_op jit(solution)/shard_map/ppermute | solution.py:406
  220.2 52.0 %collective-permute-start.21 = (bf16[4,12288]{1,0:T(4,128)(2,1)}, bf16[4,12288]{1,0:T(4,128)(2,1)S(1)}, u32[]{:S(2)}, u32[]{:S(2)}) collective-permute-start(bf16[4,12288]{1,0:T(4,128)(2,1)} %get-tuple-element.82), channel_id=1, source_target_pairs={{0,44},{1,45},{2,46},{3,47},{4,48},{5,49},{6,50},{7,51},{8,52},{9,... | collective-permute-start | bytes 294920 | tf_op jit(solution)/shard_map/ppermute | solution.py:406
  251.8 37.8 %collective-permute-start.22 = (bf16[4,12288]{1,0:T(4,128)(2,1)}, bf16[4,12288]{1,0:T(4,128)(2,1)S(1)}, u32[]{:S(2)}, u32[]{:S(2)}) collective-permute-start(bf16[4,12288]{1,0:T(4,128)(2,1)} %get-tuple-element.83), channel_id=1, source_target_pairs={{0,18},{1,19},{2,20},{3,21},{4,22},{5,23},{6,24},{7,25},{8,26},{9,... | collective-permute-start | bytes 294920 | tf_op jit(solution)/shard_map/ppermute | solution.py:406
  256.1 33.4 %collective-permute-start.23 = (bf16[4,12288]{1,0:T(4,128)(2,1)}, bf16[4,12288]{1,0:T(4,128)(2,1)S(1)}, u32[]{:S(2)}, u32[]{:S(2)}) collective-permute-start(bf16[4,12288]{1,0:T(4,128)(2,1)} %get-tuple-element.84), channel_id=1, source_target_pairs={{0,46},{1,47},{2,48},{3,49},{4,50},{5,51},{6,52},{7,53},{8,54},{9,... | collective-permute-start | bytes 294920 | tf_op jit(solution)/shard_map/ppermute | solution.py:406
  262.9 36.3 %collective-permute-start.24 = (bf16[4,12288]{1,0:T(4,128)(2,1)}, bf16[4,12288]{1,0:T(4,128)(2,1)S(1)}, u32[]{:S(2)}, u32[]{:S(2)}) collective-permute-start(bf16[4,12288]{1,0:T(4,128)(2,1)} %get-tuple-element.85), channel_id=1, source_target_pairs={{0,14},{1,15},{2,16},{3,17},{4,18},{5,19},{6,20},{7,21},{8,22},{9,... | collective-permute-start | bytes 294920 | tf_op jit(solution)/shard_map/ppermute | solution.py:406
  268.6 34.5 %collective-permute-start.25 = (bf16[4,12288]{1,0:T(4,128)(2,1)}, bf16[4,12288]{1,0:T(4,128)(2,1)S(1)}, u32[]{:S(2)}, u32[]{:S(2)}) collective-permute-start(bf16[4,12288]{1,0:T(4,128)(2,1)} %get-tuple-element.86), channel_id=1, source_target_pairs={{0,50},{1,51},{2,52},{3,53},{4,54},{5,55},{6,56},{7,57},{8,58},{9,... | collective-permute-start | bytes 294920 | tf_op jit(solution)/shard_map/ppermute | solution.py:406
  272.3 35.7 %collective-permute-start.26 = (bf16[4,12288]{1,0:T(4,128)(2,1)}, bf16[4,12288]{1,0:T(4,128)(2,1)S(1)}, u32[]{:S(2)}, u32[]{:S(2)}) collective-permute-start(bf16[4,12288]{1,0:T(4,128)(2,1)} %get-tuple-element.87), channel_id=1, source_target_pairs={{0,12},{1,13},{2,14},{3,15},{4,16},{5,17},{6,18},{7,19},{8,20},{9,... | collective-permute-start | bytes 294920 | tf_op jit(solution)/shard_map/ppermute | solution.py:406
  289.5 35.1 %collective-permute-start.27 = (bf16[4,12288]{1,0:T(4,128)(2,1)}, bf16[4,12288]{1,0:T(4,128)(2,1)S(1)}, u32[]{:S(2)}, u32[]{:S(2)}) collective-permute-start(bf16[4,12288]{1,0:T(4,128)(2,1)} %get-tuple-element.88), channel_id=1, source_target_pairs={{0,52},{1,53},{2,54},{3,55},{4,56},{5,57},{6,58},{7,59},{8,60},{9,... | collective-permute-start | bytes 294920 | tf_op jit(solution)/shard_map/ppermute | solution.py:406
  289.6 35.1 %collective-permute-start.28 = (bf16[4,12288]{1,0:T(4,128)(2,1)}, bf16[4,12288]{1,0:T(4,128)(2,1)S(1)}, u32[]{:S(2)}, u32[]{:S(2)}) collective-permute-start(bf16[4,12288]{1,0:T(4,128)(2,1)} %get-tuple-element.89), channel_id=1, source_target_pairs={{0,8},{1,9},{2,10},{3,11},{4,12},{5,13},{6,14},{7,15},{8,16},{9,17... | collective-permute-start | bytes 294920 | tf_op jit(solution)/shard_map/ppermute | solution.py:406
  299.2 27.0 %collective-permute-start.29 = (bf16[4,12288]{1,0:T(4,128)(2,1)}, bf16[4,12288]{1,0:T(4,128)(2,1)S(1)}, u32[]{:S(2)}, u32[]{:S(2)}) collective-permute-start(bf16[4,12288]{1,0:T(4,128)(2,1)} %get-tuple-element.90), channel_id=1, source_target_pairs={{0,56},{1,57},{2,58},{3,59},{4,60},{5,61},{6,62},{7,63},{8,0},{9,1... | collective-permute-start | bytes 294920 | tf_op jit(solution)/shard_map/ppermute | solution.py:406
  303.1 33.0 %collective-permute-start.30 = (bf16[4,12288]{1,0:T(4,128)(2,1)}, bf16[4,12288]{1,0:T(4,128)(2,1)S(1)}, u32[]{:S(2)}, u32[]{:S(2)}) collective-permute-start(bf16[4,12288]{1,0:T(4,128)(2,1)} %get-tuple-element.91), channel_id=1, source_target_pairs={{0,4},{1,5},{2,6},{3,7},{4,8},{5,9},{6,10},{7,11},{8,12},{9,13},{1... | collective-permute-start | bytes 294920 | tf_op jit(solution)/shard_map/ppermute | solution.py:406
  307.9 36.1 %collective-permute-start.31 = (bf16[4,12288]{1,0:T(4,128)(2,1)}, bf16[4,12288]{1,0:T(4,128)(2,1)S(1)}, u32[]{:S(2)}, u32[]{:S(2)}) collective-permute-start(bf16[4,12288]{1,0:T(4,128)(2,1)} %get-tuple-element.92), channel_id=1, source_target_pairs={{0,60},{1,61},{2,62},{3,63},{4,0},{5,1},{6,2},{7,3},{8,4},{9,5},{1... | collective-permute-start | bytes 294920 | tf_op jit(solution)/shard_map/ppermute | solution.py:406
  324.6 23.5 %collective-permute-start.32 = (bf16[4,12288]{1,0:T(4,128)(2,1)}, bf16[4,12288]{1,0:T(4,128)(2,1)S(1)}, u32[]{:S(2)}, u32[]{:S(2)}) collective-permute-start(bf16[4,12288]{1,0:T(4,128)(2,1)} %get-tuple-element.93), channel_id=1, source_target_pairs={{0,2},{1,3},{2,4},{3,5},{4,6},{5,7},{6,8},{7,9},{8,10},{9,11},{10,... | collective-permute-start | bytes 294920 | tf_op jit(solution)/shard_map/ppermute | solution.py:406
  324.7 29.9 %collective-permute-start.33 = (bf16[4,12288]{1,0:T(4,128)(2,1)}, bf16[4,12288]{1,0:T(4,128)(2,1)S(1)}, u32[]{:S(2)}, u32[]{:S(2)}) collective-permute-start(bf16[4,12288]{1,0:T(4,128)(2,1)} %get-tuple-element.94), channel_id=1, source_target_pairs={{0,62},{1,63},{2,0},{3,1},{4,2},{5,3},{6,4},{7,5},{8,6},{9,7},{10,... | collective-permute-start | bytes 294920 | tf_op jit(solution)/shard_map/ppermute | solution.py:406
  326.1 28.6 %collective-permute-start.10 = (bf16[4,12288]{1,0:T(4,128)(2,1)S(1)}, bf16[4,12288]{1,0:T(4,128)(2,1)S(1)}, u32[]{:S(2)}, u32[]{:S(2)}) collective-permute-start(bf16[4,12288]{1,0:T(4,128)(2,1)S(1)} %copy-done.44), channel_id=1, source_target_pairs={{0,30},{1,31},{2,32},{3,33},{4,34},{5,35},{6,36},{7,37},{8,38},{9,... | collective-permute-start | bytes 294920 | tf_op jit(solution)/shard_map/ppermute | solution.py:406
  336.1 52.7 %collective-permute-start.11 = (bf16[4,12288]{1,0:T(4,128)(2,1)S(1)}, bf16[4,12288]{1,0:T(4,128)(2,1)S(1)}, u32[]{:S(2)}, u32[]{:S(2)}) collective-permute-start(bf16[4,12288]{1,0:T(4,128)(2,1)S(1)} %copy-done.43), channel_id=1, source_target_pairs={{0,34},{1,35},{2,36},{3,37},{4,38},{5,39},{6,40},{7,41},{8,42},{9,... | collective-permute-start | bytes 294920 | tf_op jit(solution)/shard_map/ppermute | solution.py:406
  344.1 47.2 %collective-permute-start.5 = (bf16[4,12288]{1,0:T(4,128)(2,1)}, bf16[4,12288]{1,0:T(4,128)(2,1)S(1)}, u32[]{:S(2)}, u32[]{:S(2)}) collective-permute-start(bf16[4,12288]{1,0:T(4,128)(2,1)} %get-tuple-element.66), channel_id=1, source_target_pairs={{0,58},{1,59},{2,60},{3,61},{4,62},{5,63},{6,0},{7,1},{8,2},{9,3},... | collective-permute-start | bytes 294920 | tf_op jit(solution)/shard_map/ppermute | solution.py:406
  348.1 43.2 %collective-permute-start.6 = (bf16[4,12288]{1,0:T(4,128)(2,1)S(1)}, bf16[4,12288]{1,0:T(4,128)(2,1)S(1)}, u32[]{:S(2)}, u32[]{:S(2)}) collective-permute-start(bf16[4,12288]{1,0:T(4,128)(2,1)S(1)} %copy-done.42), channel_id=1, source_target_pairs={{0,10},{1,11},{2,12},{3,13},{4,14},{5,15},{6,16},{7,17},{8,18},{9,... | collective-permute-start | bytes 294920 | tf_op jit(solution)/shard_map/ppermute | solution.py:406
  354.6 37.0 %collective-permute-start.7 = (bf16[4,12288]{1,0:T(4,128)(2,1)S(1)}, bf16[4,12288]{1,0:T(4,128)(2,1)S(1)}, u32[]{:S(2)}, u32[]{:S(2)}) collective-permute-start(bf16[4,12288]{1,0:T(4,128)(2,1)S(1)} %copy-done.41), channel_id=1, source_target_pairs={{0,54},{1,55},{2,56},{3,57},{4,58},{5,59},{6,60},{7,61},{8,62},{9,... | collective-permute-start | bytes 294920 | tf_op jit(solution)/shard_map/ppermute | solution.py:406
  354.8 39.8 %collective-permute-start.8 = (bf16[4,12288]{1,0:T(4,128)(2,1)S(1)}, bf16[4,12288]{1,0:T(4,128)(2,1)S(1)}, u32[]{:S(2)}, u32[]{:S(2)}) collective-permute-start(bf16[4,12288]{1,0:T(4,128)(2,1)S(1)} %copy-done.40), channel_id=1, source_target_pairs={{0,16},{1,17},{2,18},{3,19},{4,20},{5,21},{6,22},{7,23},{8,24},{9,... | collective-permute-start | bytes 294920 | tf_op jit(solution)/shard_map/ppermute | solution.py:406
  388.7 26.5 %collective-permute-start.9 = (bf16[4,12288]{1,0:T(4,128)(2,1)S(1)}, bf16[4,12288]{1,0:T(4,128)(2,1)S(1)}, u32[]{:S(2)}, u32[]{:S(2)}) collective-permute-start(bf16[4,12288]{1,0:T(4,128)(2,1)S(1)} %copy-done.39), channel_id=1, source_target_pairs={{0,48},{1,49},{2,50},{3,51},{4,52},{5,53},{6,54},{7,55},{8,56},{9,... | collective-permute-start | bytes 294920 | tf_op jit(solution)/shard_map/ppermute | solution.py:406
  (37 other events, 3384.2 us)

commit v3 on v1

--- a/solution.py
+++ b/solution.py
@@ -16,7 +16,7 @@
 MAIN_TILES = 24
 UNROLL = 8
 TABLE_TILES = 8
-PLACE_TILES = 32
+PLACE_TILES = 48
 EDGE_CHUNKS = 8
 
 
@@ -30,7 +30,7 @@
 
 def shift_list(chips):
     half = chips // 2
-    rising = [k for k in (3, 5, 8, 13) if k < half]
+    rising = [k for k in (2, 3, 5, 8, 11, 15) if k < half]
     falling = [k for k in range(half - 1, 0, -1) if k not in rising]
     return [s * k for k in rising + falling for s in (1, -1)]
 
@@ -385,7 +385,8 @@
     near = lax.ppermute(edge, "az", across)
     far = lax.ppermute(edge, "az", along)
     meta_sib = lax.ppermute(meta, "az", sibling)
-    table = table_call(rg_coef, cols)
+    coef, sib = lax.optimization_barrier((rg_coef, sib))
+    table = table_call(coef, cols)
 
     rows = [4] * (len(order) + 1) + [2, 2]
     *made, power = filter_call(chips, pos, meta, meta_sib, secondary, sib, near, far, table, rows)
@@ -395,8 +396,8 @@
     arrived = []
     for at, shift in enumerate(order):
         arrived.append(lax.ppermute(made[at + 1], "az", chip_pairs(chips, shift)))
-    up, power, valid, first, last, dest = lax.optimization_barrier(
-        (up, power, line_valid, first_valid, last_valid, block_dest)
+    arrived[0], power, valid, first, last, dest = lax.optimization_barrier(
+        (arrived[0], power, line_valid, first_valid, last_valid, block_dest)
     )
     up = lax.ppermute(up, "az", chip_pairs(chips, half - half // 2))
     down = lax.ppermute(down, "az", chip_pairs(chips, -(half - half // 2)))
@@ -415,6 +416,7 @@
     mean_power = total_power / jnp.maximum(total_count, 1.0)
     power_gain = lax.rsqrt(mean_power + 0.5)
 
+    chip, core, _ = lax.optimization_barrier((chip, core, gathered))
     shifts = jnp.array([0] + order + [half], jnp.int32)
     source_chip = (chip - shifts) % chips
     source = (2 * source_chip[:, None] + jnp.stack([core, 1 - core])[None]).reshape(-1)

time: 381 us -> 424 us (1.11)
  starting transfers between devices: 232 us -> 303 us
  waiting for transfers between devices: 100 us -> 77.5 us
    ppermute x30, starting transfers between devices: 164 us -> 222 us  [shards(): arrived.append(lax.ppermute(made[at + 1], 'az', chip_pairs(chips, shift)))]
    ppermute x30, waiting for transfers between devices: 98.3 us -> 51.5 us  [shards(): arrived.append(lax.ppermute(made[at + 1], 'az', chip_pairs(chips, shift)))]
    ppermute x1, waiting for transfers between devices: 0.01 us -> 24.5 us  [shards(): up = lax.ppermute(up, 'az', chip_pairs(chips, half - half // 2))]
    ppermute x1, starting transfers between devices: 1.32 us -> 17.2 us  [shards(): down = lax.ppermute(down, 'az', chip_pairs(chips, -(half - half // 2)))]
    all_to_all x1, starting transfers between devices: 24.3 us -> 18.8 us  [shards(): lax.all_to_all(sums, 'az', split_axis=0, concat_axis=0, tiled=True)]
  transfers between devices with their start and end apart: 39 -> 39, of which waited for: 10 -> 10; matrix products, arithmetic and copies ran while one was open for 2% -> 1% of each run, Pallas kernels for 3% -> 3%
where the time goes in v3:
time: 424 us; the launch traced here: 423 us
  starting transfers between devices  303 us (71%)
  waiting for transfers between devices  77.5 us (18%)
  Pallas kernels  30 us (7%)
  between operations  6.11 us (1%)
    ppermute x30, starting transfers between devices, shards(): arrived.append(lax.ppermute(made[at + 1], 'az', chip_pairs(chips, shift)))  222 us
    ppermute x30, waiting for transfers between devices, shards(): arrived.append(lax.ppermute(made[at + 1], 'az', chip_pairs(chips, shift)))  51.5 us
    ppermute x1, waiting for transfers between devices, shards(): up = lax.ppermute(up, 'az', chip_pairs(chips, half - half // 2))  24.5 us
    all_to_all x1, starting transfers between devices, shards(): lax.all_to_all(sums, 'az', split_axis=0, concat_axis=0, tiled=True)  18.8 us
    ppermute x1, starting transfers between devices, shards(): down = lax.ppermute(down, 'az', chip_pairs(chips, -(half - half // 2)))  17.2 us
    ppermute x1, starting transfers between devices, shards(): up = lax.ppermute(made[-2], 'az', chip_pairs(chips, half // 2))  15.4 us
    pallas_call x1, Pallas kernels, filter_call(): pl.pallas_call(functools.partial(filter_body, chips, steps, len(row_count...  15.2 us
    ppermute x1, starting transfers between devices, shards(): up = lax.ppermute(up, 'az', chip_pairs(chips, half - half // 2))  10.3 us
  transfers between devices with their start and end apart: 39, of which 10 were waited for; matrix products, arithmetic and copies ran while one was open for 1% of the time, Pallas kernels for 3%

profile of v3, /device:TPU:46, one launch (start us, length us, event | category | flops | bytes accessed | tf_op | source)
XLA Modules:
  0.0 422.8 jit_solution(3913345429653909648)
XLA Ops:
  1.4 2.7 prepare.1
  4.1 0.7 collective-permute-start.2
  4.8 1.3 collective-permute-start.3
  6.1 6.7 %collective-permute-start = (f32[16,64]{1,0:T(8,128)}, f32[16,64]{1,0:T(8,128)S(1)}, u32[]{:S(2)}, u32[]{:S(2)}) collective-permute-start(f32[16,64]{1,0:T(8,128)} %get-tuple-element.49.meta_ref), channel_id=1, source_target_pairs={{0,1},{1,0},{2,3},{3,2},{4,5},{5,4},{6,7},{7,6},{8,9},{9,8},{10,11... | collective-permute-start | bytes 12296 | tf_op jit(solution)/shard_map/ppermute | solution.py:387
  12.8 7.9 %range_table.1.table_ref = bf16[96,256,128]{2,1,0:T(8,128)(2,1)} custom-call(f32[4]{0:T(128)} %coef_ref.2), custom_call_target="tpu_custom_call" | custom-call | tf_op jit(solution)/shard_map/range_table/pallas_call | solution.py:140
  21.5 15.2 %line_filter.1 = (bf16[4,12288]{1,0:T(4,128)(2,1)}, bf16[4,12288]{1,0:T(4,128)(2,1)}, bf16[4,12288]{1,0:T(4,128)(2,1)}, bf16[4,12288]{1,0:T(4,128)(2,1)}, bf16[4...) custom-call(s32[2]{0:T(128)} %pad_add_fusion.pos_ref, ...), custom_call_target="tpu_custom_call" | custom-call | tf_op jit(solution)/shard_map/line_filter/pallas_call | solution.py:311
  36.7 4.4 %collective-permute-start.4 = (bf16[4,12288]{1,0:T(4,128)(2,1)}, bf16[4,12288]{1,0:T(4,128)(2,1)S(1)}, u32[]{:S(2)}, u32[]{:S(2)}) collective-permute-start(bf16[4,12288]{1,0:T(4,128)(2,1)} %get-tuple-element.53), channel_id=1, source_target_pairs={{0,4},{1,5},{2,6},{3,7},{4,8},{5,9},{6,10},{7,11},{8,12},{9,13},{1... | collective-permute-start | bytes 294920 | tf_op jit(solution)/shard_map/ppermute | solution.py:398
  41.1 15.4 %collective-permute-start.34 = (bf16[2,12288]{1,0:T(2,128)(2,1)}, bf16[2,12288]{1,0:T(2,128)(2,1)S(1)}, u32[]{:S(2)}, u32[]{:S(2)}) collective-permute-start(bf16[2,12288]{1,0:T(2,128)(2,1)} %get-tuple-element.93), channel_id=1, source_target_pairs={{0,16},{1,17},{2,18},{3,19},{4,20},{5,21},{6,22},{7,23},{8,24},{9,... | collective-permute-start | bytes 147464 | tf_op jit(solution)/shard_map/ppermute | solution.py:394
  56.5 4.6 %collective-permute-done.4.rest_1_ = bf16[4,12288]{1,0:T(4,128)(2,1)S(1)} collective-permute-done((bf16[4,12288]{1,0:T(4,128)(2,1)}, bf16[4,12288]{1,0:T(4,128)(2,1)S(1)}, u32[]{:S(2)}, u32[]{:S(2)}) %collective-permute-start.4) | collective-permute-done | bytes 98336 | tf_op jit(solution)/shard_map/ppermute | solution.py:398
  61.2 0.6 and_select_fusion.2
  62.6 0.8 pad_maximum_fusion
  63.4 0.7 copy.15
  64.1 18.8 %all-to-all-start = ((f32[64,1,3]{2,1,0:T(1,128)}), f32[64,1,3]{2,1,0:T(1,128)S(1)}, u32[]{:S(2)}, u32[]{:S(2)}) async-start(f32[64,1,3]{2,1,0:T(1,128)} %copy.15), calls=%async_computation | async-start | bytes 65536 | tf_op jit(solution)/shard_map/all_to_all | solution.py:413
  82.9 10.1 %collective-permute-start.36 = (bf16[2,12288]{1,0:T(2,128)(2,1)}, bf16[2,12288]{1,0:T(2,128)(2,1)S(1)}, u32[]{:S(2)}, u32[]{:S(2)}) collective-permute-start(bf16[2,12288]{1,0:T(2,128)(2,1)} %get-tuple-element.94), channel_id=1, source_target_pairs={{0,48},{1,49},{2,50},{3,51},{4,52},{5,53},{6,54},{7,55},{8,56},{9,... | collective-permute-start | bytes 147464 | tf_op jit(solution)/shard_map/ppermute | solution.py:395
  93.1 0.7 collective-permute-start.10
  93.8 10.0 %collective-permute-start.11 = (bf16[4,12288]{1,0:T(4,128)(2,1)}, bf16[4,12288]{1,0:T(4,128)(2,1)S(1)}, u32[]{:S(2)}, u32[]{:S(2)}) collective-permute-start(bf16[4,12288]{1,0:T(4,128)(2,1)} %get-tuple-element.70), channel_id=1, source_target_pairs={{0,48},{1,49},{2,50},{3,51},{4,52},{5,53},{6,54},{7,55},{8,56},{9,... | collective-permute-start | bytes 294920 | tf_op jit(solution)/shard_map/ppermute | solution.py:398
  103.8 2.7 collective-permute-start.12
  106.5 10.3 %collective-permute-start.35 = (bf16[2,12288]{1,0:T(2,128)(2,1)S(1)}, bf16[2,12288]{1,0:T(2,128)(2,1)S(1)}, u32[]{:S(2)}, u32[]{:S(2)}) collective-permute-start(bf16[2,12288]{1,0:T(2,128)(2,1)S(1)} %collective-permute-done.34), channel_id=1, source_target_pairs={{0,16},{1,17},{2,18},{3,19},{4,20},{5,21},{6,22},{7,23},{8,24},{9,... | collective-permute-start | bytes 147464 | tf_op jit(solution)/shard_map/ppermute | solution.py:402
  116.9 2.7 collective-permute-start.13
  119.6 24.5 %collective-permute-done.35.rest_31_ = bf16[2,12288]{1,0:T(2,128)(2,1)S(1)} collective-permute-done((bf16[2,12288]{1,0:T(2,128)(2,1)S(1)}, bf16[2,12288]{1,0:T(2,128)(2,1)S(1)}, u32[]{:S(2)}, u32[]{:S(2)}) %collective-permute-start.35) | collective-permute-done | bytes 49184 | tf_op jit(solution)/shard_map/ppermute | solution.py:402
  144.1 17.2 %collective-permute-start.37 = (bf16[2,12288]{1,0:T(2,128)(2,1)S(1)}, bf16[2,12288]{1,0:T(2,128)(2,1)S(1)}, u32[]{:S(2)}, u32[]{:S(2)}) collective-permute-start(bf16[2,12288]{1,0:T(2,128)(2,1)S(1)} %collective-permute-done.36), channel_id=1, source_target_pairs={{0,48},{1,49},{2,50},{3,51},{4,52},{5,53},{6,54},{7,55},{8,56},{9,... | collective-permute-start | bytes 147464 | tf_op jit(solution)/shard_map/ppermute | solution.py:403
  161.6 1.5 collective-permute-done.37.rest_32_
  163.0 9.6 %collective-permute-start.14 = (bf16[4,12288]{1,0:T(4,128)(2,1)}, bf16[4,12288]{1,0:T(4,128)(2,1)S(1)}, u32[]{:S(2)}, u32[]{:S(2)}) collective-permute-start(bf16[4,12288]{1,0:T(4,128)(2,1)} %get-tuple-element.73), channel_id=1, source_target_pairs={{0,30},{1,31},{2,32},{3,33},{4,34},{5,35},{6,36},{7,37},{8,38},{9,... | collective-permute-start | bytes 294920 | tf_op jit(solution)/shard_map/ppermute | solution.py:398
  172.6 9.9 %collective-permute-start.15 = (bf16[4,12288]{1,0:T(4,128)(2,1)}, bf16[4,12288]{1,0:T(4,128)(2,1)S(1)}, u32[]{:S(2)}, u32[]{:S(2)}) collective-permute-start(bf16[4,12288]{1,0:T(4,128)(2,1)} %get-tuple-element.74), channel_id=1, source_target_pairs={{0,34},{1,35},{2,36},{3,37},{4,38},{5,39},{6,40},{7,41},{8,42},{9,... | collective-permute-start | bytes 294920 | tf_op jit(solution)/shard_map/ppermute | solution.py:398
  182.5 12.1 %collective-permute-start.16 = (bf16[4,12288]{1,0:T(4,128)(2,1)}, bf16[4,12288]{1,0:T(4,128)(2,1)S(1)}, u32[]{:S(2)}, u32[]{:S(2)}) collective-permute-start(bf16[4,12288]{1,0:T(4,128)(2,1)} %get-tuple-element.75), channel_id=1, source_target_pairs={{0,28},{1,29},{2,30},{3,31},{4,32},{5,33},{6,34},{7,35},{8,36},{9,... | collective-permute-start | bytes 294920 | tf_op jit(solution)/shard_map/ppermute | solution.py:398
  194.6 6.5 %collective-permute-start.17 = (bf16[4,12288]{1,0:T(4,128)(2,1)}, bf16[4,12288]{1,0:T(4,128)(2,1)S(1)}, u32[]{:S(2)}, u32[]{:S(2)}) collective-permute-start(bf16[4,12288]{1,0:T(4,128)(2,1)} %get-tuple-element.76), channel_id=1, source_target_pairs={{0,36},{1,37},{2,38},{3,39},{4,40},{5,41},{6,42},{7,43},{8,44},{9,... | collective-permute-start | bytes 294920 | tf_op jit(solution)/shard_map/ppermute | solution.py:398
  201.1 12.5 %collective-permute-start.18 = (bf16[4,12288]{1,0:T(4,128)(2,1)}, bf16[4,12288]{1,0:T(4,128)(2,1)S(1)}, u32[]{:S(2)}, u32[]{:S(2)}) collective-permute-start(bf16[4,12288]{1,0:T(4,128)(2,1)} %get-tuple-element.77), channel_id=1, source_target_pairs={{0,26},{1,27},{2,28},{3,29},{4,30},{5,31},{6,32},{7,33},{8,34},{9,... | collective-permute-start | bytes 294920 | tf_op jit(solution)/shard_map/ppermute | solution.py:398
  213.8 26.1 %collective-permute-start.19 = (bf16[4,12288]{1,0:T(4,128)(2,1)}, bf16[4,12288]{1,0:T(4,128)(2,1)S(1)}, u32[]{:S(2)}, u32[]{:S(2)}) collective-permute-start(bf16[4,12288]{1,0:T(4,128)(2,1)} %get-tuple-element.78), channel_id=1, source_target_pairs={{0,38},{1,39},{2,40},{3,41},{4,42},{5,43},{6,44},{7,45},{8,46},{9,... | collective-permute-start | bytes 294920 | tf_op jit(solution)/shard_map/ppermute | solution.py:398
  240.0 5.8 %collective-permute-done.16.rest_13_ = bf16[4,12288]{1,0:T(4,128)(2,1)S(1)} collective-permute-done((bf16[4,12288]{1,0:T(4,128)(2,1)}, bf16[4,12288]{1,0:T(4,128)(2,1)S(1)}, u32[]{:S(2)}, u32[]{:S(2)}) %collective-permute-start.16) | collective-permute-done | bytes 98336 | tf_op jit(solution)/shard_map/ppermute | solution.py:398
  245.8 9.7 %collective-permute-start.21 = (bf16[4,12288]{1,0:T(4,128)(2,1)}, bf16[4,12288]{1,0:T(4,128)(2,1)S(1)}, u32[]{:S(2)}, u32[]{:S(2)}) collective-permute-start(bf16[4,12288]{1,0:T(4,128)(2,1)} %get-tuple-element.80), channel_id=1, source_target_pairs={{0,40},{1,41},{2,42},{3,43},{4,44},{5,45},{6,46},{7,47},{8,48},{9,... | collective-permute-start | bytes 294920 | tf_op jit(solution)/shard_map/ppermute | solution.py:398
  255.5 1.7 collective-permute-done.17.rest_14_
  257.2 6.9 %collective-permute-start.22 = (bf16[4,12288]{1,0:T(4,128)(2,1)}, bf16[4,12288]{1,0:T(4,128)(2,1)S(1)}, u32[]{:S(2)}, u32[]{:S(2)}) collective-permute-start(bf16[4,12288]{1,0:T(4,128)(2,1)} %get-tuple-element.81), channel_id=1, source_target_pairs={{0,20},{1,21},{2,22},{3,23},{4,24},{5,25},{6,26},{7,27},{8,28},{9,... | collective-permute-start | bytes 294920 | tf_op jit(solution)/shard_map/ppermute | solution.py:398
  264.1 30.9 %collective-permute-start.23 = (bf16[4,12288]{1,0:T(4,128)(2,1)}, bf16[4,12288]{1,0:T(4,128)(2,1)S(1)}, u32[]{:S(2)}, u32[]{:S(2)}) collective-permute-start(bf16[4,12288]{1,0:T(4,128)(2,1)} %get-tuple-element.82), channel_id=1, source_target_pairs={{0,44},{1,45},{2,46},{3,47},{4,48},{5,49},{6,50},{7,51},{8,52},{9,... | collective-permute-start | bytes 294920 | tf_op jit(solution)/shard_map/ppermute | solution.py:398
  295.3 10.9 %collective-permute-start.24 = (bf16[4,12288]{1,0:T(4,128)(2,1)}, bf16[4,12288]{1,0:T(4,128)(2,1)S(1)}, u32[]{:S(2)}, u32[]{:S(2)}) collective-permute-start(bf16[4,12288]{1,0:T(4,128)(2,1)} %get-tuple-element.83), channel_id=1, source_target_pairs={{0,18},{1,19},{2,20},{3,21},{4,22},{5,23},{6,24},{7,25},{8,26},{9,... | collective-permute-start | bytes 294920 | tf_op jit(solution)/shard_map/ppermute | solution.py:398
  306.2 2.1 collective-permute-start.25
  308.2 22.8 %collective-permute-done.21.rest_18_ = bf16[4,12288]{1,0:T(4,128)(2,1)S(1)} collective-permute-done((bf16[4,12288]{1,0:T(4,128)(2,1)}, bf16[4,12288]{1,0:T(4,128)(2,1)S(1)}, u32[]{:S(2)}, u32[]{:S(2)}) %collective-permute-start.21) | collective-permute-done | bytes 98336 | tf_op jit(solution)/shard_map/ppermute | solution.py:398
  331.0 9.8 %collective-permute-start.27 = (bf16[4,12288]{1,0:T(4,128)(2,1)}, bf16[4,12288]{1,0:T(4,128)(2,1)S(1)}, u32[]{:S(2)}, u32[]{:S(2)}) collective-permute-start(bf16[4,12288]{1,0:T(4,128)(2,1)} %get-tuple-element.86), channel_id=1, source_target_pairs={{0,50},{1,51},{2,52},{3,53},{4,54},{5,55},{6,56},{7,57},{8,58},{9,... | collective-permute-start | bytes 294920 | tf_op jit(solution)/shard_map/ppermute | solution.py:398
  340.8 0.6 fusion.arrange_ref
  341.5 8.9 %collective-permute-start.29 = (bf16[4,12288]{1,0:T(4,128)(2,1)}, bf16[4,12288]{1,0:T(4,128)(2,1)S(1)}, u32[]{:S(2)}, u32[]{:S(2)}) collective-permute-start(bf16[4,12288]{1,0:T(4,128)(2,1)} %get-tuple-element.88), channel_id=1, source_target_pairs={{0,52},{1,53},{2,54},{3,55},{4,56},{5,57},{6,58},{7,59},{8,60},{9,... | collective-permute-start | bytes 294920 | tf_op jit(solution)/shard_map/ppermute | solution.py:398
  350.4 3.4 collective-permute-start.30
  353.8 4.5 %collective-permute-done.26.rest_23_ = bf16[4,12288]{1,0:T(4,128)(2,1)S(1)} collective-permute-done((bf16[4,12288]{1,0:T(4,128)(2,1)}, bf16[4,12288]{1,0:T(4,128)(2,1)S(1)}, u32[]{:S(2)}, u32[]{:S(2)}) %collective-permute-start.26) | collective-permute-done | bytes 98336 | tf_op jit(solution)/shard_map/ppermute | solution.py:398
  358.9 3.5 collective-permute-done.28.rest_25_
  362.4 20.4 %collective-permute-start.33 = (bf16[4,12288]{1,0:T(4,128)(2,1)}, bf16[4,12288]{1,0:T(4,128)(2,1)S(1)}, u32[]{:S(2)}, u32[]{:S(2)}) collective-permute-start(bf16[4,12288]{1,0:T(4,128)(2,1)} %get-tuple-element.92), channel_id=1, source_target_pairs={{0,62},{1,63},{2,0},{3,1},{4,2},{5,3},{6,4},{7,5},{8,6},{9,7},{10,... | collective-permute-start | bytes 294920 | tf_op jit(solution)/shard_map/ppermute | solution.py:398
  382.8 9.1 %collective-permute-start.5 = (bf16[4,12288]{1,0:T(4,128)(2,1)}, bf16[4,12288]{1,0:T(4,128)(2,1)S(1)}, u32[]{:S(2)}, u32[]{:S(2)}) collective-permute-start(bf16[4,12288]{1,0:T(4,128)(2,1)} %get-tuple-element.64), channel_id=1, source_target_pairs={{0,60},{1,61},{2,62},{3,63},{4,0},{5,1},{6,2},{7,3},{8,4},{9,5},{1... | collective-permute-start | bytes 294920 | tf_op jit(solution)/shard_map/ppermute | solution.py:398
  391.9 5.0 %collective-permute-start.7 = (bf16[4,12288]{1,0:T(4,128)(2,1)}, bf16[4,12288]{1,0:T(4,128)(2,1)S(1)}, u32[]{:S(2)}, u32[]{:S(2)}) collective-permute-start(bf16[4,12288]{1,0:T(4,128)(2,1)} %get-tuple-element.66), channel_id=1, source_target_pairs={{0,58},{1,59},{2,60},{3,61},{4,62},{5,63},{6,0},{7,1},{8,2},{9,3},... | collective-permute-start | bytes 294920 | tf_op jit(solution)/shard_map/ppermute | solution.py:398
  397.0 8.0 %collective-permute-start.9 = (bf16[4,12288]{1,0:T(4,128)(2,1)}, bf16[4,12288]{1,0:T(4,128)(2,1)S(1)}, u32[]{:S(2)}, u32[]{:S(2)}) collective-permute-start(bf16[4,12288]{1,0:T(4,128)(2,1)} %get-tuple-element.68), channel_id=1, source_target_pairs={{0,54},{1,55},{2,56},{3,57},{4,58},{5,59},{6,60},{7,61},{8,62},{9,... | collective-permute-start | bytes 294920 | tf_op jit(solution)/shard_map/ppermute | solution.py:398
  407.6 8.0 %collective-permute-done.8.rest_5_ = bf16[4,12288]{1,0:T(4,128)(2,1)S(1)} collective-permute-done((bf16[4,12288]{1,0:T(4,128)(2,1)}, bf16[4,12288]{1,0:T(4,128)(2,1)S(1)}, u32[]{:S(2)}, u32[]{:S(2)}) %collective-permute-start.8) | collective-permute-done | bytes 98336 | tf_op jit(solution)/shard_map/ppermute | solution.py:398
  416.3 4.2 place_lines.1
  (133 shorter events, 4.3 us)
Async XLA Ops:
  0.6 12.2 %collective-permute-start.1 = (bf16[2,64,12288]{2,1,0:T(8,128)(2,1)}, bf16[2,64,12288]{2,1,0:T(8,128)(2,1)S(1)}, u32[]{:S(2)}, u32[]{:S(2)}) collective-permute-start(bf16[2,64,12288]{2,1,0:T(8,128)(2,1)} %own_ref.1), channel_id=1, source_target_pairs={{0,1},{1,0},{2,3},{3,2},{4,5},{5,4},{6,7},{7,6},{8,9},{9,8},{10,11... | collective-permute-start | bytes 9437192 | tf_op jit(solution)/shard_map/ppermute | solution.py:379
  4.1 16.7 %collective-permute-start.2 = (bf16[2,8,12288]{2,1,0:T(8,128)(2,1)}, bf16[2,8,12288]{2,1,0:T(8,128)(2,1)S(1)}, u32[]{:S(2)}, u32[]{:S(2)}) collective-permute-start(bf16[2,8,12288]{2,1,0:T(8,128)(2,1)} %get-tuple-element.51), channel_id=1, source_target_pairs={{1,2},{3,4},{5,6},{7,8},{9,10},{11,12},{13,14},{15,16},{17,18},{19... | collective-permute-start | bytes 1179656 | tf_op jit(solution)/shard_map/ppermute | solution.py:385
  4.8 16.0 %collective-permute-start.3 = (bf16[2,8,12288]{2,1,0:T(8,128)(2,1)}, bf16[2,8,12288]{2,1,0:T(8,128)(2,1)}, u32[]{:S(2)}, u32[]{:S(2)}) collective-permute-start(bf16[2,8,12288]{2,1,0:T(8,128)(2,1)} %get-tuple-element.51), channel_id=1, source_target_pairs={{1,3},{3,5},{5,7},{7,9},{9,11},{11,13},{13,15},{15,17},{17,19},{19... | collective-permute-start | bytes 1179656 | tf_op jit(solution)/shard_map/ppermute | solution.py:386
  6.1 14.6 %collective-permute-start = (f32[16,64]{1,0:T(8,128)}, f32[16,64]{1,0:T(8,128)S(1)}, u32[]{:S(2)}, u32[]{:S(2)}) collective-permute-start(f32[16,64]{1,0:T(8,128)} %get-tuple-element.49.meta_ref), channel_id=1, source_target_pairs={{0,1},{1,0},{2,3},{3,2},{4,5},{5,4},{6,7},{7,6},{8,9},{9,8},{10,11... | collective-permute-start | bytes 12296 | tf_op jit(solution)/shard_map/ppermute | solution.py:387
  36.7 24.4 %collective-permute-start.4 = (bf16[4,12288]{1,0:T(4,128)(2,1)}, bf16[4,12288]{1,0:T(4,128)(2,1)S(1)}, u32[]{:S(2)}, u32[]{:S(2)}) collective-permute-start(bf16[4,12288]{1,0:T(4,128)(2,1)} %get-tuple-element.53), channel_id=1, source_target_pairs={{0,4},{1,5},{2,6},{3,7},{4,8},{5,9},{6,10},{7,11},{8,12},{9,13},{1... | collective-permute-start | bytes 294920 | tf_op jit(solution)/shard_map/ppermute | solution.py:398
  41.1 65.4 %collective-permute-start.34 = (bf16[2,12288]{1,0:T(2,128)(2,1)}, bf16[2,12288]{1,0:T(2,128)(2,1)S(1)}, u32[]{:S(2)}, u32[]{:S(2)}) collective-permute-start(bf16[2,12288]{1,0:T(2,128)(2,1)} %get-tuple-element.93), channel_id=1, source_target_pairs={{0,16},{1,17},{2,18},{3,19},{4,20},{5,21},{6,22},{7,23},{8,24},{9,... | collective-permute-start | bytes 147464 | tf_op jit(solution)/shard_map/ppermute | solution.py:394
  61.1 354.5 %copy-start.2 = (bf16[4,12288]{1,0:T(4,128)(2,1)}, bf16[4,12288]{1,0:T(4,128)(2,1)S(1)}, u32[]{:S(2)}) copy-start(bf16[4,12288]{1,0:T(4,128)(2,1)S(1)} %collective-permute-done.4.rest_1_) | copy-start | bytes 294916
  64.1 52.6 %all-to-all-start = ((f32[64,1,3]{2,1,0:T(1,128)}), f32[64,1,3]{2,1,0:T(1,128)S(1)}, u32[]{:S(2)}, u32[]{:S(2)}) async-start(f32[64,1,3]{2,1,0:T(1,128)} %copy.15), calls=%async_computation | async-start | bytes 65536 | tf_op jit(solution)/shard_map/all_to_all | solution.py:413
  82.9 34.0 %collective-permute-start.36 = (bf16[2,12288]{1,0:T(2,128)(2,1)}, bf16[2,12288]{1,0:T(2,128)(2,1)S(1)}, u32[]{:S(2)}, u32[]{:S(2)}) collective-permute-start(bf16[2,12288]{1,0:T(2,128)(2,1)} %get-tuple-element.94), channel_id=1, source_target_pairs={{0,48},{1,49},{2,50},{3,51},{4,52},{5,53},{6,54},{7,55},{8,56},{9,... | collective-permute-start | bytes 147464 | tf_op jit(solution)/shard_map/ppermute | solution.py:395
  93.1 79.5 %collective-permute-start.10 = (bf16[4,12288]{1,0:T(4,128)(2,1)}, bf16[4,12288]{1,0:T(4,128)(2,1)S(1)}, u32[]{:S(2)}, u32[]{:S(2)}) collective-permute-start(bf16[4,12288]{1,0:T(4,128)(2,1)} %get-tuple-element.69), channel_id=1, source_target_pairs={{0,16},{1,17},{2,18},{3,19},{4,20},{5,21},{6,22},{7,23},{8,24},{9,... | collective-permute-start | bytes 294920 | tf_op jit(solution)/shard_map/ppermute | solution.py:398
  93.8 88.7 %collective-permute-start.11 = (bf16[4,12288]{1,0:T(4,128)(2,1)}, bf16[4,12288]{1,0:T(4,128)(2,1)S(1)}, u32[]{:S(2)}, u32[]{:S(2)}) collective-permute-start(bf16[4,12288]{1,0:T(4,128)(2,1)} %get-tuple-element.70), channel_id=1, source_target_pairs={{0,48},{1,49},{2,50},{3,51},{4,52},{5,53},{6,54},{7,55},{8,56},{9,... | collective-permute-start | bytes 294920 | tf_op jit(solution)/shard_map/ppermute | solution.py:398
  103.8 90.8 %collective-permute-start.12 = (bf16[4,12288]{1,0:T(4,128)(2,1)}, bf16[4,12288]{1,0:T(4,128)(2,1)S(1)}, u32[]{:S(2)}, u32[]{:S(2)}) collective-permute-start(bf16[4,12288]{1,0:T(4,128)(2,1)} %get-tuple-element.71), channel_id=1, source_target_pairs={{0,22},{1,23},{2,24},{3,25},{4,26},{5,27},{6,28},{7,29},{8,30},{9,... | collective-permute-start | bytes 294920 | tf_op jit(solution)/shard_map/ppermute | solution.py:398
  106.5 37.6 %collective-permute-start.35 = (bf16[2,12288]{1,0:T(2,128)(2,1)S(1)}, bf16[2,12288]{1,0:T(2,128)(2,1)S(1)}, u32[]{:S(2)}, u32[]{:S(2)}) collective-permute-start(bf16[2,12288]{1,0:T(2,128)(2,1)S(1)} %collective-permute-done.34), channel_id=1, source_target_pairs={{0,16},{1,17},{2,18},{3,19},{4,20},{5,21},{6,22},{7,23},{8,24},{9,... | collective-permute-start | bytes 147464 | tf_op jit(solution)/shard_map/ppermute | solution.py:402
  116.9 84.2 %collective-permute-start.13 = (bf16[4,12288]{1,0:T(4,128)(2,1)}, bf16[4,12288]{1,0:T(4,128)(2,1)S(1)}, u32[]{:S(2)}, u32[]{:S(2)}) collective-permute-start(bf16[4,12288]{1,0:T(4,128)(2,1)} %get-tuple-element.72), channel_id=1, source_target_pairs={{0,42},{1,43},{2,44},{3,45},{4,46},{5,47},{6,48},{7,49},{8,50},{9,... | collective-permute-start | bytes 294920 | tf_op jit(solution)/shard_map/ppermute | solution.py:398
  144.1 271.5 %copy-start.32 = (bf16[2,12288]{1,0:T(2,128)(2,1)}, bf16[2,12288]{1,0:T(2,128)(2,1)S(1)}, u32[]{:S(2)}) copy-start(bf16[2,12288]{1,0:T(2,128)(2,1)S(1)} %collective-permute-done.35.rest_31_) | copy-start | bytes 147460
  144.1 18.9 %collective-permute-start.37 = (bf16[2,12288]{1,0:T(2,128)(2,1)S(1)}, bf16[2,12288]{1,0:T(2,128)(2,1)S(1)}, u32[]{:S(2)}, u32[]{:S(2)}) collective-permute-start(bf16[2,12288]{1,0:T(2,128)(2,1)S(1)} %collective-permute-done.36), channel_id=1, source_target_pairs={{0,48},{1,49},{2,50},{3,51},{4,52},{5,53},{6,54},{7,55},{8,56},{9,... | collective-permute-start | bytes 147464 | tf_op jit(solution)/shard_map/ppermute | solution.py:403
  163.0 252.6 %copy-start.33 = (bf16[2,12288]{1,0:T(2,128)(2,1)}, bf16[2,12288]{1,0:T(2,128)(2,1)S(1)}, u32[]{:S(2)}) copy-start(bf16[2,12288]{1,0:T(2,128)(2,1)S(1)} %collective-permute-done.37.rest_32_) | copy-start | bytes 147460
  163.0 50.7 %collective-permute-start.14 = (bf16[4,12288]{1,0:T(4,128)(2,1)}, bf16[4,12288]{1,0:T(4,128)(2,1)S(1)}, u32[]{:S(2)}, u32[]{:S(2)}) collective-permute-start(bf16[4,12288]{1,0:T(4,128)(2,1)} %get-tuple-element.73), channel_id=1, source_target_pairs={{0,30},{1,31},{2,32},{3,33},{4,34},{5,35},{6,36},{7,37},{8,38},{9,... | collective-permute-start | bytes 294920 | tf_op jit(solution)/shard_map/ppermute | solution.py:398
  172.6 243.1 %copy-start.3 = (bf16[4,12288]{1,0:T(4,128)(2,1)}, bf16[4,12288]{1,0:T(4,128)(2,1)S(1)}, u32[]{:S(2)}) copy-start(bf16[4,12288]{1,0:T(4,128)(2,1)S(1)} %collective-permute-done.10.rest_7_) | copy-start | bytes 294916
  172.6 67.3 %collective-permute-start.15 = (bf16[4,12288]{1,0:T(4,128)(2,1)}, bf16[4,12288]{1,0:T(4,128)(2,1)S(1)}, u32[]{:S(2)}, u32[]{:S(2)}) collective-permute-start(bf16[4,12288]{1,0:T(4,128)(2,1)} %get-tuple-element.74), channel_id=1, source_target_pairs={{0,34},{1,35},{2,36},{3,37},{4,38},{5,39},{6,40},{7,41},{8,42},{9,... | collective-permute-start | bytes 294920 | tf_op jit(solution)/shard_map/ppermute | solution.py:398
  182.5 233.2 %copy-start.4 = (bf16[4,12288]{1,0:T(4,128)(2,1)}, bf16[4,12288]{1,0:T(4,128)(2,1)S(1)}, u32[]{:S(2)}) copy-start(bf16[4,12288]{1,0:T(4,128)(2,1)S(1)} %collective-permute-done.11.rest_8_) | copy-start | bytes 294916
  182.5 63.3 %collective-permute-start.16 = (bf16[4,12288]{1,0:T(4,128)(2,1)}, bf16[4,12288]{1,0:T(4,128)(2,1)S(1)}, u32[]{:S(2)}, u32[]{:S(2)}) collective-permute-start(bf16[4,12288]{1,0:T(4,128)(2,1)} %get-tuple-element.75), channel_id=1, source_target_pairs={{0,28},{1,29},{2,30},{3,31},{4,32},{5,33},{6,34},{7,35},{8,36},{9,... | collective-permute-start | bytes 294920 | tf_op jit(solution)/shard_map/ppermute | solution.py:398
  194.6 221.1 %copy-start.5 = (bf16[4,12288]{1,0:T(4,128)(2,1)}, bf16[4,12288]{1,0:T(4,128)(2,1)S(1)}, u32[]{:S(2)}) copy-start(bf16[4,12288]{1,0:T(4,128)(2,1)S(1)} %collective-permute-done.12.rest_9_) | copy-start | bytes 294916
  194.6 62.6 %collective-permute-start.17 = (bf16[4,12288]{1,0:T(4,128)(2,1)}, bf16[4,12288]{1,0:T(4,128)(2,1)S(1)}, u32[]{:S(2)}, u32[]{:S(2)}) collective-permute-start(bf16[4,12288]{1,0:T(4,128)(2,1)} %get-tuple-element.76), channel_id=1, source_target_pairs={{0,36},{1,37},{2,38},{3,39},{4,40},{5,41},{6,42},{7,43},{8,44},{9,... | collective-permute-start | bytes 294920 | tf_op jit(solution)/shard_map/ppermute | solution.py:398
  201.1 214.6 %copy-start.6 = (bf16[4,12288]{1,0:T(4,128)(2,1)}, bf16[4,12288]{1,0:T(4,128)(2,1)S(1)}, u32[]{:S(2)}) copy-start(bf16[4,12288]{1,0:T(4,128)(2,1)S(1)} %collective-permute-done.13.rest_10_) | copy-start | bytes 294916
  201.1 63.0 %collective-permute-start.18 = (bf16[4,12288]{1,0:T(4,128)(2,1)}, bf16[4,12288]{1,0:T(4,128)(2,1)S(1)}, u32[]{:S(2)}, u32[]{:S(2)}) collective-permute-start(bf16[4,12288]{1,0:T(4,128)(2,1)} %get-tuple-element.77), channel_id=1, source_target_pairs={{0,26},{1,27},{2,28},{3,29},{4,30},{5,31},{6,32},{7,33},{8,34},{9,... | collective-permute-start | bytes 294920 | tf_op jit(solution)/shard_map/ppermute | solution.py:398
  213.8 201.9 %copy-start.7 = (bf16[4,12288]{1,0:T(4,128)(2,1)}, bf16[4,12288]{1,0:T(4,128)(2,1)S(1)}, u32[]{:S(2)}) copy-start(bf16[4,12288]{1,0:T(4,128)(2,1)S(1)} %collective-permute-done.14.rest_11_) | copy-start | bytes 294916
  213.8 81.4 %collective-permute-start.19 = (bf16[4,12288]{1,0:T(4,128)(2,1)}, bf16[4,12288]{1,0:T(4,128)(2,1)S(1)}, u32[]{:S(2)}, u32[]{:S(2)}) collective-permute-start(bf16[4,12288]{1,0:T(4,128)(2,1)} %get-tuple-element.78), channel_id=1, source_target_pairs={{0,38},{1,39},{2,40},{3,41},{4,42},{5,43},{6,44},{7,45},{8,46},{9,... | collective-permute-start | bytes 294920 | tf_op jit(solution)/shard_map/ppermute | solution.py:398
  239.9 175.8 %copy-start.8 = (bf16[4,12288]{1,0:T(4,128)(2,1)}, bf16[4,12288]{1,0:T(4,128)(2,1)S(1)}, u32[]{:S(2)}) copy-start(bf16[4,12288]{1,0:T(4,128)(2,1)S(1)} %collective-permute-done.15.rest_12_) | copy-start | bytes 294916
  239.9 66.2 %collective-permute-start.20 = (bf16[4,12288]{1,0:T(4,128)(2,1)}, bf16[4,12288]{1,0:T(4,128)(2,1)S(1)}, u32[]{:S(2)}, u32[]{:S(2)}) collective-permute-start(bf16[4,12288]{1,0:T(4,128)(2,1)} %get-tuple-element.79), channel_id=1, source_target_pairs={{0,24},{1,25},{2,26},{3,27},{4,28},{5,29},{6,30},{7,31},{8,32},{9,... | collective-permute-start | bytes 294920 | tf_op jit(solution)/shard_map/ppermute | solution.py:398
  245.8 85.2 %collective-permute-start.21 = (bf16[4,12288]{1,0:T(4,128)(2,1)}, bf16[4,12288]{1,0:T(4,128)(2,1)S(1)}, u32[]{:S(2)}, u32[]{:S(2)}) collective-permute-start(bf16[4,12288]{1,0:T(4,128)(2,1)} %get-tuple-element.80), channel_id=1, source_target_pairs={{0,40},{1,41},{2,42},{3,43},{4,44},{5,45},{6,46},{7,47},{8,48},{9,... | collective-permute-start | bytes 294920 | tf_op jit(solution)/shard_map/ppermute | solution.py:398
  257.2 73.8 %collective-permute-start.22 = (bf16[4,12288]{1,0:T(4,128)(2,1)}, bf16[4,12288]{1,0:T(4,128)(2,1)S(1)}, u32[]{:S(2)}, u32[]{:S(2)}) collective-permute-start(bf16[4,12288]{1,0:T(4,128)(2,1)} %get-tuple-element.81), channel_id=1, source_target_pairs={{0,20},{1,21},{2,22},{3,23},{4,24},{5,25},{6,26},{7,27},{8,28},{9,... | collective-permute-start | bytes 294920 | tf_op jit(solution)/shard_map/ppermute | solution.py:398
  264.1 76.8 %collective-permute-start.23 = (bf16[4,12288]{1,0:T(4,128)(2,1)}, bf16[4,12288]{1,0:T(4,128)(2,1)S(1)}, u32[]{:S(2)}, u32[]{:S(2)}) collective-permute-start(bf16[4,12288]{1,0:T(4,128)(2,1)} %get-tuple-element.82), channel_id=1, source_target_pairs={{0,44},{1,45},{2,46},{3,47},{4,48},{5,49},{6,50},{7,51},{8,52},{9,... | collective-permute-start | bytes 294920 | tf_op jit(solution)/shard_map/ppermute | solution.py:398
  295.3 46.2 %collective-permute-start.24 = (bf16[4,12288]{1,0:T(4,128)(2,1)}, bf16[4,12288]{1,0:T(4,128)(2,1)S(1)}, u32[]{:S(2)}, u32[]{:S(2)}) collective-permute-start(bf16[4,12288]{1,0:T(4,128)(2,1)} %get-tuple-element.83), channel_id=1, source_target_pairs={{0,18},{1,19},{2,20},{3,21},{4,22},{5,23},{6,24},{7,25},{8,26},{9,... | collective-permute-start | bytes 294920 | tf_op jit(solution)/shard_map/ppermute | solution.py:398
  306.2 44.3 %collective-permute-start.25 = (bf16[4,12288]{1,0:T(4,128)(2,1)}, bf16[4,12288]{1,0:T(4,128)(2,1)S(1)}, u32[]{:S(2)}, u32[]{:S(2)}) collective-permute-start(bf16[4,12288]{1,0:T(4,128)(2,1)} %get-tuple-element.84), channel_id=1, source_target_pairs={{0,46},{1,47},{2,48},{3,49},{4,50},{5,51},{6,52},{7,53},{8,54},{9,... | collective-permute-start | bytes 294920 | tf_op jit(solution)/shard_map/ppermute | solution.py:398
  331.0 27.3 %collective-permute-start.26 = (bf16[4,12288]{1,0:T(4,128)(2,1)}, bf16[4,12288]{1,0:T(4,128)(2,1)S(1)}, u32[]{:S(2)}, u32[]{:S(2)}) collective-permute-start(bf16[4,12288]{1,0:T(4,128)(2,1)} %get-tuple-element.85), channel_id=1, source_target_pairs={{0,14},{1,15},{2,16},{3,17},{4,18},{5,19},{6,20},{7,21},{8,22},{9,... | collective-permute-start | bytes 294920 | tf_op jit(solution)/shard_map/ppermute | solution.py:398
  331.0 27.9 %collective-permute-start.27 = (bf16[4,12288]{1,0:T(4,128)(2,1)}, bf16[4,12288]{1,0:T(4,128)(2,1)S(1)}, u32[]{:S(2)}, u32[]{:S(2)}) collective-permute-start(bf16[4,12288]{1,0:T(4,128)(2,1)} %get-tuple-element.86), channel_id=1, source_target_pairs={{0,50},{1,51},{2,52},{3,53},{4,54},{5,55},{6,56},{7,57},{8,58},{9,... | collective-permute-start | bytes 294920 | tf_op jit(solution)/shard_map/ppermute | solution.py:398
  340.8 21.5 %collective-permute-start.28 = (bf16[4,12288]{1,0:T(4,128)(2,1)}, bf16[4,12288]{1,0:T(4,128)(2,1)S(1)}, u32[]{:S(2)}, u32[]{:S(2)}) collective-permute-start(bf16[4,12288]{1,0:T(4,128)(2,1)} %get-tuple-element.87), channel_id=1, source_target_pairs={{0,12},{1,13},{2,14},{3,15},{4,16},{5,17},{6,18},{7,19},{8,20},{9,... | collective-permute-start | bytes 294920 | tf_op jit(solution)/shard_map/ppermute | solution.py:398
  341.5 41.3 %collective-permute-start.29 = (bf16[4,12288]{1,0:T(4,128)(2,1)}, bf16[4,12288]{1,0:T(4,128)(2,1)S(1)}, u32[]{:S(2)}, u32[]{:S(2)}) collective-permute-start(bf16[4,12288]{1,0:T(4,128)(2,1)} %get-tuple-element.88), channel_id=1, source_target_pairs={{0,52},{1,53},{2,54},{3,55},{4,56},{5,57},{6,58},{7,59},{8,60},{9,... | collective-permute-start | bytes 294920 | tf_op jit(solution)/shard_map/ppermute | solution.py:398
  350.4 41.5 %collective-permute-start.30 = (bf16[4,12288]{1,0:T(4,128)(2,1)}, bf16[4,12288]{1,0:T(4,128)(2,1)S(1)}, u32[]{:S(2)}, u32[]{:S(2)}) collective-permute-start(bf16[4,12288]{1,0:T(4,128)(2,1)} %get-tuple-element.89), channel_id=1, source_target_pairs={{0,8},{1,9},{2,10},{3,11},{4,12},{5,13},{6,14},{7,15},{8,16},{9,17... | collective-permute-start | bytes 294920 | tf_op jit(solution)/shard_map/ppermute | solution.py:398
  358.3 33.6 %collective-permute-start.31 = (bf16[4,12288]{1,0:T(4,128)(2,1)}, bf16[4,12288]{1,0:T(4,128)(2,1)S(1)}, u32[]{:S(2)}, u32[]{:S(2)}) collective-permute-start(bf16[4,12288]{1,0:T(4,128)(2,1)} %get-tuple-element.90), channel_id=1, source_target_pairs={{0,56},{1,57},{2,58},{3,59},{4,60},{5,61},{6,62},{7,63},{8,0},{9,1... | collective-permute-start | bytes 294920 | tf_op jit(solution)/shard_map/ppermute | solution.py:398
  358.9 38.0 %collective-permute-start.32 = (bf16[4,12288]{1,0:T(4,128)(2,1)}, bf16[4,12288]{1,0:T(4,128)(2,1)S(1)}, u32[]{:S(2)}, u32[]{:S(2)}) collective-permute-start(bf16[4,12288]{1,0:T(4,128)(2,1)} %get-tuple-element.91), channel_id=1, source_target_pairs={{0,2},{1,3},{2,4},{3,5},{4,6},{5,7},{6,8},{7,9},{8,10},{9,11},{10,... | collective-permute-start | bytes 294920 | tf_op jit(solution)/shard_map/ppermute | solution.py:398
  362.4 34.6 %collective-permute-start.33 = (bf16[4,12288]{1,0:T(4,128)(2,1)}, bf16[4,12288]{1,0:T(4,128)(2,1)S(1)}, u32[]{:S(2)}, u32[]{:S(2)}) collective-permute-start(bf16[4,12288]{1,0:T(4,128)(2,1)} %get-tuple-element.92), channel_id=1, source_target_pairs={{0,62},{1,63},{2,0},{3,1},{4,2},{5,3},{6,4},{7,5},{8,6},{9,7},{10,... | collective-permute-start | bytes 294920 | tf_op jit(solution)/shard_map/ppermute | solution.py:398
  382.8 24.8 %collective-permute-start.5 = (bf16[4,12288]{1,0:T(4,128)(2,1)}, bf16[4,12288]{1,0:T(4,128)(2,1)S(1)}, u32[]{:S(2)}, u32[]{:S(2)}) collective-permute-start(bf16[4,12288]{1,0:T(4,128)(2,1)} %get-tuple-element.64), channel_id=1, source_target_pairs={{0,60},{1,61},{2,62},{3,63},{4,0},{5,1},{6,2},{7,3},{8,4},{9,5},{1... | collective-permute-start | bytes 294920 | tf_op jit(solution)/shard_map/ppermute | solution.py:398
  391.9 15.7 %collective-permute-start.6 = (bf16[4,12288]{1,0:T(4,128)(2,1)}, bf16[4,12288]{1,0:T(4,128)(2,1)S(1)}, u32[]{:S(2)}, u32[]{:S(2)}) collective-permute-start(bf16[4,12288]{1,0:T(4,128)(2,1)} %get-tuple-element.65), channel_id=1, source_target_pairs={{0,6},{1,7},{2,8},{3,9},{4,10},{5,11},{6,12},{7,13},{8,14},{9,15},... | collective-permute-start | bytes 294920 | tf_op jit(solution)/shard_map/ppermute | solution.py:398
  391.9 15.7 %collective-permute-start.7 = (bf16[4,12288]{1,0:T(4,128)(2,1)}, bf16[4,12288]{1,0:T(4,128)(2,1)S(1)}, u32[]{:S(2)}, u32[]{:S(2)}) collective-permute-start(bf16[4,12288]{1,0:T(4,128)(2,1)} %get-tuple-element.66), channel_id=1, source_target_pairs={{0,58},{1,59},{2,60},{3,61},{4,62},{5,63},{6,0},{7,1},{8,2},{9,3},... | collective-permute-start | bytes 294920 | tf_op jit(solution)/shard_map/ppermute | solution.py:398
  396.9 18.7 %collective-permute-start.8 = (bf16[4,12288]{1,0:T(4,128)(2,1)}, bf16[4,12288]{1,0:T(4,128)(2,1)S(1)}, u32[]{:S(2)}, u32[]{:S(2)}) collective-permute-start(bf16[4,12288]{1,0:T(4,128)(2,1)} %get-tuple-element.67), channel_id=1, source_target_pairs={{0,10},{1,11},{2,12},{3,13},{4,14},{5,15},{6,16},{7,17},{8,18},{9,... | collective-permute-start | bytes 294920 | tf_op jit(solution)/shard_map/ppermute | solution.py:398
  397.0 18.7 %collective-permute-start.9 = (bf16[4,12288]{1,0:T(4,128)(2,1)}, bf16[4,12288]{1,0:T(4,128)(2,1)S(1)}, u32[]{:S(2)}, u32[]{:S(2)}) collective-permute-start(bf16[4,12288]{1,0:T(4,128)(2,1)} %get-tuple-element.68), channel_id=1, source_target_pairs={{0,54},{1,55},{2,56},{3,57},{4,58},{5,59},{6,60},{7,61},{8,62},{9,... | collective-permute-start | bytes 294920 | tf_op jit(solution)/shard_map/ppermute | solution.py:398
  (31 other events, 1675.1 us)
